TPU v7x, 32 devices: a whole 2x2x4 slice. The times are simulated.
32 devices in a mesh: fsdp: 8 (over y, x, core), ctx: 4 (over z).
Axes of the slice: x: 2, y: 2, z: 4, core: 2. Of those that a mesh axis runs over, the one named last changes fastest.
Arguments:
- hidden_in: bfloat16 [8, 512, 1024], P('fsdp', 'ctx'), may hold values from -24 to 24
- block_order: int32 [8, 8], P('fsdp'), may hold values from 0 to 7, each once within a row
- cotangent: bfloat16 [8, 512, 1024], P('fsdp', 'ctx'), may hold values from -6 to 6
- q_weight: bfloat16 [1024, 2048], P(('fsdp', 'ctx')), may hold values from -0.1875 to 0.1875
- k_weight: bfloat16 [1024, 1024], P(('fsdp', 'ctx')), may hold values from -0.1875 to 0.1875
- v_weight: bfloat16 [1024, 1024], P(('fsdp', 'ctx')), may hold values from -0.1875 to 0.1875
- o_weight: bfloat16 [1024, 2048], P(('fsdp', 'ctx')), may hold values from -1.5 to 1.5
- attn_gain: bfloat16 [1024], P(('fsdp', 'ctx')), may hold values from 0.5 to 1.5
- query_gain: bfloat16 [128], P(('fsdp', 'ctx')), may hold values from 0.5 to 1.5
- key_gain: bfloat16 [128], P(('fsdp', 'ctx')), may hold values from 0.5 to 1.5
- mlp_gain: bfloat16 [1024], P(('fsdp', 'ctx')), may hold values from 0.5 to 1.5
- gate_weight: bfloat16 [1024, 3072], P(('fsdp', 'ctx')), may hold values from -0.1875 to 0.1875
- up_weight: bfloat16 [1024, 3072], P(('fsdp', 'ctx')), may hold values from -0.1875 to 0.1875
- down_weight: bfloat16 [1024, 3072], P(('fsdp', 'ctx')), may hold values from -0.109375 to 0.109375
Outputs:
- hidden_out: bfloat16 [8, 512, 1024], P('fsdp', 'ctx')
- input_grad: float32 [8, 512, 1024], P('fsdp', 'ctx')
- q_grad: float32 [1024, 2048], P(('fsdp', 'ctx'))
- k_grad: float32 [1024, 1024], P(('fsdp', 'ctx'))
- v_grad: float32 [1024, 1024], P(('fsdp', 'ctx'))
- o_grad: float32 [1024, 2048], P(('fsdp', 'ctx'))
- attn_gain_grad: float32 [1024], P(('fsdp', 'ctx'))
- query_gain_grad: float32 [128], P(('fsdp', 'ctx'))
- key_gain_grad: float32 [128], P(('fsdp', 'ctx'))
- mlp_gain_grad: float32 [1024], P(('fsdp', 'ctx'))
- gate_grad: float32 [1024, 3072], P(('fsdp', 'ctx'))
- up_grad: float32 [1024, 3072], P(('fsdp', 'ctx'))
- down_grad: float32 [1024, 3072], P(('fsdp', 'ctx'))
Inputs may be any that keep to these rules, and one draw needn't show every extreme that they name: `block_order`: each row is a permutation: every position block of a sequence sits in exactly one slot.
All inputs are finite; a program needn't handle non-finite values.
Results may differ from a plain program's by a relative error of at most 0.023.
Values may be sent and summed in bfloat16 or wider, within the bound.
A program may use at most 256 MiB of HBM per device.

v0:
```python
import math

import jax
import jax.numpy as jnp
from jax import lax
from jax.sharding import PartitionSpec as P

HEADS = 16
KV_HEADS = 8
HEAD_DIM = 128


EPSILON = 1e-06
FIRST_AXIS = (((0,), (0,)), ((), ()))


def normalize(signal, gain_vec):
    inverse_rms = lax.rsqrt(jnp.mean(signal * signal, axis=-1, keepdims=True) + EPSILON)
    return (signal * inverse_rms * gain_vec, inverse_rms)


def norm_back(signal, inverse_rms, gain_vec, upstream):
    unit_values = signal * inverse_rms
    scaled_up = upstream * gain_vec
    inner = scaled_up - unit_values * jnp.mean(scaled_up * unit_values, axis=-1, keepdims=True)
    return (inverse_rms * inner, upstream * unit_values)


def rope_tables(positions, head_width):
    exponent = jnp.arange(head_width // 2, dtype=jnp.float32) * (2.0 / head_width)
    inverse = jnp.exp(-exponent * math.log(1000000.0))
    angles = positions.astype(jnp.float32)[:, None] * inverse[None, :]
    angles = jnp.concatenate([angles, angles], axis=-1)
    return (jnp.cos(angles)[:, None, :], jnp.sin(angles)[:, None, :])


def rotate(signal, cosine, sine):
    half_dim = signal.shape[-1] // 2
    turned = jnp.concatenate([-signal[..., half_dim:], signal[..., :half_dim]], axis=-1)
    return signal * cosine + turned * sine


def rotate_back(upstream, cosine, sine):
    half_dim = upstream.shape[-1] // 2
    scaled_up = upstream * sine
    return upstream * cosine + jnp.concatenate(
        [scaled_up[..., half_dim:], -scaled_up[..., :half_dim]], axis=-1
    )


def key_scores(queries, keys_piece, query_pos, key_pos, factor):
    raw_scores = (
        jnp.einsum("rkgd,nkd->kgrn", queries, keys_piece, preferred_element_type=jnp.float32)
        * factor
    )
    allowed = key_pos[None, :] <= query_pos[:, None]
    return jnp.where(allowed, jnp.exp(raw_scores), 0.0)


def local(
    hidden_in,
    block_order,
    cotangent,
    q_weight,
    k_weight,
    v_weight,
    o_weight,
    attn_gain,
    query_gain,
    key_gain,
    mlp_gain,
    gate_weight,
    up_weight,
    down_weight,
):
    inputs = hidden_in[0].astype(jnp.float32)
    row_count = inputs.shape[0]
    block_len = row_count // 2
    ctx_index = lax.axis_index("ctx")
    group_size = HEADS // KV_HEADS
    factor = 1.0 / math.sqrt(HEAD_DIM)
    positions = (
        block_order[0][:, None] * block_len + jnp.arange(block_len, dtype=jnp.int32)[None, :]
    ).reshape(-1)
    own_pos = lax.dynamic_slice_in_dim(positions, ctx_index * row_count, row_count)
    cosine, sine = rope_tables(own_pos, HEAD_DIM)
    query_full, key_full, value_full, output_full, norm_full, qgain_full, kgain_full = (
        lax.all_gather(q_weight, ("fsdp", "ctx"), axis=0, tiled=True),
        lax.all_gather(k_weight, ("fsdp", "ctx"), axis=0, tiled=True),
        lax.all_gather(v_weight, ("fsdp", "ctx"), axis=0, tiled=True),
        lax.all_gather(o_weight, ("fsdp", "ctx"), axis=0, tiled=True),
        lax.all_gather(attn_gain, ("fsdp", "ctx"), axis=0, tiled=True),
        lax.all_gather(query_gain, ("fsdp", "ctx"), axis=0, tiled=True),
        lax.all_gather(key_gain, ("fsdp", "ctx"), axis=0, tiled=True),
    )
    norm_gain = norm_full.astype(jnp.float32)
    qgain = qgain_full.astype(jnp.float32)
    kgain = kgain_full.astype(jnp.float32)
    normed, norm_scale = normalize(inputs, norm_gain)
    normed_low = normed.astype(jnp.bfloat16)
    query_proj = jnp.dot(normed_low, query_full, preferred_element_type=jnp.float32).reshape(
        row_count, HEADS, HEAD_DIM
    )
    key_proj = jnp.dot(normed_low, key_full, preferred_element_type=jnp.float32).reshape(
        row_count, KV_HEADS, HEAD_DIM
    )
    value_low = (
        jnp.dot(normed_low, value_full, preferred_element_type=jnp.float32)
        .astype(jnp.bfloat16)
        .reshape(row_count, KV_HEADS, HEAD_DIM)
    )
    query_normed, query_scale = normalize(query_proj, qgain)
    query_low = (
        rotate(query_normed, cosine, sine)
        .astype(jnp.bfloat16)
        .reshape(row_count, KV_HEADS, group_size, HEAD_DIM)
    )
    key_normed, key_scale = normalize(key_proj, kgain)
    key_low = rotate(key_normed, cosine, sine).astype(jnp.bfloat16)
    keys_piece = lax.all_gather(key_low, "ctx", axis=0, tiled=True)
    values_piece = lax.all_gather(value_low, "ctx", axis=0, tiled=True)
    key_pos = positions
    weights_exp = key_scores(query_low, keys_piece, own_pos, key_pos, factor)
    denominator = jnp.sum(weights_exp, axis=-1)
    numerator = jnp.einsum(
        "kgrn,nkd->rkgd",
        weights_exp.astype(jnp.bfloat16),
        values_piece,
        preferred_element_type=jnp.float32,
    )
    numerator, denominator = (numerator, denominator)
    denom_rows = jnp.transpose(denominator, (2, 0, 1))[..., None]
    attn_full = numerator / denom_rows
    attn_low = attn_full.astype(jnp.bfloat16).reshape(row_count, HEADS * HEAD_DIM)
    residual = inputs + jnp.dot(attn_low, output_full.T, preferred_element_type=jnp.float32)
    gate_full, up_full, down_full, mlp_gain_full = (
        lax.all_gather(gate_weight, ("fsdp", "ctx"), axis=0, tiled=True),
        lax.all_gather(up_weight, ("fsdp", "ctx"), axis=0, tiled=True),
        lax.all_gather(down_weight, ("fsdp", "ctx"), axis=0, tiled=True),
        lax.all_gather(mlp_gain, ("fsdp", "ctx"), axis=0, tiled=True),
    )
    mlp_norm_gain = mlp_gain_full.astype(jnp.float32)
    mixed, mix_scale = normalize(residual, mlp_norm_gain)
    mixed_low = mixed.astype(jnp.bfloat16)
    gate_val = jnp.dot(mixed_low, gate_full, preferred_element_type=jnp.float32)
    up_val = jnp.dot(mixed_low, up_full, preferred_element_type=jnp.float32)
    sigmoid_gate = jax.nn.sigmoid(gate_val)
    swish_gate = gate_val * sigmoid_gate
    hidden_low = (swish_gate * up_val).astype(jnp.bfloat16)
    result = residual + jnp.dot(hidden_low, down_full.T, preferred_element_type=jnp.float32)
    upstream = cotangent[0].astype(jnp.float32)
    upstream_low = cotangent[0]
    gate_back, up_back, down_back = (
        lax.all_gather(gate_weight, ("fsdp", "ctx"), axis=0, tiled=True),
        lax.all_gather(up_weight, ("fsdp", "ctx"), axis=0, tiled=True),
        lax.all_gather(down_weight, ("fsdp", "ctx"), axis=0, tiled=True),
    )
    hidden_grad = jnp.dot(upstream_low, down_back, preferred_element_type=jnp.float32)
    gate_grad_low = (
        hidden_grad * up_val * sigmoid_gate * (1.0 + gate_val * (1.0 - sigmoid_gate))
    ).astype(jnp.bfloat16)
    up_grad_low = (hidden_grad * swish_gate).astype(jnp.bfloat16)
    mixed_grad = jnp.dot(gate_grad_low, gate_back.T, preferred_element_type=jnp.float32) + jnp.dot(
        up_grad_low, up_back.T, preferred_element_type=jnp.float32
    )
    resid_from_norm, mlp_gain_term = norm_back(residual, mix_scale, mlp_norm_gain, mixed_grad)
    residual_grad = upstream + resid_from_norm
    mlp_grads = lax.psum_scatter(
        jnp.concatenate(
            [
                lax.dot_general(
                    mixed_low, gate_grad_low, FIRST_AXIS, preferred_element_type=jnp.float32
                ),
                lax.dot_general(
                    mixed_low, up_grad_low, FIRST_AXIS, preferred_element_type=jnp.float32
                ),
                lax.dot_general(
                    upstream_low, hidden_low, FIRST_AXIS, preferred_element_type=jnp.float32
                ),
            ],
            axis=1,
        ),
        ("fsdp", "ctx"),
        scatter_dimension=0,
        tiled=True,
    )
    ff_width = gate_weight.shape[1]
    resid_low = residual_grad.astype(jnp.bfloat16)
    query_back, key_back, value_back, output_back = (
        lax.all_gather(q_weight, ("fsdp", "ctx"), axis=0, tiled=True),
        lax.all_gather(k_weight, ("fsdp", "ctx"), axis=0, tiled=True),
        lax.all_gather(v_weight, ("fsdp", "ctx"), axis=0, tiled=True),
        lax.all_gather(o_weight, ("fsdp", "ctx"), axis=0, tiled=True),
    )
    attn_grad = jnp.dot(resid_low, output_back, preferred_element_type=jnp.float32).reshape(
        row_count, KV_HEADS, group_size, HEAD_DIM
    )
    output_w_grad = lax.dot_general(
        resid_low, attn_low, FIRST_AXIS, preferred_element_type=jnp.float32
    )
    share_low = (attn_grad / denom_rows).astype(jnp.bfloat16)
    denom_grad = jnp.transpose(jnp.sum(attn_grad * attn_full, axis=-1), (1, 2, 0)) / denominator
    keys_piece = lax.all_gather(key_low, "ctx", axis=0, tiled=True)
    values_piece = lax.all_gather(value_low, "ctx", axis=0, tiled=True)
    key_pos = positions
    weights_exp = key_scores(query_low, keys_piece, own_pos, key_pos, factor)
    weight_grad = jnp.einsum(
        "rkgd,nkd->kgrn", share_low, values_piece, preferred_element_type=jnp.float32
    )
    score_low = (weights_exp * (weight_grad - denom_grad[..., None])).astype(jnp.bfloat16)
    query_acc = (
        jnp.einsum("kgrn,nkd->rkgd", score_low, keys_piece, preferred_element_type=jnp.float32)
        * factor
    )
    key_part = (
        jnp.einsum("kgrn,rkgd->nkd", score_low, query_low, preferred_element_type=jnp.float32)
        * factor
    )
    value_part = jnp.einsum(
        "kgrn,rkgd->nkd",
        weights_exp.astype(jnp.bfloat16),
        share_low,
        preferred_element_type=jnp.float32,
    )
    key_acc = key_part
    value_acc = value_part
    query_rot_grad, key_acc, value_acc = (query_acc, key_acc, value_acc)
    key_rot_grad, value_grad_own = (
        lax.psum_scatter(
            key_acc.astype(jnp.bfloat16), "ctx", scatter_dimension=0, tiled=True
        ).astype(jnp.float32),
        lax.psum_scatter(
            value_acc.astype(jnp.bfloat16), "ctx", scatter_dimension=0, tiled=True
        ).astype(jnp.float32),
    )
    query_normed_grad = rotate_back(
        query_rot_grad.reshape(row_count, HEADS, HEAD_DIM), cosine, sine
    )
    query_proj_grad, query_gain_term = norm_back(query_proj, query_scale, qgain, query_normed_grad)
    query_proj_low = query_proj_grad.reshape(row_count, HEADS * HEAD_DIM).astype(jnp.bfloat16)
    key_normed_grad = rotate_back(key_rot_grad, cosine, sine)
    key_proj_grad, key_gain_term = norm_back(key_proj, key_scale, kgain, key_normed_grad)
    key_proj_low = key_proj_grad.reshape(row_count, KV_HEADS * HEAD_DIM).astype(jnp.bfloat16)
    value_proj_low = value_grad_own.reshape(row_count, KV_HEADS * HEAD_DIM).astype(jnp.bfloat16)
    normed_grad = jnp.dot(query_proj_low, query_back.T, preferred_element_type=jnp.float32)
    normed_grad = normed_grad + jnp.dot(
        key_proj_low, key_back.T, preferred_element_type=jnp.float32
    )
    normed_grad = normed_grad + jnp.dot(
        value_proj_low, value_back.T, preferred_element_type=jnp.float32
    )
    input_from_norm, attn_gain_term = norm_back(inputs, norm_scale, norm_gain, normed_grad)
    input_grad = residual_grad + input_from_norm
    query_w_grad = lax.dot_general(
        normed_low, query_proj_low, FIRST_AXIS, preferred_element_type=jnp.float32
    )
    key_w_grad = lax.dot_general(
        normed_low, key_proj_low, FIRST_AXIS, preferred_element_type=jnp.float32
    )
    value_w_grad = lax.dot_general(
        normed_low, value_proj_low, FIRST_AXIS, preferred_element_type=jnp.float32
    )
    attn_gain_sum = jnp.sum(attn_gain_term, axis=0)
    query_gain_sum = jnp.sum(query_gain_term, axis=(0, 1))
    key_gain_sum = jnp.sum(key_gain_term, axis=(0, 1))
    mlp_gain_sum = jnp.sum(mlp_gain_term, axis=0)
    summed = (
        lax.psum_scatter(query_w_grad, ("fsdp", "ctx"), scatter_dimension=0, tiled=True),
        lax.psum_scatter(key_w_grad, ("fsdp", "ctx"), scatter_dimension=0, tiled=True),
        lax.psum_scatter(value_w_grad, ("fsdp", "ctx"), scatter_dimension=0, tiled=True),
        lax.psum_scatter(output_w_grad, ("fsdp", "ctx"), scatter_dimension=0, tiled=True),
        lax.psum_scatter(attn_gain_sum, ("fsdp", "ctx"), scatter_dimension=0, tiled=True),
        lax.psum_scatter(query_gain_sum, ("fsdp", "ctx"), scatter_dimension=0, tiled=True),
        lax.psum_scatter(key_gain_sum, ("fsdp", "ctx"), scatter_dimension=0, tiled=True),
        lax.psum_scatter(mlp_gain_sum, ("fsdp", "ctx"), scatter_dimension=0, tiled=True),
    )
    return (
        result.astype(jnp.bfloat16)[None],
        input_grad[None],
        summed[0],
        summed[1],
        summed[2],
        summed[3],
        summed[4],
        summed[5],
        summed[6],
        summed[7],
        mlp_grads[:, :ff_width],
        mlp_grads[:, ff_width : 2 * ff_width],
        mlp_grads[:, 2 * ff_width :],
    )


def solution(mesh):
    return jax.shard_map(
        local,
        mesh=mesh,
        in_specs=(
            P("fsdp", "ctx", None),
            P("fsdp", None),
            P("fsdp", "ctx", None),
            P(("fsdp", "ctx"), None),
            P(("fsdp", "ctx"), None),
            P(("fsdp", "ctx"), None),
            P(("fsdp", "ctx"), None),
            P(("fsdp", "ctx")),
            P(("fsdp", "ctx")),
            P(("fsdp", "ctx")),
            P(("fsdp", "ctx")),
            P(("fsdp", "ctx"), None),
            P(("fsdp", "ctx"), None),
            P(("fsdp", "ctx"), None),
        ),
        out_specs=(
            P("fsdp", "ctx", None),
            P("fsdp", "ctx", None),
            P(("fsdp", "ctx"), None),
            P(("fsdp", "ctx"), None),
            P(("fsdp", "ctx"), None),
            P(("fsdp", "ctx"), None),
            P(("fsdp", "ctx")),
            P(("fsdp", "ctx")),
            P(("fsdp", "ctx")),
            P(("fsdp", "ctx")),
            P(("fsdp", "ctx"), None),
            P(("fsdp", "ctx"), None),
            P(("fsdp", "ctx"), None),
        ),
        check_vma=False,
    )
```

profile of v0, /device:TPU:0, one launch (start us, length us, event | category | flops | bytes accessed | tf_op | source)
XLA Modules:
  0.0 1643.0 jit_solution(4987692658793982937)
XLA Ops:
  12.9 42.2 %all-reduce.9 = (bf16[1024]{0:T(1024)(128)(2,1)S(1)}, bf16[128]{0:T(256)(128)(2,1)S(1)}, bf16[128]{0:T(256)(128)(2,1)S(1)}, bf16[1024]{0:T(1024)(128)(2,1)S(1)}) all-reduce(bf16[1024]{0:T(1024)(128)(2,1)S(1)} %dynamic-update-slice, bf16[128]{0:T(256)(128)(2,1)S(1)} %dynamic-update-slice.2, ...), channel_id=1, replica_groups=mesh['fsdp'=8,'ctx'=4] {'fsdp','ctx'}, use_global_device_ids=true, to_apply=%add | all-reduce | flops 2304 | bytes 9216
  57.4 12.8 all-gather.14.cloned.1.call-done
  70.2 3.9 copy.41
  77.6 50.7 %all-gather.10.cloned.1.call-done = bf16[1024,1024]{1,0:T(8,128)(2,1)} async-done(((bf16[32,1024]{1,0:T(8,128)(2,1)}), bf16[1024,1024]{1,0:T(8,128)(2,1)}) %all-gather.10.cloned.1.call-update) | async-done | bytes 2097168 | tf_op jit(solution)/shard_map/all_gather | solution.py:90
  134.4 57.5 %all-gather.18.cloned.1.call-done = bf16[1024,2048]{1,0:T(8,128)(2,1)} async-done(((bf16[32,2048]{1,0:T(8,128)(2,1)}), bf16[1024,2048]{1,0:T(8,128)(2,1)}) %all-gather.18.cloned.1.call-update) | async-done | bytes 4194320 | tf_op jit(solution)/shard_map/all_gather | solution.py:88
  191.9 6.5 copy.42
  202.8 19.8 %all-gather.16.cloned.1.call-done = bf16[512,8,128]{0,2,1:T(8,128)(2,1)} async-done(((bf16[128,8,128]{0,2,1:T(8,128)(2,1)}), bf16[512,8,128]{0,2,1:T(8,128)(2,1)}) %all-gather.16.cloned.1.call-update) | async-done | bytes 1048592 | tf_op jit(solution)/shard_map/all_gather | solution.py:120
  222.6 4.2 fusion.2
  226.8 26.0 %all-gather.12.cloned.1.call-done = bf16[512,8,128]{0,2,1:T(8,128)(2,1)} async-done(((bf16[128,8,128]{0,2,1:T(8,128)(2,1)}), bf16[512,8,128]{0,2,1:T(8,128)(2,1)}) %all-gather.12.cloned.1.call-update) | async-done | bytes 1048592 | tf_op jit(solution)/shard_map/all_gather | solution.py:121
  252.9 4.4 fusion.73
  257.2 58.4 %all-gather.20.cloned.1.call-done = bf16[1024,2048]{1,0:T(8,128)(2,1)} async-done(((bf16[32,2048]{1,0:T(8,128)(2,1)}), bf16[1024,2048]{1,0:T(8,128)(2,1)}) %all-gather.20.cloned.1.call-update) | async-done | bytes 4194320 | tf_op jit(solution)/shard_map/all_gather | solution.py:91
  319.6 67.0 %all-gather.24.cloned.1.call-done = bf16[1024,3072]{1,0:T(8,128)(2,1)} async-done(((bf16[32,3072]{1,0:T(8,128)(2,1)}), bf16[1024,3072]{1,0:T(8,128)(2,1)}) %all-gather.24.cloned.1.call-update) | async-done | bytes 6291472 | tf_op jit(solution)/shard_map/all_gather | solution.py:138
  386.6 4.9 fusion.75
  391.6 65.8 %all-gather.22.cloned.1.call-done = bf16[1024,3072]{1,0:T(8,128)(2,1)} async-done(((bf16[32,3072]{1,0:T(8,128)(2,1)}), bf16[1024,3072]{1,0:T(8,128)(2,1)}) %all-gather.22.cloned.1.call-update) | async-done | bytes 6291472 | tf_op jit(solution)/shard_map/all_gather | solution.py:137
  457.3 4.9 fusion.74
  462.3 65.8 %all-gather.26.cloned.1.call-done = bf16[1024,3072]{1,0:T(8,128)(2,1)} async-done(((bf16[32,3072]{1,0:T(8,128)(2,1)}), bf16[1024,3072]{1,0:T(8,128)(2,1)}) %all-gather.26.cloned.1.call-update) | async-done | bytes 6291472 | tf_op jit(solution)/shard_map/all_gather | solution.py:139
  528.1 6.5 multiply_convert_fusion
  536.8 5.9 multiply_reduce_fusion.4
  552.2 4.3 bitcast_convert_fusion
  558.8 7.5 fusion.80
  566.3 6.3 fusion.79
  572.7 7.5 convolution_bitcast_fusion
  580.2 25.1 %pad_maximum_fusion = f32[1024,9216]{1,0:T(8,128)} fusion(f32[1024,3072]{1,0:T(8,128)} %convolution_bitcast_fusion, f32[1024,3072]{1,0:T(8,128)} %fusion.80, f32[1024,3072]{1,0:T(8,128)} %fusion.79), kind=kLoop, calls=%fused_computation | loop fusion | flops 18874368 | bytes 75497472 | tf_op jit(solution)/shard_map/concatenate | solution.py:169
  616.0 5.2 fusion.54
  625.3 5.6 fusion.46
  632.2 6.8 fusion.9
  644.5 40.3 %all-reduce.8 = (f32[1024]{0:T(1024)S(1)}, f32[128]{0:T(128)S(1)}, f32[128]{0:T(128)S(1)}, f32[1024]{0:T(1024)S(1)}) all-reduce(f32[1024]{0:T(1024)S(1)} %get-tuple-element.19, f32[128]{0:T(128)S(1)} %get-tuple-element.13, f32[128]{0:T(128)S(1)} %copy-done.33, ...), channel_id=8, replica_groups=mesh['fsdp'=8,'ctx'=4] {'fsdp','ctx'}, use_global_device_ids=true, to_apply=%region_17.18.clone | all-reduce | flops 2304 | bytes 18432
  688.2 271.7 %reduce-scatter.20.cloned.1.call-done = f32[32,9216]{1,0:T(8,128)} async-done(((f32[1024,9216]{1,0:T(8,128)}), f32[32,9216]{1,0:T(8,128)}) %reduce-scatter.20.cloned.1.call-update) | async-done | bytes 1179664 | tf_op jit(solution)/shard_map/reduce_scatter | solution.py:168
  962.2 149.0 %reduce-scatter.14.cloned.1.call-done = f32[32,1024]{1,0:T(8,128)} async-done(((f32[1024,1024]{1,0:T(8,128)}), f32[32,1024]{1,0:T(8,128)}) %reduce-scatter.14.cloned.1.call-update) | async-done | bytes 131088 | tf_op jit(solution)/shard_map/reduce_scatter | solution.py:269
  1111.3 151.4 %reduce-scatter.16.cloned.1.call-done = f32[32,1024]{1,0:T(8,128)} async-done(((f32[1024,1024]{1,0:T(8,128)}), f32[32,1024]{1,0:T(8,128)}) %reduce-scatter.16.cloned.1.call-update) | async-done | bytes 131088 | tf_op jit(solution)/shard_map/reduce_scatter | solution.py:270
  1262.7 187.2 %reduce-scatter.18.cloned.1.call-done = f32[32,2048]{1,0:T(8,128)} async-done(((f32[1024,2048]{1,0:T(8,128)}), f32[32,2048]{1,0:T(8,128)}) %reduce-scatter.18.cloned.1.call-update) | async-done | bytes 262160 | tf_op jit(solution)/shard_map/reduce_scatter | solution.py:271
  1449.9 186.2 %reduce-scatter.12.cloned.1.call-done = f32[32,2048]{1,0:T(8,128)} async-done(((f32[1024,2048]{1,0:T(8,128)}), f32[32,2048]{1,0:T(8,128)}) %reduce-scatter.12.cloned.1.call-update) | async-done | bytes 262160 | tf_op jit(solution)/shard_map/reduce_scatter | solution.py:268
  (176 shorter events, 66.3 us)
Async XLA Ops:
  7.2 66.9 %copy-start.1 = (bf16[1,128,1024]{2,1,0:T(8,128)(2,1)S(1)}, bf16[1,128,1024]{2,1,0:T(8,128)(2,1)}, u32[]{:S(2)}) copy-start(bf16[1,128,1024]{2,1,0:T(8,128)(2,1)} %param.14) | copy-start | bytes 786436
  7.2 63.0 %all-gather.14.cloned.1.call-start = ((), (), s32[]{:S(2)}) async-start(), calls=%async_computation.9 | async-start | bytes 2162688 | tf_op jit(solution)/shard_map/all_gather | solution.py:89
  7.9 120.4 %all-gather.10.cloned.1.call-start = ((), (), s32[]{:S(2)}) async-start(), calls=%async_computation.7 | async-start | bytes 2162688 | tf_op jit(solution)/shard_map/all_gather | solution.py:90
  8.7 183.2 %all-gather.18.cloned.1.call-start = ((), (), s32[]{:S(2)}) async-start(), calls=%async_computation.11 | async-start | bytes 4325376 | tf_op jit(solution)/shard_map/all_gather | solution.py:88
  9.4 213.2 %all-gather.16.cloned.1.call-start = ((), (), s32[]{:S(2)}) async-start(), calls=%async_computation.10 | async-start | bytes 1310720 | tf_op jit(solution)/shard_map/all_gather | solution.py:120
  55.0 21.6 %copy-start.25 = (f32[128]{0:T(128)}, f32[128]{0:T(128)S(1)}, u32[]{:S(2)}) copy-start(f32[128]{0:T(128)S(1)} %convert_element_type.126) | copy-start | bytes 1540
  57.4 141.1 %copy-start.22 = (f32[128]{0:T(128)}, f32[128]{0:T(128)S(1)}, u32[]{:S(2)}) copy-start(f32[128]{0:T(128)S(1)} %add_rsqrt_fusion.3) | copy-start | bytes 1540
  77.6 175.3 %all-gather.12.cloned.1.call-start = ((), (), s32[]{:S(2)}) async-start(), calls=%async_computation.8 | async-start | bytes 1310720 | tf_op jit(solution)/shard_map/all_gather | solution.py:121
  131.3 184.4 %all-gather.20.cloned.1.call-start = ((), (), s32[]{:S(2)}) async-start(), calls=%async_computation.12 | async-start | bytes 4325376 | tf_op jit(solution)/shard_map/all_gather | solution.py:91
  131.9 254.7 %all-gather.24.cloned.1.call-start = ((), (), s32[]{:S(2)}) async-start(), calls=%async_computation.14 | async-start | bytes 6488064 | tf_op jit(solution)/shard_map/all_gather | solution.py:138
  132.6 324.7 %all-gather.22.cloned.1.call-start = ((), (), s32[]{:S(2)}) async-start(), calls=%async_computation.13 | async-start | bytes 6488064 | tf_op jit(solution)/shard_map/all_gather | solution.py:137
  133.4 394.7 %all-gather.26.cloned.1.call-start = ((), (), s32[]{:S(2)}) async-start(), calls=%async_computation.15 | async-start | bytes 6488064 | tf_op jit(solution)/shard_map/all_gather | solution.py:139
  134.1 471.3 %reduce-scatter.22.cloned.1.call-start = ((), (), s32[]{:S(2)}) async-start(), calls=%async_computation.21 | async-start | bytes 1310720
  134.2 68.3 %copy-start.29 = (f32[128]{0:T(128)}, f32[128]{0:T(128)S(1)}, u32[]{:S(2)}) copy-start(f32[128]{0:T(128)S(1)} %convert_element_type.129) | copy-start | bytes 1540
  134.2 185.3 %copy-start.18 = (f32[1024]{0:T(1024)}, f32[1024]{0:T(1024)S(1)}, u32[]{:S(2)}) copy-start(f32[1024]{0:T(1024)S(1)} %convert_element_type.133) | copy-start | bytes 12292
  134.4 118.5 %copy-start.20 = (pred[128,512]{0,1:T(8,128)(4,1)}, pred[128,512]{0,1:T(8,128)(4,1)S(1)}, u32[]{:S(2)}) copy-start(pred[128,512]{0,1:T(8,128)(4,1)S(1)} %broadcast_compare_fusion) | copy-start | bytes 196612
  202.8 54.5 %copy-start.10 = (bf16[128,16,128]{0,2,1:T(8,128)(2,1)}, bf16[128,16,128]{0,2,1:T(8,128)(2,1)S(1)}, u32[]{:S(2)}) copy-start(bf16[128,16,128]{0,2,1:T(8,128)(2,1)S(1)} %fusion.11) | copy-start | bytes 1572868
  226.8 30.4 %copy-start.27 = (f32[8,2,128]{2,1,0:T(2,128)}, f32[8,2,128]{2,1,0:T(2,128)S(1)}, u32[]{:S(2)}) copy-start(f32[8,2,128]{2,1,0:T(2,128)S(1)} %get-tuple-element.52) | copy-start | bytes 24580
  257.2 62.2 %copy-start.12 = (bf16[128,8,2,128]{0,3,2,1:T(8,128)(2,1)}, bf16[128,8,2,128]{0,3,2,1:T(8,128)(2,1)S(1)}, u32[]{:S(2)}) copy-start(bf16[128,8,2,128]{0,3,2,1:T(8,128)(2,1)S(1)} %get-tuple-element.54) | copy-start | bytes 1572868
  319.5 72.1 %copy-start.31 = (f32[128]{0:T(128)}, f32[128]{0:T(128)S(1)}, u32[]{:S(2)}) copy-start(f32[128]{0:T(128)S(1)} %add_rsqrt_fusion.2) | copy-start | bytes 1540
  391.6 136.5 %copy-start.14 = (bf16[1,128,1024]{2,1,0:T(8,128)(2,1)S(1)}, bf16[1,128,1024]{2,1,0:T(8,128)(2,1)}, u32[]{:S(2)}) copy-start(bf16[1,128,1024]{2,1,0:T(8,128)(2,1)} %param.16) | copy-start | bytes 786436
  534.5 8.2 copy-start.7
  534.5 8.2 copy-start.9
  552.1 60.0 %reduce-scatter.24.cloned.1.call-start = ((), (), s32[]{:S(2)}) async-start(), calls=%async_computation.22 | async-start | bytes 1310720 | tf_op jit(solution)/shard_map/convert_element_type | solution.py:244
  558.8 7.5 copy-start.8
  572.6 387.3 %reduce-scatter.20.cloned.1.call-start = ((), (), s32[]{:S(2)}) async-start(), calls=%async_computation.20 | async-start | bytes 38928384 | tf_op jit(solution)/shard_map/reduce_scatter | solution.py:168
  605.3 505.9 %reduce-scatter.14.cloned.1.call-start = ((), (), s32[]{:S(2)}) async-start(), calls=%async_computation.17 | async-start | bytes 4325376 | tf_op jit(solution)/shard_map/reduce_scatter | solution.py:269
  611.8 650.9 %reduce-scatter.16.cloned.1.call-start = ((), (), s32[]{:S(2)}) async-start(), calls=%async_computation.18 | async-start | bytes 4325376 | tf_op jit(solution)/shard_map/reduce_scatter | solution.py:270
  615.9 834.0 %reduce-scatter.18.cloned.1.call-start = ((), (), s32[]{:S(2)}) async-start(), calls=%async_computation.19 | async-start | bytes 8650752 | tf_op jit(solution)/shard_map/reduce_scatter | solution.py:271
  621.3 1014.8 %reduce-scatter.12.cloned.1.call-start = ((), (), s32[]{:S(2)}) async-start(), calls=%async_computation.16 | async-start | bytes 8650752 | tf_op jit(solution)/shard_map/reduce_scatter | solution.py:268
  631.0 8.0 copy-start.17
  632.2 9.7 copy-start.5
  (20 other events, 61.5 us)
Sparse Core Ops, SparseCore 0:
  10.9 59.1 all-gather.13
  73.1 55.2 all-gather.9
  131.4 60.4 all-gather.17
  193.9 28.7 all-gather.15
  224.6 28.2 all-gather.11
  255.7 59.9 all-gather.19
  318.6 68.0 all-gather.23
  389.5 67.7 all-gather.21
  460.2 67.7 all-gather.25
  552.3 25.7 reduce-scatter.21
  580.4 25.7 reduce-scatter.23
  612.5 347.3 reduce-scatter.19
  962.8 148.4 reduce-scatter.13
  1114.0 148.6 reduce-scatter.15
  1265.4 184.4 reduce-scatter.17
  1452.6 183.4 reduce-scatter.11
where the time goes:
time: 1650 us; the launch traced here: 1640 us
  waiting for transfers between devices  1370 us (83%)
  matrix products  109 us (7%)
  blocking collectives  82.5 us (5%)
  other arithmetic  33.2 us (2%)
  local copies, waits for them, and re-layouts  28 us (2%)
    reduce_scatter x1, waiting for transfers between devices, local(): lax.psum_scatter(jnp.concatenate([lax.dot_general(mixed_low, gate_grad_lo...  272 us
    reduce_scatter x1, waiting for transfers between devices, local(): lax.psum_scatter(output_w_grad, ('fsdp', 'ctx'), scatter_dimension=0, til...  187 us
    reduce_scatter x1, waiting for transfers between devices, local(): lax.psum_scatter(query_w_grad, ('fsdp', 'ctx'), scatter_dimension=0, tile...  186 us
    reduce_scatter x1, waiting for transfers between devices, local(): lax.psum_scatter(value_w_grad, ('fsdp', 'ctx'), scatter_dimension=0, tile...  151 us
    reduce_scatter x1, waiting for transfers between devices, local(): lax.psum_scatter(key_w_grad, ('fsdp', 'ctx'), scatter_dimension=0, tiled=...  149 us
    unnamed x2, blocking collectives  82.5 us
    all_gather x1, waiting for transfers between devices, local(): lax.all_gather(up_weight, ('fsdp', 'ctx'), axis=0, tiled=True)  67 us
    all_gather x1, waiting for transfers between devices, local(): lax.all_gather(down_weight, ('fsdp', 'ctx'), axis=0, tiled=True)  65.8 us
  transfers between devices with their start and end apart: 16, of which 14 were waited for; matrix products, arithmetic and copies ran while one was open for 9% of the time, Pallas kernels for 0%

commit v1 on v0

v1 whole, which is shorter than its diff:
```python
import functools
import math

import jax
import jax.numpy as jnp
from jax import lax
from jax.sharding import PartitionSpec as P

HEADS = 16
KV_HEADS = 8
HEAD_DIM = 128
EPSILON = 1e-06
FIRST_AXIS = (((0,), (0,)), ((), ()))
LAST_AXIS = (((1,), (1,)), ((), ()))
BF16 = jnp.bfloat16
F32 = jnp.float32


def mm(left, right, dims=(((1,), (0,)), ((), ()))):
    return lax.dot_general(left, right, dims, preferred_element_type=F32)


def rms(signal):
    return lax.rsqrt(jnp.mean(signal * signal, axis=-1, keepdims=True) + EPSILON)


def norm_back(signal, inverse_rms, gain_vec, upstream):
    unit_values = signal * inverse_rms
    scaled_up = upstream * gain_vec
    inner = scaled_up - unit_values * jnp.mean(scaled_up * unit_values, axis=-1, keepdims=True)
    return (inverse_rms * inner, upstream * unit_values)


def rope_tables(positions, head_width):
    exponent = jnp.arange(head_width // 2, dtype=F32) * (2.0 / head_width)
    inverse = jnp.exp(-exponent * math.log(1000000.0))
    angles = positions.astype(F32)[:, None] * inverse[None, :]
    angles = jnp.concatenate([angles, angles], axis=-1)
    return (jnp.cos(angles), jnp.sin(angles))


def rotate(signal, cosine, sine):
    half = signal.shape[-1] // 2
    turned = jnp.concatenate([-signal[..., half:], signal[..., :half]], axis=-1)
    return signal * cosine + turned * sine


def rotate_back(upstream, cosine, sine):
    half = upstream.shape[-1] // 2
    scaled_up = upstream * sine
    return upstream * cosine + jnp.concatenate(
        [scaled_up[..., half:], -scaled_up[..., :half]], axis=-1
    )


def gather_columns(ctx, shards):
    rows = shards[0].shape[0]
    cut = [s.reshape(rows, ctx, s.shape[1] // ctx).transpose(1, 0, 2) for s in shards]
    widths = [c.shape[2] for c in cut]
    both = jnp.concatenate(cut, axis=2)
    both = lax.all_to_all(both, "ctx", 0, 0, tiled=True)
    both = both.reshape(ctx * rows, -1)
    whole = lax.all_gather(both, "fsdp", axis=0, tiled=True)
    out, at = [], 0
    for width in widths:
        out.append(whole[:, at : at + width])
        at += width
    return out


def scatter_grads(ctx, fsdp, grads):
    rows = grads[0].shape[0] // (ctx * fsdp)
    widths = [g.shape[1] for g in grads]
    both = jnp.concatenate([g.astype(BF16) for g in grads], axis=1)
    both = lax.psum_scatter(both, "fsdp", scatter_dimension=0, tiled=True)
    both = lax.all_to_all(both.reshape(ctx, rows, -1), "ctx", 0, 0, tiled=True)
    out, at = [], 0
    for width in widths:
        piece = both[:, :, at : at + width]
        out.append(piece.transpose(1, 0, 2).reshape(rows, ctx * width).astype(F32))
        at += width
    return out


def ctx_gather(rows):
    return lax.all_gather(rows, "ctx", axis=0, tiled=True)


def ctx_scatter(partial):
    return lax.psum_scatter(partial.astype(BF16), "ctx", scatter_dimension=0, tiled=True).astype(
        F32
    )


def local(
    ctx,
    fsdp,
    hidden_in,
    block_order,
    cotangent,
    q_weight,
    k_weight,
    v_weight,
    o_weight,
    attn_gain,
    query_gain,
    key_gain,
    mlp_gain,
    gate_weight,
    up_weight,
    down_weight,
):
    inputs = hidden_in[0].astype(F32)
    row_count = inputs.shape[0]
    tokens = row_count * ctx
    slots = block_order.shape[1]
    block_len = tokens // slots
    heads, kv_heads = HEADS // ctx, KV_HEADS // ctx
    group = heads // kv_heads
    factor = 1.0 / math.sqrt(HEAD_DIM)
    positions = (
        block_order[0][:, None] * block_len + jnp.arange(block_len, dtype=jnp.int32)[None, :]
    ).reshape(-1)
    cosine, sine = rope_tables(positions, HEAD_DIM)
    cosine, sine = cosine[:, None, :], sine[:, None, :]

    both = ("fsdp", "ctx")
    norm_gain, qgain, kgain, mlp_norm_gain = (
        lax.all_gather(g, both, axis=0, tiled=True).astype(F32)
        for g in (attn_gain, query_gain, key_gain, mlp_gain)
    )
    norm_scale = rms(inputs)
    normed = ctx_gather((inputs * norm_scale * norm_gain).astype(BF16))
    upstream = ctx_gather(cotangent[0])
    q_full, k_full, v_full, o_full = gather_columns(ctx, (q_weight, k_weight, v_weight, o_weight))
    gate_full, up_full, down_full = gather_columns(ctx, (gate_weight, up_weight, down_weight))

    query_proj = mm(normed, q_full).reshape(tokens, heads, HEAD_DIM)
    key_proj = mm(normed, k_full).reshape(tokens, kv_heads, HEAD_DIM)
    value_low = mm(normed, v_full).astype(BF16).reshape(tokens, kv_heads, HEAD_DIM)
    query_scale, key_scale = rms(query_proj), rms(key_proj)
    query_low = (
        rotate(query_proj * query_scale * qgain, cosine, sine)
        .astype(BF16)
        .reshape(tokens, kv_heads, group, HEAD_DIM)
    )
    key_low = rotate(key_proj * key_scale * kgain, cosine, sine).astype(BF16)
    scores = jnp.einsum("rkgd,nkd->kgrn", query_low, key_low, preferred_element_type=F32) * factor
    allowed = positions[None, :] <= positions[:, None]
    weights_exp = jnp.where(allowed, jnp.exp(scores), 0.0)
    denominator = jnp.sum(weights_exp, axis=-1)
    weights_low = weights_exp.astype(BF16)
    numerator = jnp.einsum("kgrn,nkd->rkgd", weights_low, value_low, preferred_element_type=F32)
    denom_rows = jnp.transpose(denominator, (2, 0, 1))[..., None]
    attn_full = numerator / denom_rows
    attn_low = attn_full.astype(BF16).reshape(tokens, heads * HEAD_DIM)
    residual = inputs + ctx_scatter(mm(attn_low, o_full, LAST_AXIS))

    mix_scale = rms(residual)
    mixed = ctx_gather((residual * mix_scale * mlp_norm_gain).astype(BF16))
    gate_val = mm(mixed, gate_full)
    up_val = mm(mixed, up_full)
    sigmoid_gate = jax.nn.sigmoid(gate_val)
    swish_gate = gate_val * sigmoid_gate
    hidden_low = (swish_gate * up_val).astype(BF16)
    result = residual + ctx_scatter(mm(hidden_low, down_full, LAST_AXIS))
    hidden_grad = mm(upstream, down_full)
    gate_back = (
        hidden_grad * up_val * sigmoid_gate * (1.0 + gate_val * (1.0 - sigmoid_gate))
    ).astype(BF16)
    up_back = (hidden_grad * swish_gate).astype(BF16)
    mixed_grad = ctx_scatter(mm(gate_back, gate_full, LAST_AXIS) + mm(up_back, up_full, LAST_AXIS))
    resid_from_norm, mlp_gain_term = norm_back(residual, mix_scale, mlp_norm_gain, mixed_grad)
    residual_grad = cotangent[0].astype(F32) + resid_from_norm
    mlp_grads = scatter_grads(
        ctx,
        fsdp,
        (
            mm(mixed, gate_back, FIRST_AXIS),
            mm(mixed, up_back, FIRST_AXIS),
            mm(upstream, hidden_low, FIRST_AXIS),
        ),
    )
    resid_low = ctx_gather(residual_grad.astype(BF16))

    attn_grad = mm(resid_low, o_full).reshape(tokens, kv_heads, group, HEAD_DIM)
    share_low = (attn_grad / denom_rows).astype(BF16)
    denom_grad = jnp.transpose(jnp.sum(attn_grad * attn_full, axis=-1), (1, 2, 0)) / denominator
    weight_grad = jnp.einsum("rkgd,nkd->kgrn", share_low, value_low, preferred_element_type=F32)
    score_low = (weights_exp * (weight_grad - denom_grad[..., None])).astype(BF16)
    query_rot = (
        jnp.einsum("kgrn,nkd->rkgd", score_low, key_low, preferred_element_type=F32) * factor
    ).reshape(tokens, heads, HEAD_DIM)
    key_rot = (
        jnp.einsum("kgrn,rkgd->nkd", score_low, query_low, preferred_element_type=F32) * factor
    )
    value_back = (
        jnp.einsum("kgrn,rkgd->nkd", weights_low, share_low, preferred_element_type=F32)
        .reshape(tokens, kv_heads * HEAD_DIM)
        .astype(BF16)
    )
    query_grad, query_term = norm_back(
        query_proj, query_scale, qgain, rotate_back(query_rot, cosine, sine)
    )
    key_grad, key_term = norm_back(key_proj, key_scale, kgain, rotate_back(key_rot, cosine, sine))
    query_back = query_grad.reshape(tokens, heads * HEAD_DIM).astype(BF16)
    key_back = key_grad.reshape(tokens, kv_heads * HEAD_DIM).astype(BF16)
    normed_grad = ctx_scatter(
        mm(query_back, q_full, LAST_AXIS)
        + mm(key_back, k_full, LAST_AXIS)
        + mm(value_back, v_full, LAST_AXIS)
    )
    input_from_norm, attn_gain_term = norm_back(inputs, norm_scale, norm_gain, normed_grad)
    input_grad = residual_grad + input_from_norm
    attn_grads = scatter_grads(
        ctx,
        fsdp,
        (
            mm(normed, query_back, FIRST_AXIS),
            mm(normed, key_back, FIRST_AXIS),
            mm(normed, value_back, FIRST_AXIS),
            mm(resid_low, attn_low, FIRST_AXIS),
        ),
    )
    gains = (
        jnp.sum(attn_gain_term, axis=0),
        jnp.sum(query_term, axis=(0, 1)),
        jnp.sum(key_term, axis=(0, 1)),
        jnp.sum(mlp_gain_term, axis=0),
    )
    gains = [lax.psum_scatter(g, both, scatter_dimension=0, tiled=True) for g in gains]
    return (
        result.astype(BF16)[None],
        input_grad[None],
        *attn_grads,
        *gains,
        *mlp_grads,
    )


def solution(mesh):
    ctx, fsdp = mesh.shape["ctx"], mesh.shape["fsdp"]
    tokens = P("fsdp", "ctx", None)
    matrix = P(("fsdp", "ctx"), None)
    vector = P(("fsdp", "ctx"))
    return jax.shard_map(
        functools.partial(local, ctx, fsdp),
        mesh=mesh,
        in_specs=(tokens, P("fsdp", None), tokens)
        + (matrix,) * 4
        + (vector,) * 4
        + (matrix,) * 3,
        out_specs=(tokens,) * 2 + (matrix,) * 4 + (vector,) * 4 + (matrix,) * 3,
        check_vma=False,
    )
```

time: 1650 us -> 549 us (0.33)
  waiting for transfers between devices: 1370 us -> 267 us
  blocking collectives: 82.5 us -> 143 us
  matrix products: 109 us -> 50.2 us
    reduce_scatter x5 -> x6, waiting for transfers between devices: 946 us -> 130 us  [the longest x2 69.4 us: scatter_grads(): both = lax.psum_scatter(both, 'fsdp', scatter_dimension=0, tiled=True)]
    all_gather x9 -> x6, waiting for transfers between devices: 424 us -> 136 us  [the longest x2 68.8 us: gather_columns(): whole = lax.all_gather(both, 'fsdp', axis=0, tiled=True)]
    all_to_all x0 -> x2, blocking collectives: none -> 60.1 us  [gather_columns(): both = lax.all_to_all(both, 'ctx', 0, 0, tiled=True)]
    dot_general x26, matrix products: 107 us -> 49.4 us  [the longest x21 40.6 us: mm(): return lax.dot_general(left, right, dims, preferred_element_type=F32)]
    concatenate x1 -> x5, other arithmetic: 25.1 us -> 6.38 us  [the longest x2 4.41 us: scatter_grads(): both = jnp.concatenate([g.astype(BF16) for g in grads], axis=1)]
  transfers between devices with their start and end apart: 16 -> 14, of which waited for: 14 -> 11; matrix products, arithmetic and copies ran while one was open for 9% -> 12% of each run, Pallas kernels for 0% -> 0%
where the time goes in v1:
time: 549 us; the launch traced here: 547 us
  waiting for transfers between devices  267 us (49%)
  blocking collectives  143 us (26%)
  matrix products  50.2 us (9%)
  local copies, waits for them, and re-layouts  36.7 us (7%)
  other arithmetic  25.1 us (5%)
  between operations  15 us (3%)
  starting transfers between devices  10.1 us (2%)
    unnamed x2, blocking collectives  83.3 us
    reduce_scatter x2, waiting for transfers between devices, scatter_grads(): both = lax.psum_scatter(both, 'fsdp', scatter_dimension=0, tiled=True)  69.4 us
    all_gather x2, waiting for transfers between devices, gather_columns(): whole = lax.all_gather(both, 'fsdp', axis=0, tiled=True)  68.8 us
    all_gather x4, waiting for transfers between devices, ctx_gather(): return lax.all_gather(rows, 'ctx', axis=0, tiled=True)  67.2 us
    reduce_scatter x4, waiting for transfers between devices, ctx_scatter(): lax.psum_scatter(partial.astype(BF16), 'ctx', scatter_dimension=0, tiled=...  60.7 us
    all_to_all x2, blocking collectives, gather_columns(): both = lax.all_to_all(both, 'ctx', 0, 0, tiled=True)  60.1 us
    dot_general x21, matrix products, mm(): return lax.dot_general(left, right, dims, preferred_element_type=F32)  40.6 us
    unnamed x114, local copies, waits for them, and re-layouts  27.2 us
  transfers between devices with their start and end apart: 14, of which 11 were waited for; matrix products, arithmetic and copies ran while one was open for 12% of the time, Pallas kernels for 0%

profile of v1, /device:TPU:0, one launch (start us, length us, event | category | flops | bytes accessed | tf_op | source)
XLA Modules:
  0.0 547.2 jit_solution(12101319528620576484)
XLA Ops:
  11.7 42.1 %all-reduce.9 = (bf16[1024]{0:T(1024)(128)(2,1)S(1)}, bf16[128]{0:T(256)(128)(2,1)S(1)}, bf16[128]{0:T(256)(128)(2,1)S(1)}, bf16[1024]{0:T(1024)(128)(2,1)S(1)}) all-reduce(bf16[1024]{0:T(1024)(128)(2,1)S(1)} %dynamic-update-slice, bf16[128]{0:T(256)(128)(2,1)S(1)} %dynamic-update-slice.1, ...), channel_id=1, replica_groups=mesh['fsdp'=8,'ctx'=4] {'fsdp','ctx'}, use_global_device_ids=true, to_apply=%add | all-reduce | flops 2304 | bytes 9216
  59.6 24.3 %all_to_all.20 = bf16[4,32,1536]{2,1,0:T(8,128)(2,1)} all-to-all(bf16[4,32,1536]{2,1,0:T(8,128)(2,1)S(1)} %copy.74), channel_id=1, replica_groups=mesh['fsdp'=8,'ctx'=4] {'ctx'}, dimensions={0} | all-to-all | bytes 786432 | tf_op jit(solution)/shard_map/all_to_all | solution.py:61
  86.9 4.2 all-gather.8.cloned.1.call-done
  91.1 33.0 %all-gather.10.cloned.1.call-done = bf16[1024,1536]{1,0:T(8,128)(2,1)} async-done(((bf16[128,1536]{1,0:T(8,128)(2,1)}), bf16[1024,1536]{1,0:T(8,128)(2,1)}) %all-gather.10.cloned.1.call-update) | async-done | bytes 3145744 | tf_op jit(solution)/shard_map/all_gather | solution.py:63
  126.9 2.0 multiply_reduce_fusion.3
  133.0 2.0 fusion.77
  138.5 35.9 %all_to_all.21 = bf16[4,32,2304]{2,1,0:T(8,128)(2,1)} all-to-all(bf16[4,32,2304]{2,1,0:T(8,128)(2,1)S(1)} %copy.78), channel_id=1, replica_groups=mesh['fsdp'=8,'ctx'=4] {'ctx'}, dimensions={0} | all-to-all | bytes 1179648 | tf_op jit(solution)/shard_map/all_to_all | solution.py:61
  179.5 35.8 %all-gather.14.cloned.1.call-done = bf16[1024,2304]{1,0:T(8,128)(2,1)} async-done(((bf16[128,2304]{1,0:T(8,128)(2,1)}), bf16[1024,2304]{1,0:T(8,128)(2,1)}) %all-gather.14.cloned.1.call-update) | async-done | bytes 4718608 | tf_op jit(solution)/shard_map/all_gather | solution.py:63
  215.2 30.0 %all-gather.12.cloned.1.call-done = bf16[512,1024]{1,0:T(8,128)(2,1)} async-done(((bf16[128,1024]{1,0:T(8,128)(2,1)}), bf16[512,1024]{1,0:T(8,128)(2,1)}) %all-gather.12.cloned.1.call-update) | async-done | bytes 1048592 | tf_op jit(solution)/shard_map/all_gather | solution.py:86
  245.2 4.0 fusion.14
  249.2 3.6 fusion.18
  252.8 21.3 %all-gather.18.cloned.1.call-done = bf16[1,512,1024]{2,1,0:T(8,128)(2,1)} async-done(((bf16[1,128,1024]{2,1,0:T(8,128)(2,1)}), bf16[1,512,1024]{2,1,0:T(8,128)(2,1)}) %all-gather.18.cloned.1.call-update) | async-done | bytes 1048592 | tf_op jit(solution)/shard_map/all_gather | solution.py:86
  274.1 5.0 fusion.7
  279.1 3.0 fusion.16
  282.1 3.5 add_convert_fusion.1
  285.7 26.8 %reduce-scatter.15.cloned.1.call-done = bf16[128,1024]{1,0:T(8,128)(2,1)} async-done(((bf16[512,1024]{1,0:T(8,128)(2,1)}), bf16[128,1024]{1,0:T(8,128)(2,1)}) %reduce-scatter.15.cloned.1.call-update) | async-done | bytes 262160 | tf_op jit(solution)/shard_map/reduce_scatter | solution.py:90
  313.8 1.9 fusion.74
  315.8 2.6 convolution_convert_fusion.1
  320.9 2.5 pad_maximum_fusion
  323.4 6.9 %copy.113 = bf16[1024,2304]{1,0:T(8,128)(2,1)} copy(bf16[1024,2304]{0,1:T(8,128)(2,1)} %pad_maximum_fusion) | data formatting | bytes 9437184
  330.6 11.7 %all-gather.16.cloned.1.call-done = bf16[512,1024]{1,0:T(8,128)(2,1)} async-done(((bf16[128,1024]{1,0:T(8,128)(2,1)}), bf16[512,1024]{1,0:T(8,128)(2,1)}) %all-gather.16.cloned.1.call-update) | async-done | bytes 1048592 | tf_op jit(solution)/shard_map/all_gather | solution.py:86
  342.3 2.4 multiply_reduce_fusion.2
  344.8 4.0 fusion.1
  367.3 5.0 copy.111
  373.4 3.4 convolution_convert_fusion.3
  376.8 22.2 %reduce-scatter.21.cloned.1.call-done = bf16[128,2304]{1,0:T(8,128)(2,1)} async-done(((bf16[1024,2304]{1,0:T(8,128)(2,1)}), bf16[128,2304]{1,0:T(8,128)(2,1)}) %reduce-scatter.21.cloned.1.call-update) | async-done | bytes 589840 | tf_op jit(solution)/shard_map/reduce_scatter | solution.py:75
  399.0 4.6 all-to-all-start.3
  403.6 32.6 %reduce-scatter.17.cloned.1.call-done = bf16[128,1024]{1,0:T(8,128)(2,1)} async-done(((bf16[512,1024]{1,0:T(8,128)(2,1)}), bf16[128,1024]{1,0:T(8,128)(2,1)}) %reduce-scatter.17.cloned.1.call-update) | async-done | bytes 262160 | tf_op jit(solution)/shard_map/reduce_scatter | solution.py:90
  437.4 47.3 %reduce-scatter.19.cloned.1.call-done = bf16[128,1536]{1,0:T(8,128)(2,1)} async-done(((bf16[1024,1536]{1,0:T(8,128)(2,1)}), bf16[128,1536]{1,0:T(8,128)(2,1)}) %reduce-scatter.19.cloned.1.call-update) | async-done | bytes 393232 | tf_op jit(solution)/shard_map/reduce_scatter | solution.py:75
  484.6 4.6 all-to-all-start.2
  489.2 41.2 %all-reduce.8 = (f32[1024]{0:T(1024)S(1)}, f32[128]{0:T(128)S(1)}, f32[128]{0:T(128)S(1)}, f32[1024]{0:T(1024)S(1)}) all-reduce(f32[1024]{0:T(1024)S(1)} %get-tuple-element.19, f32[128]{0:T(128)S(1)} %get-tuple-element.13, f32[128]{0:T(128)S(1)} %get-tuple-element.17, ...), channel_id=8, replica_groups=mesh['fsdp'=8,'ctx'=4] {'fsdp','ctx'}, use_global_device_ids=true, to_apply=%region_16.17.clone | all-reduce | flops 2304 | bytes 18432
  532.8 2.3 fusion.46
  (222 shorter events, 60.8 us)
Async XLA Ops:
  7.2 76.8 %copy-start.38 = (s32[1,8]{1,0:T(1,128)S(1)}, s32[1,8]{1,0:T(1,128)}, u32[]{:S(2)}) copy-start(s32[1,8]{1,0:T(1,128)} %param.15) | copy-start | bytes 100
  7.2 83.9 %all-gather.8.cloned.1.call-start = ((), (), s32[]{:S(2)}) async-start(), calls=%async_computation.10 | async-start | bytes 1310720 | tf_op jit(solution)/shard_map/all_gather | solution.py:86
  55.6 68.5 %all-gather.10.cloned.1.call-start = ((), (), s32[]{:S(2)}) async-start(), calls=%async_computation.11 | async-start | bytes 3538944 | tf_op jit(solution)/shard_map/all_gather | solution.py:63
  83.9 91.8 %reduce-scatter.11.cloned.1.call-start = ((), (), s32[]{:S(2)}) async-start(), calls=%async_computation.12 | async-start | bytes 1310720 | tf_op jit(solution)/shard_map/reduce_scatter | solution.py:90
  86.0 44.0 %copy-start.8 = (f32[512,128]{0,1:T(8,128)}, f32[512,128]{0,1:T(8,128)S(1)}, u32[]{:S(2)}) copy-start(f32[512,128]{0,1:T(8,128)S(1)} %get-tuple-element.52) | copy-start | bytes 786436
  91.1 35.8 %copy-start.6 = (bf16[512,1024]{1,0:T(8,128)(2,1)S(1)}, bf16[512,1024]{1,0:T(8,128)(2,1)}, u32[]{:S(2)}) copy-start(bf16[512,1024]{1,0:T(8,128)(2,1)} %all-gather.8.cloned.1.call-done) | copy-start | bytes 3145732
  135.1 2.8 copy-start.33
  135.1 2.9 copy-start.34
  137.6 38.1 %copy-start = (bf16[1,128,1024]{2,1,0:T(8,128)(2,1)S(1)}, bf16[1,128,1024]{2,1,0:T(8,128)(2,1)}, u32[]{:S(2)}) copy-start(bf16[1,128,1024]{2,1,0:T(8,128)(2,1)} %param.14) | copy-start | bytes 786436
  137.6 77.6 %all-gather.14.cloned.1.call-start = ((), (), s32[]{:S(2)}) async-start(), calls=%async_computation.14 | async-start | bytes 5308416 | tf_op jit(solution)/shard_map/all_gather | solution.py:63
  174.4 70.9 %all-gather.12.cloned.1.call-start = ((), (), s32[]{:S(2)}) async-start(), calls=%async_computation.13 | async-start | bytes 1310720 | tf_op jit(solution)/shard_map/all_gather | solution.py:86
  178.7 95.4 %all-gather.18.cloned.1.call-start = ((), (), s32[]{:S(2)}) async-start(), calls=%async_computation.19 | async-start | bytes 1310720 | tf_op jit(solution)/shard_map/all_gather | solution.py:86
  179.3 133.2 %reduce-scatter.15.cloned.1.call-start = ((), (), s32[]{:S(2)}) async-start(), calls=%async_computation.16 | async-start | bytes 1310720 | tf_op jit(solution)/shard_map/reduce_scatter | solution.py:90
  245.2 4.0 copy-start.35
  279.1 3.0 copy-start.46
  279.1 6.5 %copy-start.45 = (bf16[512,768]{1,0:T(8,128)(2,1)}, bf16[512,768]{1,0:T(8,128)(2,1)S(1)}, u32[]{:S(2)}) copy-start(bf16[512,768]{1,0:T(8,128)(2,1)S(1)} %get-tuple-element.30) | copy-start | bytes 2359300
  282.1 30.4 %copy-start.3 = (bf16[128,1024]{1,0:T(8,128)(2,1)S(1)}, bf16[128,1024]{1,0:T(8,128)(2,1)}, u32[]{:S(2)}) copy-start(bf16[128,1024]{1,0:T(8,128)(2,1)} %reduce-scatter.11.cloned.1.call-done) | copy-start | bytes 786436
  282.1 31.7 %copy-start.14 = (bf16[1,128,1024]{2,1,0:T(8,128)(2,1)S(1)}, bf16[1,128,1024]{2,1,0:T(8,128)(2,1)}, u32[]{:S(2)}) copy-start(bf16[1,128,1024]{2,1,0:T(8,128)(2,1)} %param.16) | copy-start | bytes 786436
  285.6 56.7 %all-gather.16.cloned.1.call-start = ((), (), s32[]{:S(2)}) async-start(), calls=%async_computation.17 | async-start | bytes 1310720 | tf_op jit(solution)/shard_map/all_gather | solution.py:86
  315.7 83.3 %reduce-scatter.21.cloned.1.call-start = ((), (), s32[]{:S(2)}) async-start(), calls=%async_computation.21 | async-start | bytes 5308416 | tf_op jit(solution)/shard_map/reduce_scatter | solution.py:75
  330.3 12.0 %copy-start.24 = (f32[512,2,2,128]{0,3,2,1:T(8,128)S(1)}, f32[512,2,2,128]{0,3,2,1:T(8,128)}, u32[]{:S(2)}) copy-start(f32[512,2,2,128]{0,3,2,1:T(8,128)} %get-tuple-element.61) | copy-start | bytes 3145732
  330.4 105.8 %reduce-scatter.17.cloned.1.call-start = ((), (), s32[]{:S(2)}) async-start(), calls=%async_computation.18 | async-start | bytes 1310720 | tf_op jit(solution)/shard_map/reduce_scatter | solution.py:90
  344.7 4.0 copy-start.26
  344.7 4.0 copy-start.23
  353.4 4.2 copy-start.18
  357.1 2.9 copy-start.44
  362.6 122.0 %reduce-scatter.19.cloned.1.call-start = ((), (), s32[]{:S(2)}) async-start(), calls=%async_computation.20 | async-start | bytes 3538944 | tf_op jit(solution)/shard_map/reduce_scatter | solution.py:75
  372.3 160.5 %copy-start.15 = (bf16[1,128,1024]{2,1,0:T(8,128)(2,1)S(1)}, bf16[1,128,1024]{2,1,0:T(8,128)(2,1)}, u32[]{:S(2)}) copy-start(bf16[1,128,1024]{2,1,0:T(8,128)(2,1)} %param.16) | copy-start | bytes 786436
  372.3 160.5 %copy-start.16 = (bf16[128,1024]{1,0:T(8,128)(2,1)S(1)}, bf16[128,1024]{1,0:T(8,128)(2,1)}, u32[]{:S(2)}) copy-start(bf16[128,1024]{1,0:T(8,128)(2,1)} %reduce-scatter.15.cloned.1.call-done) | copy-start | bytes 786436
  372.3 160.5 %reduce-scatter.13.cloned.1.call-start = ((), (), s32[]{:S(2)}) async-start(), calls=%async_computation.15 | async-start | bytes 1310720 | tf_op jit(solution)/shard_map/reduce_scatter | solution.py:90
  399.0 38.4 %all-to-all-start.3 = ((bf16[4,32,2304]{2,1,0:T(8,128)(2,1)}), bf16[4,32,2304]{2,1,0:T(8,128)(2,1)S(1)}, u32[]{:S(2)}, u32[]{:S(2)}) async-start(bf16[4,32,2304]{2,1,0:T(8,128)(2,1)} %bitcast.251), calls=%async_computation.7 | async-start | bytes 1179648 | tf_op jit(solution)/shard_map/all_to_all | solution.py:76
  484.6 52.9 %all-to-all-start.2 = ((bf16[4,32,1536]{2,1,0:T(8,128)(2,1)}), bf16[4,32,1536]{2,1,0:T(8,128)(2,1)S(1)}, u32[]{:S(2)}, u32[]{:S(2)}) async-start(bf16[4,32,1536]{2,1,0:T(8,128)(2,1)} %bitcast.254), calls=%async_computation.6 | async-start | bytes 786432 | tf_op jit(solution)/shard_map/all_to_all | solution.py:76
  (32 other events, 55.6 us)
Sparse Core Ops, SparseCore 0:
  55.7 35.3 all-gather.7
  93.0 31.0 all-gather.9
  137.8 37.9 reduce-scatter.10
  177.5 37.6 all-gather.13
  217.2 27.9 all-gather.11
  246.7 27.3 all-gather.17
  285.8 26.6 reduce-scatter.14
  315.8 26.4 all-gather.15
  345.8 53.1 reduce-scatter.20
  401.1 34.9 reduce-scatter.16
  439.5 45.0 reduce-scatter.18
  486.8 31.3 reduce-scatter.12

commit v2 on v1

--- a/solution.py
+++ b/solution.py
@@ -1,9 +1,12 @@
 import functools
 import math
+import types
 
 import jax
 import jax.numpy as jnp
 from jax import lax
+from jax.experimental import pallas as pl
+from jax.experimental.pallas import tpu as pltpu
 from jax.sharding import PartitionSpec as P
 
 HEADS = 16
@@ -14,6 +17,7 @@
 LAST_AXIS = (((1,), (1,)), ((), ()))
 BF16 = jnp.bfloat16
 F32 = jnp.float32
+VMEM_LIMIT = 67043328
 
 
 def mm(left, right, dims=(((1,), (0,)), ((), ()))):
@@ -238,13 +242,737 @@
     )
 
 
+def rope_fwd(u, cosine, sine):
+    return u * cosine + pltpu.roll(u, HEAD_DIM // 2, u.ndim - 1) * sine
+
+
+def rope_bwd(du, cosine, sine):
+    return du * cosine - pltpu.roll(du, HEAD_DIM // 2, du.ndim - 1) * sine
+
+
+class Sizes:
+    def __init__(self, ctx, fsdp, rows, shards):
+        self.ctx, self.fsdp, self.rows = ctx, fsdp, rows
+        self.chips = fsdp // 2
+        self.shard = shards[0].shape[0]
+        self.block = self.shard * ctx
+        self.width = self.block * fsdp
+        self.tokens = rows * ctx
+        self.heads, self.kv = HEADS // ctx, KV_HEADS // ctx
+        self.cols = [s.shape[1] // ctx for s in shards]
+        self.attn_cols = sum(self.cols[:4])
+        self.mlp_cols = sum(self.cols[4:])
+        self.lines = self.width // HEAD_DIM
+        self.gain_rows = 8 * ((2 * self.lines + 2 + 7) // 8)
+
+
+def scratch_of(n):
+    bf, f32 = (lambda *s: pltpu.VMEM(s, BF16)), (lambda *s: pltpu.VMEM(s, F32))
+    sem = lambda *s: pltpu.SemaphoreType.DMA(s)
+    c, d, s, h, kv = n.ctx, n.width, n.tokens, n.heads, n.kv
+    ff = n.cols[4]
+    out = dict(
+        wa=bf(d, n.attn_cols),
+        wm=bf(d, n.mlp_cols),
+        xb=bf(c, n.rows, d),
+        gb=bf(c, n.rows, d),
+        mb=bf(c, n.rows, d),
+        rb=bf(c, n.rows, d),
+        xn=bf(s, d),
+        qp=f32(h, s, HEAD_DIM),
+        kp=f32(kv, s, HEAD_DIM),
+        qr=bf(h, s, HEAD_DIM),
+        kr=bf(kv, s, HEAD_DIM),
+        vv=bf(kv, s, HEAD_DIM),
+        es=f32(h, s, s),
+        af=f32(h, s, HEAD_DIM),
+        at=bf(s, h * HEAD_DIM),
+        da=f32(h, s, HEAD_DIM),
+        dk=f32(kv, s, HEAD_DIM),
+        dv=f32(kv, s, HEAD_DIM),
+        ds=bf(s, s),
+        eb=bf(s, s),
+        wb=bf(s, HEAD_DIM),
+        dqkv=bf(s, (h + 2 * kv) * HEAD_DIM),
+        hid=bf(s, ff),
+        dgu=bf(s, 2 * ff),
+        ho=f32(n.rows, d),
+        dh=f32(n.rows, d),
+        gv=f32(2, 1, d),
+        ga=bf(d, n.attn_cols),
+        gm=bf(d, n.mlp_cols),
+        ga_sib=bf(n.chips, n.block, n.attn_cols),
+        gm_sib=bf(n.chips, n.block, n.mlp_cols),
+        ga_in=bf(n.chips - 1, n.block, n.attn_cols),
+        gm_in=bf(n.chips - 1, n.block, n.mlp_cols),
+        ga_z=bf(n.block, n.attn_cols),
+        gm_z=bf(n.block, n.mlp_cols),
+        ga_land=bf(c, n.shard, n.attn_cols),
+        gm_land=bf(c, n.shard, n.mlp_cols),
+        local_sem=sem(9),
+    )
+    for name in ("o", "x2", "x1"):
+        out["p_" + name] = bf(c, n.rows, d)
+        out["l_" + name] = bf(c, n.rows, d)
+        out["r_" + name] = bf(c, n.rows, d)
+        out["sem_" + name] = sem(4, c)
+    out["p_y"] = bf(c, n.rows, d)
+    out["i_y"] = bf(c - 1, n.rows, d)
+    out["sem_y"] = sem(2, c)
+    out["sem_g"] = sem(2, c)
+    for name in ("xb", "mb", "rb"):
+        out["sem_" + name] = sem(3, c)
+    out["sem_wa"] = sem(2, c - 1, 4)
+    out["sem_wm"] = sem(2, c - 1, 3)
+    for name in ("wa", "wm"):
+        out["sem_p" + name] = sem(2, n.chips)
+        out["sem_s" + name] = sem(2, n.chips)
+    for name in ("ga", "gm"):
+        out["sem_s" + name] = sem(2, n.chips)
+        out["sem_p" + name] = sem(2, n.chips)
+        out["sem_z" + name] = sem(2, c)
+    for name in ("g0", "g1"):
+        out[name + "_in"] = f32(n.chips + c, n.gain_rows, HEAD_DIM)
+        out[name + "_acc"] = f32(4, n.gain_rows, HEAD_DIM)
+        out["sem_" + name] = sem(2, n.chips + c)
+    return out
+
+
+def layer_kernel(n, names, *refs):
+    r = types.SimpleNamespace(**dict(zip(names, refs)))
+    c, f = lax.axis_index("ctx"), lax.axis_index("fsdp")
+    chip, core = f // 2, f % 2
+    sibling = chip * 2 + 1 - core
+    rows, d, block, shard = n.rows, n.width, n.block, n.shard
+    sends = []
+
+    def ahead(by):
+        return lax.rem(c + by, n.ctx)
+
+    def behind(by):
+        return lax.rem(c + n.ctx - by, n.ctx)
+
+    def chip_ahead(by):
+        return lax.rem(chip + by, n.chips)
+
+    def chip_behind(by):
+        return lax.rem(chip + n.chips - by, n.chips)
+
+    def remote(src, dst, send_sem, recv_sem, to_f=None, to_c=None):
+        return pltpu.make_async_remote_copy(
+            src_ref=src,
+            dst_ref=dst,
+            send_sem=send_sem,
+            recv_sem=recv_sem,
+            device_id={"fsdp": f if to_f is None else to_f, "ctx": c if to_c is None else to_c},
+            device_id_type=pl.DeviceIdType.MESH,
+        )
+
+    def send(src, dst, send_sem, recv_sem, to_f=None, to_c=None):
+        copy = remote(src, dst, send_sem, recv_sem, to_f, to_c)
+        copy.start()
+        sends.append(copy.wait_send)
+
+    def arrived(dst, recv_sem):
+        remote(dst, dst, recv_sem, recv_sem).wait_recv()
+
+    def send_if(cond, src, dst, send_sem, recv_sem, to_c):
+        copy = remote(src, dst, send_sem, recv_sem, None, to_c)
+        pl.when(cond)(copy.start)
+        sends.append(lambda: pl.when(cond)(copy.wait_send))
+
+    barrier = pltpu.get_barrier_semaphore()
+
+    def greet(to_f, to_c):
+        pl.semaphore_signal(
+            barrier,
+            inc=1,
+            device_id={"fsdp": to_f, "ctx": to_c},
+            device_id_type=pl.DeviceIdType.MESH,
+        )
+
+    for by in range(1, n.ctx):
+        greet(f, ahead(by))
+    for by in range(1, n.chips):
+        greet(chip_ahead(by) * 2 + core, c)
+    greet(sibling, c)
+    pl.semaphore_wait(barrier, n.ctx - 1 + n.chips)
+
+    right, left = jnp.minimum(c + 1, n.ctx - 1), jnp.maximum(c - 1, 0)
+
+    def gather_start(src, buf, sem):
+        send_if(c + 1 < n.ctx, src, buf.at[c], sem.at[0, 0], sem.at[2, c], right)
+        send_if(c > 0, src, buf.at[c], sem.at[1, 0], sem.at[2, c], left)
+
+    def gather_relay(buf, sem):
+        for by in range(1, n.ctx):
+            low = jnp.maximum(c - by, 0)
+            pl.when(c - by >= 0)(lambda: arrived(buf.at[low], sem.at[2, low]))
+            send_if(
+                (c - by >= 0) & (c + 1 < n.ctx),
+                buf.at[low],
+                buf.at[low],
+                sem.at[0, by],
+                sem.at[2, low],
+                right,
+            )
+            high = jnp.minimum(c + by, n.ctx - 1)
+            pl.when(c + by < n.ctx)(lambda: arrived(buf.at[high], sem.at[2, high]))
+            send_if(
+                (c + by < n.ctx) & (c > 0),
+                buf.at[high],
+                buf.at[high],
+                sem.at[1, by],
+                sem.at[2, high],
+                left,
+            )
+
+    def scatter(part, from_left, from_right, sem, fill=None):
+        for step in range(n.ctx - 1):
+            target = step
+            down = c > target
+
+            @pl.when(down & (c + 1 < n.ctx))
+            def _():
+                arrived(from_right.at[target], sem.at[3, target])
+                part[target] = (part[target].astype(F32) + from_right[target].astype(F32)).astype(
+                    BF16
+                )
+
+            send_if(
+                down,
+                part.at[target],
+                from_right.at[target],
+                sem.at[1, target],
+                sem.at[3, target],
+                left,
+            )
+            target = n.ctx - 1 - step
+            up = c < target
+
+            @pl.when(up & (c > 0))
+            def _():
+                arrived(from_left.at[target], sem.at[2, target])
+                part[target] = (part[target].astype(F32) + from_left[target].astype(F32)).astype(
+                    BF16
+                )
+
+            send_if(
+                up, part.at[target], from_left.at[target], sem.at[0, target], sem.at[2, target], right
+            )
+            if fill:
+                fill(step)
+
+    def scatter_total(part, from_left, from_right, sem, out):
+        out[...] = out[...] + part[c].astype(F32)
+
+        @pl.when(c > 0)
+        def _():
+            arrived(from_left.at[c], sem.at[2, c])
+            out[...] = out[...] + from_left[c].astype(F32)
+
+        @pl.when(c + 1 < n.ctx)
+        def _():
+            arrived(from_right.at[c], sem.at[3, c])
+            out[...] = out[...] + from_right[c].astype(F32)
+
+    def block_of(buf, index):
+        return buf.at[pl.ds(pl.multiple_of(index * block, block), block), :]
+
+    def piece_of(buf, line, at, width):
+        start = pl.multiple_of(f * block + line * shard, shard)
+        return buf.at[pl.ds(start, shard), pl.ds(at, width)]
+
+    def weights_send(shards, cols, buf, sem):
+        for by in range(1, n.ctx):
+            at = 0
+            for i, (src, width) in enumerate(zip(shards, cols)):
+                column = pl.multiple_of(ahead(by) * width, HEAD_DIM)
+                send(
+                    src.at[:, pl.ds(column, width)],
+                    piece_of(buf, c, at, width),
+                    sem.at[0, by - 1, i],
+                    sem.at[1, by - 1, i],
+                    None,
+                    ahead(by),
+                )
+                at += width
+
+    def weights_own(shards, cols, buf, first):
+        at, out = 0, []
+        for i, (src, width) in enumerate(zip(shards, cols)):
+            column = pl.multiple_of(c * width, HEAD_DIM)
+            copy = pltpu.make_async_copy(
+                src.at[:, pl.ds(column, width)],
+                piece_of(buf, c, at, width),
+                r.local_sem.at[first + i],
+            )
+            copy.start()
+            out.append(copy)
+            at += width
+        return out
+
+    def weights_spread(own, cols, buf, sem, plane_sem, sib_sem):
+        for copy in own:
+            copy.wait()
+        for by in range(1, n.ctx):
+            at = 0
+            for i, width in enumerate(cols):
+                arrived(piece_of(buf, behind(by), at, width), sem.at[1, by - 1, i])
+                at += width
+        mine = block_of(buf, f)
+        for by in range(1, n.chips):
+            send(
+                mine, mine, plane_sem.at[0, by], plane_sem.at[1, by], chip_ahead(by) * 2 + core
+            )
+        send(mine, mine, sib_sem.at[0, 0], sib_sem.at[1, 0], sibling)
+
+    def weights_forward(buf, plane_sem, sib_sem):
+        for by in range(1, n.chips):
+            piece = block_of(buf, chip_behind(by) * 2 + core)
+            arrived(piece, plane_sem.at[1, by])
+            send(piece, piece, sib_sem.at[0, by], sib_sem.at[1, by], sibling)
+
+    def weights_wait(buf, sib_sem):
+        for by in range(n.chips):
+            arrived(block_of(buf, chip_behind(by) * 2 + 1 - core), sib_sem.at[1, by])
+
+    def grads_pair(buf, sib_in, sib_sem):
+        for by in range(n.chips):
+            send(
+                block_of(buf, chip_ahead(by) * 2 + 1 - core),
+                sib_in.at[by],
+                sib_sem.at[0, by],
+                sib_sem.at[1, by],
+                sibling,
+            )
+
+    def grads_plane(buf, sib_in, sib_sem, plane_in, plane_sem):
+        for by in range(1, n.chips):
+            arrived(sib_in.at[by], sib_sem.at[1, by])
+            piece = block_of(buf, chip_ahead(by) * 2 + core)
+            piece[...] = (piece[...].astype(F32) + sib_in[by].astype(F32)).astype(BF16)
+            send(
+                piece,
+                plane_in.at[by - 1],
+                plane_sem.at[0, by],
+                plane_sem.at[1, by],
+                chip_ahead(by) * 2 + core,
+            )
+
+    def grads_line(buf, sib_in, sib_sem, plane_in, plane_sem, total, land, line_sem):
+        arrived(sib_in.at[0], sib_sem.at[1, 0])
+        for by in range(1, n.chips):
+            arrived(plane_in.at[by - 1], plane_sem.at[1, by])
+        acc = block_of(buf, f)[...].astype(F32) + sib_in[0].astype(F32)
+        for by in range(1, n.chips):
+            acc = acc + plane_in[by - 1].astype(F32)
+        total[...] = acc.astype(BF16)
+        for by in range(1, n.ctx):
+            start = pl.multiple_of(ahead(by) * shard, shard)
+            send(
+                total.at[pl.ds(start, shard), :],
+                land.at[c],
+                line_sem.at[0, by],
+                line_sem.at[1, by],
+                None,
+                ahead(by),
+            )
+        land[c] = total[pl.ds(pl.multiple_of(c * shard, shard), shard), :]
+
+    def grads_out(land, line_sem, outs, cols):
+        for by in range(1, n.ctx):
+            arrived(land.at[behind(by)], line_sem.at[1, by])
+        at = 0
+        for out, width in zip(outs, cols):
+            for j in range(n.ctx):
+                out[:, j * width : (j + 1) * width] = land[j, :, at : at + width].astype(F32)
+            at += width
+
+    def save_lines(first, line):
+        for j in range(n.lines):
+            r.g1_acc[3, first + j : first + j + 1, :] = line[:, j * HEAD_DIM : (j + 1) * HEAD_DIM]
+
+    def small_start(src, incoming, sem):
+        send(src, incoming.at[0], sem.at[0, 0], sem.at[1, 0], sibling)
+
+    def small_plane(src, incoming, acc, sem):
+        arrived(incoming.at[0], sem.at[1, 0])
+        acc[0] = src[...] + incoming[0]
+        for by in range(1, n.chips):
+            send(
+                acc.at[0],
+                incoming.at[by],
+                sem.at[0, by],
+                sem.at[1, by],
+                chip_ahead(by) * 2 + core,
+            )
+
+    def small_line(incoming, acc, sem):
+        total = acc[0]
+        for by in range(1, n.chips):
+            arrived(incoming.at[by], sem.at[1, by])
+            total = total + incoming[by]
+        acc[1] = total
+        for by in range(1, n.ctx):
+            slot = n.chips + by
+            send(acc.at[1], incoming.at[slot], sem.at[0, slot], sem.at[1, slot], None, ahead(by))
+
+    def small_end(incoming, acc, sem):
+        total = acc[1]
+        for by in range(1, n.ctx):
+            slot = n.chips + by
+            arrived(incoming.at[slot], sem.at[1, slot])
+            total = total + incoming[slot]
+        return total
+
+    attn_shards, mlp_shards = (r.wq, r.wk, r.wv, r.wo), (r.wg, r.wu, r.wd)
+    attn_cols, mlp_cols = n.cols[:4], n.cols[4:]
+    q_cols, k_cols, _, o_cols = attn_cols
+    ff = mlp_cols[0]
+    group = n.heads // n.kv
+    factor = 1.0 / math.sqrt(HEAD_DIM)
+
+    small_start(r.gains, r.g0_in, r.sem_g0)
+    weights_send(attn_shards, attn_cols, r.wa, r.sem_wa)
+    gather_start(r.hidden, r.xb, r.sem_xb)
+    own_x = pltpu.make_async_copy(r.hidden, r.xb.at[c], r.local_sem.at[7])
+    own_x.start()
+    own_g = pltpu.make_async_copy(r.cot, r.gb.at[c], r.local_sem.at[8])
+    own_g.start()
+    own_attn = weights_own(attn_shards, attn_cols, r.wa, 0)
+    own_mlp = weights_own(mlp_shards, mlp_cols, r.wm, 4)
+    small_plane(r.gains, r.g0_in, r.g0_acc, r.sem_g0)
+    small_line(r.g0_in, r.g0_acc, r.sem_g0)
+    gains = small_end(r.g0_in, r.g0_acc, r.sem_g0)
+    r.g0_acc[2] = gains
+    for j in range(n.lines):
+        r.gv[0, :, j * HEAD_DIM : (j + 1) * HEAD_DIM] = r.g0_acc[2, j : j + 1, :]
+        r.gv[1, :, j * HEAD_DIM : (j + 1) * HEAD_DIM] = r.g0_acc[
+            2, n.lines + j : n.lines + j + 1, :
+        ]
+    qgain = r.g0_acc[2, 2 * n.lines : 2 * n.lines + 1, :]
+    kgain = r.g0_acc[2, 2 * n.lines + 1 : 2 * n.lines + 2, :]
+    attn_gain, mlp_gain = r.gv[0], r.gv[1]
+
+    weights_spread(own_attn, attn_cols, r.wa, r.sem_wa, r.sem_pwa, r.sem_swa)
+    gather_relay(r.xb, r.sem_xb)
+    weights_send(mlp_shards, mlp_cols, r.wm, r.sem_wm)
+    for by in range(1, n.ctx):
+        send(r.cot, r.gb.at[c], r.sem_g.at[0, by], r.sem_g.at[1, by], None, ahead(by))
+    own_x.wait()
+    own_g.wait()
+
+    def norm_rows(j, carry):
+        x = r.xb[j].astype(F32)
+        start = pl.multiple_of(j * rows, rows)
+        r.xn[pl.ds(start, rows), :] = (x * rms(x) * attn_gain).astype(BF16)
+        return carry
+
+    lax.fori_loop(0, n.ctx, norm_rows, 0)
+    weights_forward(r.wa, r.sem_pwa, r.sem_swa)
+    weights_wait(r.wa, r.sem_swa)
+
+    cosine, sine = r.cos, r.sin
+    tile = 2 * HEAD_DIM if n.kv % 2 == 0 else HEAD_DIM
+    for at in range(0, q_cols + 2 * k_cols, tile):
+        product = mm(r.xn[...], r.wa[:, at : at + tile])
+        for part in range(tile // HEAD_DIM):
+            head = at // HEAD_DIM + part
+            u = product[:, part * HEAD_DIM : (part + 1) * HEAD_DIM]
+            if head < n.heads:
+                r.qp[head] = u
+                r.qr[head] = rope_fwd(u * rms(u) * qgain, cosine[...], sine[...]).astype(BF16)
+            elif head < n.heads + n.kv:
+                r.kp[head - n.heads] = u
+                r.kr[head - n.heads] = rope_fwd(u * rms(u) * kgain, cosine[...], sine[...]).astype(
+                    BF16
+                )
+            else:
+                r.vv[head - n.heads - n.kv] = u.astype(BF16)
+    half = n.tokens // 2
+
+    def head_forward(h, carry):
+        kv = h // group
+        for q0 in (0, half):
+            s = mm(r.qr[h, q0 : q0 + half, :], r.kr[kv], LAST_AXIS)
+            allowed = r.posk[...] <= r.posq[q0 : q0 + half, :]
+            e = jnp.where(allowed, jnp.exp(s * factor), 0.0)
+            r.es[h, q0 : q0 + half, :] = e
+            total = jnp.sum(e, axis=-1, keepdims=True)
+            a = mm(e.astype(BF16), r.vv[kv]) / total
+            r.af[h, q0 : q0 + half, :] = a
+            lane = pl.multiple_of(h * HEAD_DIM, HEAD_DIM)
+            r.at[q0 : q0 + half, pl.ds(lane, HEAD_DIM)] = a.astype(BF16)
+        return carry
+
+    lax.fori_loop(0, n.heads, head_forward, 0)
+    o_at = q_cols + 2 * k_cols
+
+    def by_rows(left, right, out):
+        def step(j, carry):
+            start = pl.multiple_of(j * rows, rows)
+            out[j] = mm(left[pl.ds(start, rows), :], right(), LAST_AXIS).astype(BF16)
+            return carry
+
+        lax.fori_loop(0, n.ctx, step, 0)
+
+    by_rows(r.at, lambda: r.wa[:, o_at:], r.p_o)
+    scatter(r.p_o, r.l_o, r.r_o, r.sem_o)
+    weights_spread(own_mlp, mlp_cols, r.wm, r.sem_wm, r.sem_pwm, r.sem_swm)
+    r.ho[...] = r.xb[c].astype(F32)
+    scatter_total(r.p_o, r.l_o, r.r_o, r.sem_o, r.ho)
+    h_own = r.ho[...]
+    r.mb[c] = (h_own * rms(h_own) * mlp_gain).astype(BF16)
+    gather_start(r.mb.at[c], r.mb, r.sem_mb)
+    gather_relay(r.mb, r.sem_mb)
+    weights_forward(r.wm, r.sem_pwm, r.sem_swm)
+    for by in range(1, n.ctx):
+        arrived(r.gb.at[behind(by)], r.sem_g.at[1, by])
+    weights_wait(r.wm, r.sem_swm)
+
+    mixed = r.mb[...].reshape(n.tokens, d)
+    upstream = r.gb[...].reshape(n.tokens, d)
+    tile = 2 * HEAD_DIM if ff % (2 * HEAD_DIM) == 0 else HEAD_DIM
+    for at in range(0, ff, tile):
+        gate = mm(mixed, r.wm[:, at : at + tile])
+        up = mm(mixed, r.wm[:, ff + at : ff + at + tile])
+        back = mm(upstream, r.wm[:, 2 * ff + at : 2 * ff + at + tile])
+        sig = jax.nn.sigmoid(gate)
+        swish = gate * sig
+        r.hid[:, at : at + tile] = (swish * up).astype(BF16)
+        r.dgu[:, at : at + tile] = (back * up * sig * (1.0 + gate * (1.0 - sig))).astype(BF16)
+        r.dgu[:, ff + at : ff + at + tile] = (back * swish).astype(BF16)
+
+    by_rows(r.dgu, lambda: r.wm[:, : 2 * ff], r.p_x2)
+    scatter(r.p_x2, r.l_x2, r.r_x2, r.sem_x2)
+    by_rows(r.hid, lambda: r.wm[:, 2 * ff :], r.p_y)
+    r.dh[...] = jnp.zeros_like(r.dh)
+    scatter_total(r.p_x2, r.l_x2, r.r_x2, r.sem_x2, r.dh)
+    h_own = r.ho[...]
+    from_norm, term = norm_back(h_own, rms(h_own), mlp_gain, r.dh[...])
+    r.g1_acc[3] = jnp.zeros_like(r.g1_acc[3])
+    save_lines(n.lines, jnp.sum(term, axis=0, keepdims=True))
+    r.dh[...] = r.gb[c].astype(F32) + from_norm
+    r.rb[c] = r.dh[...].astype(BF16)
+    gather_start(r.rb.at[c], r.rb, r.sem_rb)
+    gather_relay(r.rb, r.sem_rb)
+    for by in range(1, n.ctx):
+        send(
+            r.p_y.at[ahead(by)], r.i_y.at[by - 1], r.sem_y.at[0, by], r.sem_y.at[1, by], None, ahead(by)
+        )
+    for at in range(0, 2 * ff, tile):
+        r.gm[:, at : at + tile] = mm(mixed, r.dgu[:, at : at + tile], FIRST_AXIS).astype(BF16)
+    for at in range(0, ff, tile):
+        r.gm[:, 2 * ff + at : 2 * ff + at + tile] = mm(
+            upstream, r.hid[:, at : at + tile], FIRST_AXIS
+        ).astype(BF16)
+    grads_pair(r.gm, r.gm_sib, r.sem_sgm)
+
+    upstream = r.rb[...].reshape(n.tokens, d)
+    for at in range(0, o_cols, HEAD_DIM):
+        r.da[at // HEAD_DIM] = mm(upstream, r.wa[:, o_at + at : o_at + at + HEAD_DIM])
+    grads_plane(r.gm, r.gm_sib, r.sem_sgm, r.gm_in, r.sem_pgm)
+    r.dk[...] = jnp.zeros_like(r.dk)
+    r.dv[...] = jnp.zeros_like(r.dv)
+
+    def head_backward(h, carry):
+        kv = h // group
+        for q0 in (0, half):
+            span = slice(q0, q0 + half)
+            e = r.es[h, span, :]
+            total = jnp.sum(e, axis=-1, keepdims=True)
+            da = r.da[h, span, :]
+            w = (da / total).astype(BF16)
+            dl = jnp.sum(da * r.af[h, span, :], axis=-1, keepdims=True) / total
+            ds = (e * (mm(w, r.vv[kv], LAST_AXIS) - dl)).astype(BF16)
+            r.ds[span, :] = ds
+            r.eb[span, :] = e.astype(BF16)
+            r.wb[span, :] = w
+            r.da[h, span, :] = mm(ds, r.kr[kv])
+        r.dk[kv] = r.dk[kv] + mm(r.ds[...], r.qr[h], FIRST_AXIS)
+        r.dv[kv] = r.dv[kv] + mm(r.eb[...], r.wb[...], FIRST_AXIS)
+        return carry
+
+    lax.fori_loop(0, n.heads, head_backward, 0)
+
+    def query_backward(h, term):
+        u = r.qp[h]
+        du, gain_term = norm_back(
+            u, rms(u), qgain, rope_bwd(r.da[h] * factor, cosine[...], sine[...])
+        )
+        lane = pl.multiple_of(h * HEAD_DIM, HEAD_DIM)
+        r.dqkv[:, pl.ds(lane, HEAD_DIM)] = du.astype(BF16)
+        return term + jnp.sum(gain_term, axis=0, keepdims=True)
+
+    q_term = lax.fori_loop(0, n.heads, query_backward, jnp.zeros((1, HEAD_DIM), F32))
+    k_term = jnp.zeros((1, HEAD_DIM), F32)
+    for kv in range(n.kv):
+        u = r.kp[kv]
+        du, gain_term = norm_back(
+            u, rms(u), kgain, rope_bwd(r.dk[kv] * factor, cosine[...], sine[...])
+        )
+        at = q_cols + kv * HEAD_DIM
+        r.dqkv[:, at : at + HEAD_DIM] = du.astype(BF16)
+        at += k_cols
+        r.dqkv[:, at : at + HEAD_DIM] = r.dv[kv].astype(BF16)
+        k_term = k_term + jnp.sum(gain_term, axis=0, keepdims=True)
+    by_rows(r.dqkv, lambda: r.wa[:, :o_at], r.p_x1)
+    scatter(r.p_x1, r.l_x1, r.r_x1, r.sem_x1)
+    for at in range(0, o_at, 2 * HEAD_DIM):
+        r.ga[:, at : at + 2 * HEAD_DIM] = mm(
+            r.xn[...], r.dqkv[:, at : at + 2 * HEAD_DIM], FIRST_AXIS
+        ).astype(BF16)
+    r.ga[:, o_at:] = mm(upstream, r.at[...], FIRST_AXIS).astype(BF16)
+    grads_pair(r.ga, r.ga_sib, r.sem_sga)
+    grads_line(
+        r.gm, r.gm_sib, r.sem_sgm, r.gm_in, r.sem_pgm, r.gm_z, r.gm_land, r.sem_zgm
+    )
+    grads_plane(r.ga, r.ga_sib, r.sem_sga, r.ga_in, r.sem_pga)
+
+    r.out_input[...] = jnp.zeros_like(r.out_input)
+    scatter_total(r.p_x1, r.l_x1, r.r_x1, r.sem_x1, r.out_input)
+    x = r.xb[c].astype(F32)
+    from_norm, term = norm_back(x, rms(x), attn_gain, r.out_input[...])
+    save_lines(0, jnp.sum(term, axis=0, keepdims=True))
+    r.out_input[...] = r.dh[...] + from_norm
+    r.g1_acc[3, 2 * n.lines : 2 * n.lines + 1, :] = q_term
+    r.g1_acc[3, 2 * n.lines + 1 : 2 * n.lines + 2, :] = k_term
+    small_start(r.g1_acc.at[3], r.g1_in, r.sem_g1)
+    small_plane(r.g1_acc.at[3], r.g1_in, r.g1_acc, r.sem_g1)
+    out = r.ho[...] + r.p_y[c].astype(F32)
+    for by in range(1, n.ctx):
+        arrived(r.i_y.at[by - 1], r.sem_y.at[1, by])
+        out = out + r.i_y[by - 1].astype(F32)
+    r.out_hidden[...] = out.astype(BF16)
+    small_line(r.g1_in, r.g1_acc, r.sem_g1)
+    grads_line(
+        r.ga, r.ga_sib, r.sem_sga, r.ga_in, r.sem_pga, r.ga_z, r.ga_land, r.sem_zga
+    )
+    grads_out(r.gm_land, r.sem_zgm, (r.og, r.ou, r.od), mlp_cols)
+    r.out_gains[...] = small_end(r.g1_in, r.g1_acc, r.sem_g1)
+    grads_out(r.ga_land, r.sem_zga, (r.oq, r.ok, r.ov, r.oo), attn_cols)
+    for wait in sends:
+        wait()
+
+
+def fused(
+    ctx,
+    fsdp,
+    hidden_in,
+    block_order,
+    cotangent,
+    q_weight,
+    k_weight,
+    v_weight,
+    o_weight,
+    attn_gain,
+    query_gain,
+    key_gain,
+    mlp_gain,
+    gate_weight,
+    up_weight,
+    down_weight,
+):
+    shards = (q_weight, k_weight, v_weight, o_weight, gate_weight, up_weight, down_weight)
+    n = Sizes(ctx, fsdp, hidden_in.shape[1], shards)
+    me = lax.axis_index("fsdp") * ctx + lax.axis_index("ctx")
+    count = ctx * fsdp
+    slots = block_order.shape[1]
+    block_len = n.tokens // slots
+    positions = (
+        block_order[0][:, None] * block_len + jnp.arange(block_len, dtype=jnp.int32)[None, :]
+    ).reshape(-1)
+    cosine, sine = rope_tables(positions, HEAD_DIM)
+    sign = jnp.where(jnp.arange(HEAD_DIM) < HEAD_DIM // 2, -1.0, 1.0)
+    sine = sine * sign
+
+    def placed(gain):
+        own = jnp.arange(count, dtype=jnp.int32)[:, None] == me
+        whole = jnp.where(own, gain.astype(F32)[None, :], 0.0)
+        return whole.reshape(-1, HEAD_DIM)
+
+    gains = jnp.concatenate([placed(g) for g in (attn_gain, mlp_gain, query_gain, key_gain)])
+    gains = jnp.pad(gains, ((0, n.gain_rows - gains.shape[0]), (0, 0)))
+    hbm, vmem = pl.BlockSpec(memory_space=pl.ANY), pl.BlockSpec(memory_space=pltpu.VMEM)
+    inputs = dict(
+        hidden=(hidden_in[0], hbm),
+        cot=(cotangent[0], hbm),
+        wq=(q_weight, hbm),
+        wk=(k_weight, hbm),
+        wv=(v_weight, hbm),
+        wo=(o_weight, hbm),
+        wg=(gate_weight, hbm),
+        wu=(up_weight, hbm),
+        wd=(down_weight, hbm),
+        gains=(gains, vmem),
+        cos=(cosine, vmem),
+        sin=(sine, vmem),
+        posq=(positions[:, None], vmem),
+        posk=(positions[None, :], vmem),
+    )
+    outputs = dict(
+        out_hidden=jax.ShapeDtypeStruct((n.rows, n.width), BF16),
+        out_input=jax.ShapeDtypeStruct((n.rows, n.width), F32),
+        oq=jax.ShapeDtypeStruct(q_weight.shape, F32),
+        ok=jax.ShapeDtypeStruct(k_weight.shape, F32),
+        ov=jax.ShapeDtypeStruct(v_weight.shape, F32),
+        oo=jax.ShapeDtypeStruct(o_weight.shape, F32),
+        og=jax.ShapeDtypeStruct(gate_weight.shape, F32),
+        ou=jax.ShapeDtypeStruct(up_weight.shape, F32),
+        od=jax.ShapeDtypeStruct(down_weight.shape, F32),
+        out_gains=jax.ShapeDtypeStruct((n.gain_rows, HEAD_DIM), F32),
+    )
+    scratch = scratch_of(n)
+    result, input_grad, oq, ok, ov, oo, og, ou, od, sums = pl.pallas_call(
+        functools.partial(layer_kernel, n, [*inputs, *outputs, *scratch]),
+        out_shape=tuple(outputs.values()),
+        in_specs=[spec for _, spec in inputs.values()],
+        out_specs=tuple(vmem for _ in outputs),
+        scratch_shapes=list(scratch.values()),
+        compiler_params=pltpu.CompilerParams(
+            collective_id=0, has_side_effects=True, vmem_limit_bytes=VMEM_LIMIT
+        ),
+        name="layer",
+    )(*[value for value, _ in inputs.values()])
+
+    def own(first, size):
+        flat = sums[first : first + size // HEAD_DIM].reshape(-1)
+        return lax.dynamic_slice_in_dim(flat, me * (size // count), size // count)
+
+    lines = n.lines
+    return (
+        result[None],
+        input_grad[None],
+        oq,
+        ok,
+        ov,
+        oo,
+        own(0, n.width),
+        own(2 * lines, HEAD_DIM),
+        own(2 * lines + 1, HEAD_DIM),
+        own(lines, n.width),
+        og,
+        ou,
+        od,
+    )
+
+
+def fits(ctx, fsdp, shard_rows):
+    return shard_rows % 16 == 0 and fsdp % 2 == 0 and KV_HEADS % ctx == 0
+
+
 def solution(mesh):
     ctx, fsdp = mesh.shape["ctx"], mesh.shape["fsdp"]
     tokens = P("fsdp", "ctx", None)
     matrix = P(("fsdp", "ctx"), None)
     vector = P(("fsdp", "ctx"))
+    def step(hidden_in, block_order, cotangent, q_weight, *rest):
+        whole = fused if fits(ctx, fsdp, q_weight.shape[0]) else local
+        return whole(ctx, fsdp, hidden_in, block_order, cotangent, q_weight, *rest)
+
     return jax.shard_map(
-        functools.partial(local, ctx, fsdp),
+        step,
         mesh=mesh,
         in_specs=(tokens, P("fsdp", None), tokens)
         + (matrix,) * 4

time: 549 us -> 264 us (0.48)
  waiting for transfers between devices: 267 us -> 0 us
  Pallas kernels: 0 us -> 243 us
  blocking collectives: 143 us -> 0 us
  matrix products: 50.2 us -> 0 us
  other arithmetic: 25.1 us -> 2.77 us
  local copies, waits for them, and re-layouts: 36.7 us -> 16.6 us
  between operations: 15 us -> 0.74 us
  starting transfers between devices: 10.1 us -> 0 us
    pallas_call x0 -> x1, Pallas kernels: none -> 243 us  [fused(): pl.pallas_call(functools.partial(layer_kernel, n, [*inputs, *outputs, *sc...]
    all_gather x6 -> x0, waiting for transfers between devices: 136 us -> none  [the longest x2 68.8 us: gather_columns(): whole = lax.all_gather(both, 'fsdp', axis=0, tiled=True)]
    reduce_scatter x6 -> x0, waiting for transfers between devices: 130 us -> none  [the longest x2 69.4 us: scatter_grads(): both = lax.psum_scatter(both, 'fsdp', scatter_dimension=0, tiled=True)]
    unnamed x2 -> x0, blocking collectives: 83.3 us -> none
    all_to_all x2 -> x0, blocking collectives: 60.1 us -> none  [gather_columns(): both = lax.all_to_all(both, 'ctx', 0, 0, tiled=True)]
    dot_general x27 -> x0, matrix products: 50.2 us -> none  [the longest x21 40.6 us: mm(): return lax.dot_general(left, right, dims, preferred_element_type=F32)]
    unnamed x114 -> x35, local copies, waits for them, and re-layouts: 27.2 us -> 11.3 us
    all_to_all x2 -> x0, starting transfers between devices: 9.18 us -> none  [scatter_grads(): both = lax.all_to_all(both.reshape(ctx, rows, -1), 'ctx', 0, 0, tiled=True)]
  transfers between devices with their start and end apart: 14 -> 0, of which waited for: 11 -> 0; matrix products, arithmetic and copies ran while one was open for 12% -> 0% of each run, Pallas kernels for 0% -> 0%
where the time goes in v2:
time: 264 us; the launch traced here: 263 us
  Pallas kernels  243 us (92%)
  local copies, waits for them, and re-layouts  16.6 us (6%)
  other arithmetic  2.77 us (1%)
    pallas_call x1, Pallas kernels, fused(): pl.pallas_call(functools.partial(layer_kernel, n, [*inputs, *outputs, *sc...  243 us
    unnamed x35, local copies, waits for them, and re-layouts  11.3 us

profile of v2, /device:TPU:0, one launch (start us, length us, event | category | flops | bytes accessed | tf_op | source)
XLA Modules:
  0.0 263.0 jit_solution(2809370461070629988)
XLA Ops:
  0.7 0.6 copy-done.10
  1.3 0.7 copy-done.11
  2.0 0.1 select_n.55
  2.1 0.1 select_n.57
  2.3 0.1 broadcast_in_dim.95
  2.4 0.6 copy-done.8
  3.1 0.6 copy-done.9
  3.7 0.1 broadcast_in_dim.97
  3.8 0.6 select_maximum_fusion.refs_9_
  4.6 0.1 broadcast_multiply_fusion
  4.7 1.8 sine_multiply_fusion
  6.6 0.9 add.60.refs_12_
  7.5 0.7 add.57.refs_13_
  8.1 242.8 %layer.1 = (bf16[128,1024]{1,0:T(8,128)(2,1)}, f32[128,1024]{1,0:T(8,128)}, f32[32,2048]{1,0:T(8,128)}, f32[32,1024]{1,0:T(8,128)}, f32[32,1024]{1,0:T(8,128)}, ...) custom-call(bf16[128,1024]{1,0:T(8,128)(2,1)} %bitcast.16, ...), custom_call_target="tpu_custom_call" | custom-call | tf_op jit(solution)/shard_map/layer/pallas_call | solution.py:927
  251.0 0.8 fusion.2
  251.8 0.6 dynamic-slice_bitcast_fusion
  252.3 0.7 slice_bitcast_fusion
  253.0 0.6 dynamic_slice.16
  253.6 0.6 dynamic_slice.21
  254.2 1.7 copy.37
  255.9 0.8 copy.38
  256.7 0.3 copy-done.5
  257.0 0.7 copy.39
  257.7 0.3 copy-done.7
  258.0 0.7 copy.40
  258.6 0.7 copy.41
  259.3 0.7 copy.42
  260.0 0.7 copy.43
  260.7 0.4 copy-done.2
  261.1 0.7 copy.44
  261.9 0.4 copy-done.1
  262.3 0.7 copy.45
  (33 shorter events, 0.5 us)
Async XLA Ops:
  0.6 0.7 copy-start.10
  1.3 0.7 copy-start.11
  2.3 0.7 copy-start.8
  3.0 0.7 copy-start.9
  3.8 0.7 copy-start.12
  251.0 4.9 %copy-start = (f32[128,1024]{1,0:T(8,128)S(1)}, f32[128,1024]{1,0:T(8,128)}, u32[]{:S(2)}) copy-start(f32[128,1024]{1,0:T(8,128)} %get-tuple-element.24) | copy-start | bytes 1572868
  255.9 1.1 copy-start.5
  257.0 1.0 copy-start.7
  257.0 1.7 copy-start.6
  257.9 1.3 copy-start.4
  258.6 1.4 copy-start.3
  260.0 1.1 copy-start.2
  261.1 1.1 copy-start.1

commit v3 on v2

--- a/solution.py
+++ b/solution.py
@@ -18,6 +18,7 @@
 BF16 = jnp.bfloat16
 F32 = jnp.float32
 VMEM_LIMIT = 67043328
+PARTS = 2
 
 
 def mm(left, right, dims=(((1,), (0,)), ((), ()))):
@@ -264,6 +265,7 @@
         self.mlp_cols = sum(self.cols[4:])
         self.lines = self.width // HEAD_DIM
         self.gain_rows = 8 * ((2 * self.lines + 2 + 7) // 8)
+        self.each, self.few = self.width // (ctx * fsdp), HEAD_DIM // (ctx * fsdp)
 
 
 def scratch_of(n):
@@ -294,11 +296,16 @@
         eb=bf(s, s),
         wb=bf(s, HEAD_DIM),
         dqkv=bf(s, (h + 2 * kv) * HEAD_DIM),
-        hid=bf(s, ff),
-        dgu=bf(s, 2 * ff),
+        hid=bf(c, n.rows, ff),
+        dgu=bf(c, n.rows, 2 * ff),
         ho=f32(n.rows, d),
         dh=f32(n.rows, d),
         gv=f32(2, 1, d),
+        gp=f32(n.gain_rows, HEAD_DIM),
+        cos=f32(s, HEAD_DIM),
+        sin=f32(s, HEAD_DIM),
+        posq=pltpu.VMEM((s, HEAD_DIM), jnp.int32),
+        posk=pltpu.VMEM((1, s), jnp.int32),
         ga=bf(d, n.attn_cols),
         gm=bf(d, n.mlp_cols),
         ga_sib=bf(n.chips, n.block, n.attn_cols),
@@ -307,29 +314,21 @@
         gm_in=bf(n.chips - 1, n.block, n.mlp_cols),
         ga_z=bf(n.block, n.attn_cols),
         gm_z=bf(n.block, n.mlp_cols),
-        ga_land=bf(c, n.shard, n.attn_cols),
-        gm_land=bf(c, n.shard, n.mlp_cols),
         local_sem=sem(9),
     )
-    for name in ("o", "x2", "x1"):
+    for name in ("o", "y", "x2", "x1"):
         out["p_" + name] = bf(c, n.rows, d)
         out["l_" + name] = bf(c, n.rows, d)
         out["r_" + name] = bf(c, n.rows, d)
-        out["sem_" + name] = sem(4, c)
-    out["p_y"] = bf(c, n.rows, d)
-    out["i_y"] = bf(c - 1, n.rows, d)
-    out["sem_y"] = sem(2, c)
-    out["sem_g"] = sem(2, c)
-    for name in ("xb", "mb", "rb"):
-        out["sem_" + name] = sem(3, c)
+        out["sem_" + name] = sem(4, c, PARTS)
+    for name in ("xb", "gb", "mb", "rb"):
+        out["sem_" + name] = sem(3, c, PARTS)
     out["sem_wa"] = sem(2, c - 1, 4)
     out["sem_wm"] = sem(2, c - 1, 3)
-    for name in ("wa", "wm"):
-        out["sem_p" + name] = sem(2, n.chips)
-        out["sem_s" + name] = sem(2, n.chips)
-    for name in ("ga", "gm"):
-        out["sem_s" + name] = sem(2, n.chips)
-        out["sem_p" + name] = sem(2, n.chips)
+    for name in ("pq", "po", "pm"):
+        out["sem_" + name] = sem(4, n.chips)
+    for name in ("gm", "go", "gq"):
+        out["sem_" + name] = sem(4, n.chips)
         out["sem_z" + name] = sem(2, c)
     for name in ("g0", "g1"):
         out[name + "_in"] = f32(n.chips + c, n.gain_rows, HEAD_DIM)
@@ -399,96 +398,95 @@
     pl.semaphore_wait(barrier, n.ctx - 1 + n.chips)
 
     right, left = jnp.minimum(c + 1, n.ctx - 1), jnp.maximum(c - 1, 0)
-
-    def gather_start(src, buf, sem):
-        send_if(c + 1 < n.ctx, src, buf.at[c], sem.at[0, 0], sem.at[2, c], right)
-        send_if(c > 0, src, buf.at[c], sem.at[1, 0], sem.at[2, c], left)
-
-    def gather_relay(buf, sem):
-        for by in range(1, n.ctx):
-            low = jnp.maximum(c - by, 0)
-            pl.when(c - by >= 0)(lambda: arrived(buf.at[low], sem.at[2, low]))
-            send_if(
-                (c - by >= 0) & (c + 1 < n.ctx),
-                buf.at[low],
-                buf.at[low],
-                sem.at[0, by],
-                sem.at[2, low],
-                right,
-            )
-            high = jnp.minimum(c + by, n.ctx - 1)
-            pl.when(c + by < n.ctx)(lambda: arrived(buf.at[high], sem.at[2, high]))
-            send_if(
-                (c + by < n.ctx) & (c > 0),
-                buf.at[high],
-                buf.at[high],
-                sem.at[1, by],
-                sem.at[2, high],
-                left,
-            )
-
-    def scatter(part, from_left, from_right, sem, fill=None):
+    part_rows = rows // PARTS
+
+    def part_of(buf, j, k):
+        return buf.at[j, pl.ds(k * part_rows, part_rows), :]
+
+    def gather_start(src, buf, sem, k, to=None):
+        piece = src.at[pl.ds(k * part_rows, part_rows), :]
+        here = part_of(buf, c, k)
+        up, down = c + 1 < n.ctx, c > 0
+        if to == "between":
+            up, down = c + 1 < n.ctx - 1, c > 1
+        elif to == "ends":
+            up, down = c + 1 == n.ctx - 1, c == 1
+        send_if(up, piece, here, sem.at[0, 0, k], sem.at[2, c, k], right)
+        send_if(down, piece, here, sem.at[1, 0, k], sem.at[2, c, k], left)
+
+    def gather_relay(buf, sem, by, k):
+        low, high = jnp.maximum(c - by, 0), jnp.minimum(c + by, n.ctx - 1)
+        piece, here = part_of(buf, low, k), sem.at[2, low, k]
+        pl.when(c - by >= 0)(functools.partial(arrived, piece, here))
+        cond = (c - by >= 0) & (c + 1 < n.ctx)
+        send_if(cond, piece, piece, sem.at[0, by, k], here, right)
+        piece, here = part_of(buf, high, k), sem.at[2, high, k]
+        pl.when(c + by < n.ctx)(functools.partial(arrived, piece, here))
+        cond = (c + by < n.ctx) & (c > 0)
+        send_if(cond, piece, piece, sem.at[1, by, k], here, left)
+
+    def rows_of(k):
+        return slice(k * part_rows, (k + 1) * part_rows)
+
+    def scatter_send(cond, part, there, sem, target, k, way, to_c):
+        send_if(
+            cond,
+            part_of(part, target, k),
+            part_of(there, target, k),
+            sem.at[way, target, k],
+            sem.at[2 + way, target, k],
+            to_c,
+        )
+
+    def scatter_add(part, there, sem, target, k, way):
+        arrived(part_of(there, target, k), sem.at[2 + way, target, k])
+        span = rows_of(k)
+        part[target, span, :] = (
+            part[target, span, :].astype(F32) + there[target, span, :].astype(F32)
+        ).astype(BF16)
+
+    def scatter_start(g, k):
         for step in range(n.ctx - 1):
-            target = step
-            down = c > target
-
-            @pl.when(down & (c + 1 < n.ctx))
-            def _():
-                arrived(from_right.at[target], sem.at[3, target])
-                part[target] = (part[target].astype(F32) + from_right[target].astype(F32)).astype(
-                    BF16
-                )
-
-            send_if(
-                down,
-                part.at[target],
-                from_right.at[target],
-                sem.at[1, target],
-                sem.at[3, target],
-                left,
-            )
-            target = n.ctx - 1 - step
-            up = c < target
-
-            @pl.when(up & (c > 0))
-            def _():
-                arrived(from_left.at[target], sem.at[2, target])
-                part[target] = (part[target].astype(F32) + from_left[target].astype(F32)).astype(
-                    BF16
-                )
-
-            send_if(
-                up, part.at[target], from_left.at[target], sem.at[0, target], sem.at[2, target], right
-            )
-            if fill:
-                fill(step)
-
-    def scatter_total(part, from_left, from_right, sem, out):
-        out[...] = out[...] + part[c].astype(F32)
+            scatter_send(c == n.ctx - 1, g.part, g.high, g.sem, step, k, 1, left)
+            scatter_send(c == 0, g.part, g.low, g.sem, n.ctx - 1 - step, k, 0, right)
+
+    def scatter_relay(g, step, k):
+        target = step
+        down = (c > target) & (c + 1 < n.ctx)
+        pl.when(down)(functools.partial(scatter_add, g.part, g.high, g.sem, target, k, 1))
+        scatter_send(down, g.part, g.high, g.sem, target, k, 1, left)
+        target = n.ctx - 1 - step
+        up = (c < target) & (c > 0)
+        pl.when(up)(functools.partial(scatter_add, g.part, g.low, g.sem, target, k, 0))
+        scatter_send(up, g.part, g.low, g.sem, target, k, 0, right)
+
+    def scatter_total(g, out, k):
+        span = rows_of(k)
+        out[span, :] = out[span, :] + g.part[c, span, :].astype(F32)
 
         @pl.when(c > 0)
         def _():
-            arrived(from_left.at[c], sem.at[2, c])
-            out[...] = out[...] + from_left[c].astype(F32)
+            arrived(part_of(g.low, c, k), g.sem.at[2, c, k])
+            out[span, :] = out[span, :] + g.low[c, span, :].astype(F32)
 
         @pl.when(c + 1 < n.ctx)
         def _():
-            arrived(from_right.at[c], sem.at[3, c])
-            out[...] = out[...] + from_right[c].astype(F32)
-
-    def block_of(buf, index):
-        return buf.at[pl.ds(pl.multiple_of(index * block, block), block), :]
+            arrived(part_of(g.high, c, k), g.sem.at[3, c, k])
+            out[span, :] = out[span, :] + g.high[c, span, :].astype(F32)
+
+    def block_of(buf, index, span):
+        return buf.at[pl.ds(pl.multiple_of(index * block, block), block), pl.ds(*span)]
 
     def piece_of(buf, line, at, width):
         start = pl.multiple_of(f * block + line * shard, shard)
         return buf.at[pl.ds(start, shard), pl.ds(at, width)]
 
-    def weights_send(shards, cols, buf, sem):
+    def weights_send(shards, cols, buf, sem, now=None):
         for by in range(1, n.ctx):
             at = 0
             for i, (src, width) in enumerate(zip(shards, cols)):
                 column = pl.multiple_of(ahead(by) * width, HEAD_DIM)
-                send(
+                copy = remote(
                     src.at[:, pl.ds(column, width)],
                     piece_of(buf, c, at, width),
                     sem.at[0, by - 1, i],
@@ -496,6 +494,13 @@
                     None,
                     ahead(by),
                 )
+                at_end = (ahead(by) == 0) | (ahead(by) == n.ctx - 1)
+                if now is None:
+                    copy.start()
+                else:
+                    pl.when(at_end if now == "ends" else ~at_end)(copy.start)
+                if now != "ends":
+                    sends.append(copy.wait_send)
                 at += width
 
     def weights_own(shards, cols, buf, first):
@@ -512,119 +517,104 @@
             at += width
         return out
 
-    def weights_spread(own, cols, buf, sem, plane_sem, sib_sem):
+    def weights_spread(own, cols, sem, g):
         for copy in own:
             copy.wait()
         for by in range(1, n.ctx):
-            at = 0
+            at = g.span[0]
             for i, width in enumerate(cols):
-                arrived(piece_of(buf, behind(by), at, width), sem.at[1, by - 1, i])
+                arrived(piece_of(g.buf, behind(by), at, width), sem.at[1, by - 1, g.first + i])
                 at += width
-        mine = block_of(buf, f)
+        mine = block_of(g.buf, f, g.span)
         for by in range(1, n.chips):
+            send(mine, mine, g.sem.at[0, by], g.sem.at[1, by], chip_ahead(by) * 2 + core)
+        send(mine, mine, g.sem.at[2, 0], g.sem.at[3, 0], sibling)
+
+    def weights_forward(g):
+        for by in range(1, n.chips):
+            piece = block_of(g.buf, chip_behind(by) * 2 + core, g.span)
+            arrived(piece, g.sem.at[1, by])
+            send(piece, piece, g.sem.at[2, by], g.sem.at[3, by], sibling)
+
+    def weights_wait(g):
+        for by in range(n.chips):
+            arrived(block_of(g.buf, chip_behind(by) * 2 + 1 - core, g.span), g.sem.at[3, by])
+
+    def share_of(buf, index, span):
+        return buf.at[pl.ds(pl.multiple_of(index * block, block), block), pl.ds(*span)]
+
+    def grads_pair(g):
+        for by in (*range(1, n.chips), 0):
             send(
-                mine, mine, plane_sem.at[0, by], plane_sem.at[1, by], chip_ahead(by) * 2 + core
-            )
-        send(mine, mine, sib_sem.at[0, 0], sib_sem.at[1, 0], sibling)
-
-    def weights_forward(buf, plane_sem, sib_sem):
-        for by in range(1, n.chips):
-            piece = block_of(buf, chip_behind(by) * 2 + core)
-            arrived(piece, plane_sem.at[1, by])
-            send(piece, piece, sib_sem.at[0, by], sib_sem.at[1, by], sibling)
-
-    def weights_wait(buf, sib_sem):
-        for by in range(n.chips):
-            arrived(block_of(buf, chip_behind(by) * 2 + 1 - core), sib_sem.at[1, by])
-
-    def grads_pair(buf, sib_in, sib_sem):
-        for by in range(n.chips):
-            send(
-                block_of(buf, chip_ahead(by) * 2 + 1 - core),
-                sib_in.at[by],
-                sib_sem.at[0, by],
-                sib_sem.at[1, by],
+                share_of(g.whole, chip_ahead(by) * 2 + 1 - core, g.span),
+                g.pair.at[by, :, pl.ds(*g.span)],
+                g.sem.at[0, by],
+                g.sem.at[1, by],
                 sibling,
             )
 
-    def grads_plane(buf, sib_in, sib_sem, plane_in, plane_sem):
+    def grads_plane(g):
         for by in range(1, n.chips):
-            arrived(sib_in.at[by], sib_sem.at[1, by])
-            piece = block_of(buf, chip_ahead(by) * 2 + core)
-            piece[...] = (piece[...].astype(F32) + sib_in[by].astype(F32)).astype(BF16)
+            theirs = g.pair.at[by, :, pl.ds(*g.span)]
+            arrived(theirs, g.sem.at[1, by])
+            piece = share_of(g.whole, chip_ahead(by) * 2 + core, g.span)
+            piece[...] = (piece[...].astype(F32) + theirs[...].astype(F32)).astype(BF16)
             send(
                 piece,
-                plane_in.at[by - 1],
-                plane_sem.at[0, by],
-                plane_sem.at[1, by],
+                g.plane.at[by - 1, :, pl.ds(*g.span)],
+                g.sem.at[2, by],
+                g.sem.at[3, by],
                 chip_ahead(by) * 2 + core,
             )
 
-    def grads_line(buf, sib_in, sib_sem, plane_in, plane_sem, total, land, line_sem):
-        arrived(sib_in.at[0], sib_sem.at[1, 0])
+    def grads_line(g):
+        theirs = g.pair.at[0, :, pl.ds(*g.span)]
+        arrived(theirs, g.sem.at[1, 0])
+        acc = share_of(g.whole, f, g.span)[...].astype(F32) + theirs[...].astype(F32)
         for by in range(1, n.chips):
-            arrived(plane_in.at[by - 1], plane_sem.at[1, by])
-        acc = block_of(buf, f)[...].astype(F32) + sib_in[0].astype(F32)
-        for by in range(1, n.chips):
-            acc = acc + plane_in[by - 1].astype(F32)
-        total[...] = acc.astype(BF16)
+            theirs = g.plane.at[by - 1, :, pl.ds(*g.span)]
+            arrived(theirs, g.sem.at[3, by])
+            acc = acc + theirs[...].astype(F32)
+        g.total[:, pl.ds(*g.span)] = acc.astype(BF16)
         for by in range(1, n.ctx):
             start = pl.multiple_of(ahead(by) * shard, shard)
             send(
-                total.at[pl.ds(start, shard), :],
-                land.at[c],
-                line_sem.at[0, by],
-                line_sem.at[1, by],
+                g.total.at[pl.ds(start, shard), pl.ds(*g.span)],
+                g.land.at[c, :, pl.ds(*g.span)],
+                g.line_sem.at[0, by],
+                g.line_sem.at[1, by],
                 None,
                 ahead(by),
             )
-        land[c] = total[pl.ds(pl.multiple_of(c * shard, shard), shard), :]
-
-    def grads_out(land, line_sem, outs, cols):
+        start = pl.multiple_of(c * shard, shard)
+        g.land[c, :, pl.ds(*g.span)] = g.total[pl.ds(start, shard), pl.ds(*g.span)]
+
+    def grads_wait(g):
         for by in range(1, n.ctx):
-            arrived(land.at[behind(by)], line_sem.at[1, by])
-        at = 0
-        for out, width in zip(outs, cols):
-            for j in range(n.ctx):
-                out[:, j * width : (j + 1) * width] = land[j, :, at : at + width].astype(F32)
-            at += width
-
-    def save_lines(first, line):
-        for j in range(n.lines):
-            r.g1_acc[3, first + j : first + j + 1, :] = line[:, j * HEAD_DIM : (j + 1) * HEAD_DIM]
-
-    def small_start(src, incoming, sem):
-        send(src, incoming.at[0], sem.at[0, 0], sem.at[1, 0], sibling)
-
-    def small_plane(src, incoming, acc, sem):
-        arrived(incoming.at[0], sem.at[1, 0])
-        acc[0] = src[...] + incoming[0]
-        for by in range(1, n.chips):
-            send(
-                acc.at[0],
-                incoming.at[by],
-                sem.at[0, by],
-                sem.at[1, by],
-                chip_ahead(by) * 2 + core,
-            )
-
-    def small_line(incoming, acc, sem):
-        total = acc[0]
-        for by in range(1, n.chips):
-            arrived(incoming.at[by], sem.at[1, by])
-            total = total + incoming[by]
-        acc[1] = total
-        for by in range(1, n.ctx):
-            slot = n.chips + by
-            send(acc.at[1], incoming.at[slot], sem.at[0, slot], sem.at[1, slot], None, ahead(by))
-
-    def small_end(incoming, acc, sem):
-        total = acc[1]
-        for by in range(1, n.ctx):
-            slot = n.chips + by
+            arrived(g.land.at[behind(by), :, pl.ds(*g.span)], g.line_sem.at[1, by])
+
+    def small_peers(way):
+        if way == "line":
+            return [(n.chips + by, f, ahead(by)) for by in range(1, n.ctx)]
+        if way == "plane":
+            return [(by, chip_ahead(by) * 2 + core, c) for by in range(1, n.chips)]
+        return [(0, sibling, c)]
+
+    def small_send(src, incoming, sem, way):
+        for slot, to_f, to_c in small_peers(way):
+            send(src, incoming.at[slot], sem.at[0, slot], sem.at[1, slot], to_f, to_c)
+
+    def small_sum(own, incoming, sem, way):
+        total = own[...]
+        for slot, _, _ in small_peers(way):
             arrived(incoming.at[slot], sem.at[1, slot])
             total = total + incoming[slot]
         return total
+
+    def save_lines(first, line):
+        for j in range(n.lines):
+            row = slice(first + j, first + j + 1)
+            r.g1_acc[3, row, :] += line[:, j * HEAD_DIM : (j + 1) * HEAD_DIM]
 
     attn_shards, mlp_shards = (r.wq, r.wk, r.wv, r.wo), (r.wg, r.wu, r.wd)
     attn_cols, mlp_cols = n.cols[:4], n.cols[4:]
@@ -633,19 +623,79 @@
     group = n.heads // n.kv
     factor = 1.0 / math.sqrt(HEAD_DIM)
 
-    small_start(r.gains, r.g0_in, r.sem_g0)
+    o_at = q_cols + 2 * k_cols
+    attn_bufs = dict(whole=r.ga, pair=r.ga_sib, plane=r.ga_in, total=r.ga_z, land=r.ga_land)
+    mlp_bufs = dict(whole=r.gm, pair=r.gm_sib, plane=r.gm_in, total=r.gm_z, land=r.gm_land)
+    plane_q = types.SimpleNamespace(buf=r.wa, span=(0, o_at), first=0, sem=r.sem_pq)
+    plane_o = types.SimpleNamespace(buf=r.wa, span=(o_at, o_cols), first=3, sem=r.sem_po)
+    plane_m = types.SimpleNamespace(buf=r.wm, span=(0, n.mlp_cols), first=0, sem=r.sem_pm)
+    group_m = types.SimpleNamespace(
+        **mlp_bufs, span=(0, n.mlp_cols), sem=r.sem_gm, line_sem=r.sem_zgm
+    )
+    group_o = types.SimpleNamespace(
+        **attn_bufs, span=(o_at, o_cols), sem=r.sem_go, line_sem=r.sem_zgo
+    )
+    group_q = types.SimpleNamespace(**attn_bufs, span=(0, o_at), sem=r.sem_gq, line_sem=r.sem_zgq)
+
+    sum_o, sum_y, sum_x2, sum_x1 = (
+        types.SimpleNamespace(part=part, low=low, high=high, sem=sem)
+        for part, low, high, sem in (
+            (r.p_o, r.l_o, r.r_o, r.sem_o),
+            (r.p_y, r.l_y, r.r_y, r.sem_y),
+            (r.p_x2, r.l_x2, r.r_x2, r.sem_x2),
+            (r.p_x1, r.l_x1, r.r_x1, r.sem_x1),
+        )
+    )
+    r.g1_acc[3] = jnp.zeros_like(r.g1_acc[3])
+
+    me = f * n.ctx + c
+    lane = lax.broadcasted_iota(jnp.int32, (1, HEAD_DIM), 1)
+
+    def place(row, at, size, first):
+        moved = pltpu.roll(r.gains[...], lax.rem(at + HEAD_DIM - first, HEAD_DIM), 1)
+        r.gp[pl.ds(row, 1), :] = jnp.where((lane >= at) & (lane < at + size), moved, 0.0)
+
+    r.gp[...] = jnp.zeros_like(r.gp)
+    row, at = me * n.each // HEAD_DIM, lax.rem(me * n.each, HEAD_DIM)
+    place(row, at, n.each, 0)
+    place(n.lines + row, at, n.each, n.each)
+    place(2 * n.lines, me * n.few, n.few, 2 * n.each)
+    place(2 * n.lines + 1, me * n.few, n.few, 2 * n.each + n.few)
+    small_send(r.gp, r.g0_in, r.sem_g0, "line")
     weights_send(attn_shards, attn_cols, r.wa, r.sem_wa)
-    gather_start(r.hidden, r.xb, r.sem_xb)
+    for k in range(PARTS):
+        gather_start(r.hidden, r.xb, r.sem_xb, k)
     own_x = pltpu.make_async_copy(r.hidden, r.xb.at[c], r.local_sem.at[7])
     own_x.start()
     own_g = pltpu.make_async_copy(r.cot, r.gb.at[c], r.local_sem.at[8])
     own_g.start()
     own_attn = weights_own(attn_shards, attn_cols, r.wa, 0)
     own_mlp = weights_own(mlp_shards, mlp_cols, r.wm, 4)
-    small_plane(r.gains, r.g0_in, r.g0_acc, r.sem_g0)
-    small_line(r.g0_in, r.g0_acc, r.sem_g0)
-    gains = small_end(r.g0_in, r.g0_acc, r.sem_g0)
-    r.g0_acc[2] = gains
+    r.g0_acc[0] = small_sum(r.gp, r.g0_in, r.sem_g0, "line")
+    small_send(r.g0_acc.at[0], r.g0_in, r.sem_g0, "pair")
+    slots = r.order.shape[1]
+    slot_len = n.tokens // slots
+    exponent = (lane % (HEAD_DIM // 2)).astype(F32) * (2.0 / HEAD_DIM)
+    inverse = jnp.exp(-exponent * math.log(1000000.0))
+    sign = jnp.where(lane < HEAD_DIM // 2, -1.0, 1.0)
+    for j in range(slots):
+        first = r.order[0, j] * slot_len
+        span = slice(j * slot_len, (j + 1) * slot_len)
+        position = first + lax.broadcasted_iota(jnp.int32, (slot_len, HEAD_DIM), 0)
+        r.posq[span, :] = position
+        angle = position.astype(F32) * inverse
+        r.cos[span, :] = jnp.cos(angle)
+        r.sin[span, :] = jnp.sin(angle) * sign
+    token = lax.broadcasted_iota(jnp.int32, (1, n.tokens), 1)
+    posk = token % slot_len
+    for j in range(slots):
+        posk = posk + jnp.where(token // slot_len == j, r.order[0, j] * slot_len, 0)
+    r.posk[...] = posk
+    r.g0_acc[1] = small_sum(r.g0_acc.at[0], r.g0_in, r.sem_g0, "pair")
+    small_send(r.g0_acc.at[1], r.g0_in, r.sem_g0, "plane")
+    weights_spread(own_attn[:3], attn_cols[:3], r.sem_wa, plane_q)
+    weights_spread(own_attn[3:], attn_cols[3:], r.sem_wa, plane_o)
+    r.g0_acc[2] = small_sum(r.g0_acc.at[1], r.g0_in, r.sem_g0, "plane")
     for j in range(n.lines):
         r.gv[0, :, j * HEAD_DIM : (j + 1) * HEAD_DIM] = r.g0_acc[2, j : j + 1, :]
         r.gv[1, :, j * HEAD_DIM : (j + 1) * HEAD_DIM] = r.g0_acc[
@@ -654,12 +704,13 @@
     qgain = r.g0_acc[2, 2 * n.lines : 2 * n.lines + 1, :]
     kgain = r.g0_acc[2, 2 * n.lines + 1 : 2 * n.lines + 2, :]
     attn_gain, mlp_gain = r.gv[0], r.gv[1]
-
-    weights_spread(own_attn, attn_cols, r.wa, r.sem_wa, r.sem_pwa, r.sem_swa)
-    gather_relay(r.xb, r.sem_xb)
-    weights_send(mlp_shards, mlp_cols, r.wm, r.sem_wm)
     for by in range(1, n.ctx):
-        send(r.cot, r.gb.at[c], r.sem_g.at[0, by], r.sem_g.at[1, by], None, ahead(by))
+        if by == n.ctx - 1:
+            weights_send(mlp_shards, mlp_cols, r.wm, r.sem_wm, "between")
+            for k in range(PARTS):
+                gather_start(r.cot, r.gb, r.sem_gb, k, "between")
+        for k in range(PARTS):
+            gather_relay(r.xb, r.sem_xb, by, k)
     own_x.wait()
     own_g.wait()
 
@@ -670,8 +721,11 @@
         return carry
 
     lax.fori_loop(0, n.ctx, norm_rows, 0)
-    weights_forward(r.wa, r.sem_pwa, r.sem_swa)
-    weights_wait(r.wa, r.sem_swa)
+    weights_forward(plane_q)
+    weights_wait(plane_q)
+    weights_send(mlp_shards, mlp_cols, r.wm, r.sem_wm, "ends")
+    for k in range(PARTS):
+        gather_start(r.cot, r.gb, r.sem_gb, k, "ends")
 
     cosine, sine = r.cos, r.sin
     tile = 2 * HEAD_DIM if n.kv % 2 == 0 else HEAD_DIM
@@ -696,7 +750,7 @@
         kv = h // group
         for q0 in (0, half):
             s = mm(r.qr[h, q0 : q0 + half, :], r.kr[kv], LAST_AXIS)
-            allowed = r.posk[...] <= r.posq[q0 : q0 + half, :]
+            allowed = r.posk[...] <= r.posq[q0 : q0 + half, 0:1]
             e = jnp.where(allowed, jnp.exp(s * factor), 0.0)
             r.es[h, q0 : q0 + half, :] = e
             total = jnp.sum(e, axis=-1, keepdims=True)
@@ -707,72 +761,131 @@
         return carry
 
     lax.fori_loop(0, n.heads, head_forward, 0)
-    o_at = q_cols + 2 * k_cols
+    weights_forward(plane_o)
+    weights_wait(plane_o)
 
     def by_rows(left, right, out):
-        def step(j, carry):
-            start = pl.multiple_of(j * rows, rows)
-            out[j] = mm(left[pl.ds(start, rows), :], right(), LAST_AXIS).astype(BF16)
-            return carry
-
-        lax.fori_loop(0, n.ctx, step, 0)
-
-    by_rows(r.at, lambda: r.wa[:, o_at:], r.p_o)
-    scatter(r.p_o, r.l_o, r.r_o, r.sem_o)
-    weights_spread(own_mlp, mlp_cols, r.wm, r.sem_wm, r.sem_pwm, r.sem_swm)
-    r.ho[...] = r.xb[c].astype(F32)
-    scatter_total(r.p_o, r.l_o, r.r_o, r.sem_o, r.ho)
-    h_own = r.ho[...]
-    r.mb[c] = (h_own * rms(h_own) * mlp_gain).astype(BF16)
-    gather_start(r.mb.at[c], r.mb, r.sem_mb)
-    gather_relay(r.mb, r.sem_mb)
-    weights_forward(r.wm, r.sem_pwm, r.sem_swm)
-    for by in range(1, n.ctx):
-        arrived(r.gb.at[behind(by)], r.sem_g.at[1, by])
-    weights_wait(r.wm, r.sem_swm)
-
+        step = 2 * HEAD_DIM
+        for at in range(0, d, step):
+            product = mm(left[...], right(slice(at, at + step)), LAST_AXIS)
+            out[:, :, at : at + step] = product.astype(BF16).reshape(n.ctx, rows, step)
+
+    by_rows(r.at, lambda span: r.wa[span, o_at:], r.p_o)
+    steps = range(n.ctx - 1)
+    for k in range(PARTS):
+        scatter_start(sum_o, k)
+    weights_spread(own_mlp, mlp_cols, r.sem_wm, plane_m)
+
+    def residual(k):
+        span = rows_of(k)
+        r.ho[span, :] = r.xb[c, span, :].astype(F32)
+        scatter_total(sum_o, r.ho, k)
+        own = r.ho[span, :]
+        r.mb[c, span, :] = (own * rms(own) * mlp_gain).astype(BF16)
+        gather_start(r.mb.at[c], r.mb, r.sem_mb, k)
+
+    for by in range(1, n.ctx - 1):
+        for k in range(PARTS):
+            gather_relay(r.gb, r.sem_gb, by, k)
+    for step in steps:
+        scatter_relay(sum_o, step, 0)
+    residual(0)
+    for k in range(1, PARTS):
+        for step in steps:
+            scatter_relay(sum_o, step, k)
+        gather_relay(r.mb, r.sem_mb, 1, k - 1)
+        residual(k)
+    weights_forward(plane_m)
+    for by in range(2, n.ctx):
+        gather_relay(r.mb, r.sem_mb, by, 0)
+    for k in range(PARTS):
+        gather_relay(r.gb, r.sem_gb, n.ctx - 1, k)
+    weights_wait(plane_m)
+
+    tile = 2 * HEAD_DIM if ff % (2 * HEAD_DIM) == 0 else HEAD_DIM
+    span_rows = n.ctx * part_rows
+
+    def mlp_part(k):
+        span = rows_of(k)
+        mixed = r.mb[:, span, :].reshape(span_rows, d)
+        upstream = r.gb[:, span, :].reshape(span_rows, d)
+        for at in range(0, ff, tile):
+            gate = mm(mixed, r.wm[:, at : at + tile])
+            up = mm(mixed, r.wm[:, ff + at : ff + at + tile])
+            back = mm(upstream, r.wm[:, 2 * ff + at : 2 * ff + at + tile])
+            sig = jax.nn.sigmoid(gate)
+            swish = gate * sig
+            shape = (n.ctx, part_rows, tile)
+            r.hid[:, span, at : at + tile] = (swish * up).astype(BF16).reshape(shape)
+            r.dgu[:, span, at : at + tile] = (
+                (back * up * sig * (1.0 + gate * (1.0 - sig))).astype(BF16).reshape(shape)
+            )
+            r.dgu[:, span, ff + at : ff + at + tile] = (
+                (back * swish).astype(BF16).reshape(shape)
+            )
+        both = r.dgu[:, span, :].reshape(span_rows, 2 * ff)
+        for at in range(0, d, 2 * HEAD_DIM):
+            product = mm(both, r.wm[at : at + 2 * HEAD_DIM, : 2 * ff], LAST_AXIS).astype(BF16)
+            r.p_x2[:, span, at : at + 2 * HEAD_DIM] = product.reshape(
+                n.ctx, part_rows, 2 * HEAD_DIM
+            )
+        scatter_start(sum_x2, k)
+
+    def residual_back(k):
+        span = rows_of(k)
+        r.dh[span, :] = jnp.zeros((part_rows, d), F32)
+        scatter_total(sum_x2, r.dh, k)
+        own = r.ho[span, :]
+        from_norm, term = norm_back(own, rms(own), mlp_gain, r.dh[span, :])
+        save_lines(n.lines, jnp.sum(term, axis=0, keepdims=True))
+        r.dh[span, :] = r.gb[c, span, :].astype(F32) + from_norm
+        r.rb[c, span, :] = r.dh[span, :].astype(BF16)
+        gather_start(r.rb.at[c], r.rb, r.sem_rb, k)
+
+    mlp_part(0)
+    for k in range(1, PARTS):
+        for step in steps:
+            gather_relay(r.mb, r.sem_mb, step + 1, k)
+            scatter_relay(sum_x2, step, k - 1)
+        mlp_part(k)
+        residual_back(k - 1)
+    hidden = r.hid[...].reshape(n.tokens, ff)
+    by_rows(hidden, lambda span: r.wm[span, 2 * ff :], r.p_y)
+    scatter_start(sum_y, 0)
     mixed = r.mb[...].reshape(n.tokens, d)
     upstream = r.gb[...].reshape(n.tokens, d)
-    tile = 2 * HEAD_DIM if ff % (2 * HEAD_DIM) == 0 else HEAD_DIM
+    for at in range(0, 2 * ff, tile):
+        part = r.dgu[:, :, at : at + tile].reshape(n.tokens, tile)
+        r.gm[:, at : at + tile] = mm(mixed, part, FIRST_AXIS).astype(BF16)
     for at in range(0, ff, tile):
-        gate = mm(mixed, r.wm[:, at : at + tile])
-        up = mm(mixed, r.wm[:, ff + at : ff + at + tile])
-        back = mm(upstream, r.wm[:, 2 * ff + at : 2 * ff + at + tile])
-        sig = jax.nn.sigmoid(gate)
-        swish = gate * sig
-        r.hid[:, at : at + tile] = (swish * up).astype(BF16)
-        r.dgu[:, at : at + tile] = (back * up * sig * (1.0 + gate * (1.0 - sig))).astype(BF16)
-        r.dgu[:, ff + at : ff + at + tile] = (back * swish).astype(BF16)
-
-    by_rows(r.dgu, lambda: r.wm[:, : 2 * ff], r.p_x2)
-    scatter(r.p_x2, r.l_x2, r.r_x2, r.sem_x2)
-    by_rows(r.hid, lambda: r.wm[:, 2 * ff :], r.p_y)
-    r.dh[...] = jnp.zeros_like(r.dh)
-    scatter_total(r.p_x2, r.l_x2, r.r_x2, r.sem_x2, r.dh)
-    h_own = r.ho[...]
-    from_norm, term = norm_back(h_own, rms(h_own), mlp_gain, r.dh[...])
-    r.g1_acc[3] = jnp.zeros_like(r.g1_acc[3])
-    save_lines(n.lines, jnp.sum(term, axis=0, keepdims=True))
-    r.dh[...] = r.gb[c].astype(F32) + from_norm
-    r.rb[c] = r.dh[...].astype(BF16)
-    gather_start(r.rb.at[c], r.rb, r.sem_rb)
-    gather_relay(r.rb, r.sem_rb)
-    for by in range(1, n.ctx):
-        send(
-            r.p_y.at[ahead(by)], r.i_y.at[by - 1], r.sem_y.at[0, by], r.sem_y.at[1, by], None, ahead(by)
-        )
-    for at in range(0, 2 * ff, tile):
-        r.gm[:, at : at + tile] = mm(mixed, r.dgu[:, at : at + tile], FIRST_AXIS).astype(BF16)
-    for at in range(0, ff, tile):
-        r.gm[:, 2 * ff + at : 2 * ff + at + tile] = mm(
-            upstream, r.hid[:, at : at + tile], FIRST_AXIS
-        ).astype(BF16)
-    grads_pair(r.gm, r.gm_sib, r.sem_sgm)
+        part = r.hid[:, :, at : at + tile].reshape(n.tokens, tile)
+        r.gm[:, 2 * ff + at : 2 * ff + at + tile] = mm(upstream, part, FIRST_AXIS).astype(BF16)
+    grads_pair(group_m)
+    for step in steps:
+        scatter_relay(sum_x2, step, PARTS - 1)
+        if step == 0:
+            grads_plane(group_m)
+    for k in range(PARTS - 1):
+        gather_relay(r.rb, r.sem_rb, 1, k)
+    residual_back(PARTS - 1)
+    for k in range(1, PARTS):
+        scatter_start(sum_y, k)
+    for k in range(PARTS - 1):
+        gather_relay(r.rb, r.sem_rb, 2, k)
+    gather_relay(r.rb, r.sem_rb, 1, PARTS - 1)
+    gather_relay(r.rb, r.sem_rb, 2, PARTS - 1)
+    for step in steps:
+        scatter_relay(sum_y, step, 0)
+    for by in range(3, n.ctx):
+        for k in range(PARTS):
+            gather_relay(r.rb, r.sem_rb, by, k)
 
     upstream = r.rb[...].reshape(n.tokens, d)
     for at in range(0, o_cols, HEAD_DIM):
         r.da[at // HEAD_DIM] = mm(upstream, r.wa[:, o_at + at : o_at + at + HEAD_DIM])
-    grads_plane(r.gm, r.gm_sib, r.sem_sgm, r.gm_in, r.sem_pgm)
+    r.ga[:, o_at:] = mm(upstream, r.at[...], FIRST_AXIS).astype(BF16)
+    grads_pair(group_o)
+    grads_line(group_m)
     r.dk[...] = jnp.zeros_like(r.dk)
     r.dv[...] = jnp.zeros_like(r.dv)
 
@@ -806,6 +919,10 @@
         return term + jnp.sum(gain_term, axis=0, keepdims=True)
 
     q_term = lax.fori_loop(0, n.heads, query_backward, jnp.zeros((1, HEAD_DIM), F32))
+    for k in range(1, PARTS):
+        for step in steps:
+            scatter_relay(sum_y, step, k)
+    grads_plane(group_o)
     k_term = jnp.zeros((1, HEAD_DIM), F32)
     for kv in range(n.kv):
         u = r.kp[kv]
@@ -817,41 +934,42 @@
         at += k_cols
         r.dqkv[:, at : at + HEAD_DIM] = r.dv[kv].astype(BF16)
         k_term = k_term + jnp.sum(gain_term, axis=0, keepdims=True)
-    by_rows(r.dqkv, lambda: r.wa[:, :o_at], r.p_x1)
-    scatter(r.p_x1, r.l_x1, r.r_x1, r.sem_x1)
     for at in range(0, o_at, 2 * HEAD_DIM):
         r.ga[:, at : at + 2 * HEAD_DIM] = mm(
             r.xn[...], r.dqkv[:, at : at + 2 * HEAD_DIM], FIRST_AXIS
         ).astype(BF16)
-    r.ga[:, o_at:] = mm(upstream, r.at[...], FIRST_AXIS).astype(BF16)
-    grads_pair(r.ga, r.ga_sib, r.sem_sga)
-    grads_line(
-        r.gm, r.gm_sib, r.sem_sgm, r.gm_in, r.sem_pgm, r.gm_z, r.gm_land, r.sem_zgm
-    )
-    grads_plane(r.ga, r.ga_sib, r.sem_sga, r.ga_in, r.sem_pga)
-
+    grads_pair(group_q)
+    by_rows(r.dqkv, lambda span: r.wa[span, :o_at], r.p_x1)
+    for k in range(PARTS):
+        scatter_start(sum_x1, k)
+    grads_plane(group_q)
+    grads_line(group_o)
+    for k in range(PARTS):
+        for step in steps:
+            scatter_relay(sum_x1, step, k)
+        if k == 0:
+            grads_line(group_q)
+    for k in range(PARTS):
+        scatter_total(sum_y, r.ho, k)
+    r.out_hidden[...] = r.ho[...].astype(BF16)
     r.out_input[...] = jnp.zeros_like(r.out_input)
-    scatter_total(r.p_x1, r.l_x1, r.r_x1, r.sem_x1, r.out_input)
+    for k in range(PARTS):
+        scatter_total(sum_x1, r.out_input, k)
     x = r.xb[c].astype(F32)
     from_norm, term = norm_back(x, rms(x), attn_gain, r.out_input[...])
     save_lines(0, jnp.sum(term, axis=0, keepdims=True))
     r.out_input[...] = r.dh[...] + from_norm
     r.g1_acc[3, 2 * n.lines : 2 * n.lines + 1, :] = q_term
     r.g1_acc[3, 2 * n.lines + 1 : 2 * n.lines + 2, :] = k_term
-    small_start(r.g1_acc.at[3], r.g1_in, r.sem_g1)
-    small_plane(r.g1_acc.at[3], r.g1_in, r.g1_acc, r.sem_g1)
-    out = r.ho[...] + r.p_y[c].astype(F32)
-    for by in range(1, n.ctx):
-        arrived(r.i_y.at[by - 1], r.sem_y.at[1, by])
-        out = out + r.i_y[by - 1].astype(F32)
-    r.out_hidden[...] = out.astype(BF16)
-    small_line(r.g1_in, r.g1_acc, r.sem_g1)
-    grads_line(
-        r.ga, r.ga_sib, r.sem_sga, r.ga_in, r.sem_pga, r.ga_z, r.ga_land, r.sem_zga
-    )
-    grads_out(r.gm_land, r.sem_zgm, (r.og, r.ou, r.od), mlp_cols)
-    r.out_gains[...] = small_end(r.g1_in, r.g1_acc, r.sem_g1)
-    grads_out(r.ga_land, r.sem_zga, (r.oq, r.ok, r.ov, r.oo), attn_cols)
+    small_send(r.g1_acc.at[3], r.g1_in, r.sem_g1, "pair")
+    r.g1_acc[0] = small_sum(r.g1_acc.at[3], r.g1_in, r.sem_g1, "pair")
+    small_send(r.g1_acc.at[0], r.g1_in, r.sem_g1, "plane")
+    r.g1_acc[1] = small_sum(r.g1_acc.at[0], r.g1_in, r.sem_g1, "plane")
+    small_send(r.g1_acc.at[1], r.g1_in, r.sem_g1, "line")
+    grads_wait(group_m)
+    grads_wait(group_o)
+    grads_wait(group_q)
+    r.out_gains[...] = small_sum(r.g1_acc.at[1], r.g1_in, r.sem_g1, "line")
     for wait in sends:
         wait()
 
@@ -876,24 +994,8 @@
 ):
     shards = (q_weight, k_weight, v_weight, o_weight, gate_weight, up_weight, down_weight)
     n = Sizes(ctx, fsdp, hidden_in.shape[1], shards)
-    me = lax.axis_index("fsdp") * ctx + lax.axis_index("ctx")
-    count = ctx * fsdp
-    slots = block_order.shape[1]
-    block_len = n.tokens // slots
-    positions = (
-        block_order[0][:, None] * block_len + jnp.arange(block_len, dtype=jnp.int32)[None, :]
-    ).reshape(-1)
-    cosine, sine = rope_tables(positions, HEAD_DIM)
-    sign = jnp.where(jnp.arange(HEAD_DIM) < HEAD_DIM // 2, -1.0, 1.0)
-    sine = sine * sign
-
-    def placed(gain):
-        own = jnp.arange(count, dtype=jnp.int32)[:, None] == me
-        whole = jnp.where(own, gain.astype(F32)[None, :], 0.0)
-        return whole.reshape(-1, HEAD_DIM)
-
-    gains = jnp.concatenate([placed(g) for g in (attn_gain, mlp_gain, query_gain, key_gain)])
-    gains = jnp.pad(gains, ((0, n.gain_rows - gains.shape[0]), (0, 0)))
+    gains = jnp.concatenate([attn_gain, mlp_gain, query_gain, key_gain]).astype(F32)
+    gains = jnp.pad(gains, (0, HEAD_DIM - gains.shape[0])).reshape(1, HEAD_DIM)
     hbm, vmem = pl.BlockSpec(memory_space=pl.ANY), pl.BlockSpec(memory_space=pltpu.VMEM)
     inputs = dict(
         hidden=(hidden_in[0], hbm),
@@ -906,25 +1008,17 @@
         wu=(up_weight, hbm),
         wd=(down_weight, hbm),
         gains=(gains, vmem),
-        cos=(cosine, vmem),
-        sin=(sine, vmem),
-        posq=(positions[:, None], vmem),
-        posk=(positions[None, :], vmem),
+        order=(block_order, pl.BlockSpec(memory_space=pltpu.SMEM)),
     )
     outputs = dict(
         out_hidden=jax.ShapeDtypeStruct((n.rows, n.width), BF16),
         out_input=jax.ShapeDtypeStruct((n.rows, n.width), F32),
-        oq=jax.ShapeDtypeStruct(q_weight.shape, F32),
-        ok=jax.ShapeDtypeStruct(k_weight.shape, F32),
-        ov=jax.ShapeDtypeStruct(v_weight.shape, F32),
-        oo=jax.ShapeDtypeStruct(o_weight.shape, F32),
-        og=jax.ShapeDtypeStruct(gate_weight.shape, F32),
-        ou=jax.ShapeDtypeStruct(up_weight.shape, F32),
-        od=jax.ShapeDtypeStruct(down_weight.shape, F32),
+        ga_land=jax.ShapeDtypeStruct((ctx, n.shard, n.attn_cols), BF16),
+        gm_land=jax.ShapeDtypeStruct((ctx, n.shard, n.mlp_cols), BF16),
         out_gains=jax.ShapeDtypeStruct((n.gain_rows, HEAD_DIM), F32),
     )
     scratch = scratch_of(n)
-    result, input_grad, oq, ok, ov, oo, og, ou, od, sums = pl.pallas_call(
+    landed = pl.pallas_call(
         functools.partial(layer_kernel, n, [*inputs, *outputs, *scratch]),
         out_shape=tuple(outputs.values()),
         in_specs=[spec for _, spec in inputs.values()],
@@ -936,11 +1030,15 @@
         name="layer",
     )(*[value for value, _ in inputs.values()])
 
-    def own(first, size):
-        flat = sums[first : first + size // HEAD_DIM].reshape(-1)
-        return lax.dynamic_slice_in_dim(flat, me * (size // count), size // count)
-
-    lines = n.lines
+    finals = [(n.rows, n.width, BF16), (n.rows, n.width, F32)]
+    finals += [(s.shape[0], s.shape[1], F32) for s in shards] + [(8, HEAD_DIM, F32)]
+    result, input_grad, oq, ok, ov, oo, og, ou, od, sums = pl.pallas_call(
+        functools.partial(emit_kernel, n),
+        out_shape=tuple(jax.ShapeDtypeStruct(f[:2], f[2]) for f in finals),
+        in_specs=[vmem] * len(outputs),
+        out_specs=tuple(vmem for _ in finals),
+        name="emit",
+    )(*landed)
     return (
         result[None],
         input_grad[None],
@@ -948,18 +1046,48 @@
         ok,
         ov,
         oo,
-        own(0, n.width),
-        own(2 * lines, HEAD_DIM),
-        own(2 * lines + 1, HEAD_DIM),
-        own(lines, n.width),
+        sums[0, : n.each],
+        sums[2, : n.few],
+        sums[3, : n.few],
+        sums[1, : n.each],
         og,
         ou,
         od,
     )
 
 
+def emit_kernel(n, result, input_grad, attn_land, mlp_land, sums, *outs):
+    outs[0][...] = result[...]
+    outs[1][...] = input_grad[...]
+    which = 2
+    for land, widths in ((attn_land, n.cols[:4]), (mlp_land, n.cols[4:])):
+        at = 0
+        for width in widths:
+            for j in range(n.ctx):
+                outs[which][:, j * width : (j + 1) * width] = land[j, :, at : at + width].astype(
+                    F32
+                )
+            at += width
+            which += 1
+    me = lax.axis_index("fsdp") * n.ctx + lax.axis_index("ctx")
+    row, at = me * n.each // HEAD_DIM, lax.rem(me * n.each, HEAD_DIM)
+    sums_out = outs[which]
+    sums_out[...] = jnp.zeros_like(sums_out)
+    for i, (line, lane) in enumerate(
+        (
+            (row, at),
+            (n.lines + row, at),
+            (2 * n.lines, me * n.few),
+            (2 * n.lines + 1, me * n.few),
+        )
+    ):
+        back = lax.rem(HEAD_DIM - lane, HEAD_DIM)
+        sums_out[i : i + 1, :] = pltpu.roll(sums[pl.ds(line, 1), :], back, 1)
+
+
 def fits(ctx, fsdp, shard_rows):
-    return shard_rows % 16 == 0 and fsdp % 2 == 0 and KV_HEADS % ctx == 0
+    per_tile = HEAD_DIM % (2 * shard_rows) == 0 and HEAD_DIM % (ctx * fsdp) == 0
+    return per_tile and shard_rows % 16 == 0 and fsdp % 2 == 0 and KV_HEADS % ctx == 0
 
 
 def solution(mesh):

time: 264 us -> 221 us (0.84)
  Pallas kernels: 243 us -> 217 us
  local copies, waits for them, and re-layouts: 16.6 us -> 2.38 us
    pallas_call x1, Pallas kernels: 243 us -> 214 us  [fused(): pl.pallas_call(functools.partial(layer_kernel, n, [*inputs, *outputs, *sc...]
    unnamed x35 -> x10, local copies, waits for them, and re-layouts: 11.3 us -> 1.35 us
    pallas_call x0 -> x1, Pallas kernels: none -> 2.98 us  [fused(): pl.pallas_call(functools.partial(emit_kernel, n), out_shape=tuple((jax.Sh...]
where the time goes in v3:
time: 221 us
  Pallas kernels  217 us (98%)
  local copies, waits for them, and re-layouts  2.38 us (1%)
    pallas_call x1, Pallas kernels, fused(): pl.pallas_call(functools.partial(layer_kernel, n, [*inputs, *outputs, *sc...  214 us

profile of v3, /device:TPU:0, one launch (start us, length us, event | category | flops | bytes accessed | tf_op | source)
XLA Modules:
  0.0 221.1 jit_solution(15613427610311326868)
XLA Ops:
  0.6 0.0 copy-start.4
  0.7 0.0 copy-start.1
  0.7 0.0 copy-start.2
  0.7 0.0 copy-start.3
  0.7 0.6 copy-done.4
  1.3 0.0 copy-done.1
  1.3 0.0 copy-done.2
  1.3 0.0 copy-done.3
  1.3 0.6 fusion.1.refs_9_
  1.9 214.5 %layer.1 = (bf16[128,1024]{1,0:T(8,128)(2,1)}, f32[128,1024]{1,0:T(8,128)}, bf16[4,32,1536]{2,1,0:T(8,128)(2,1)}, bf16[4,32,2304]{2,1,0:T(8,128)(2,1)}, f32[24,128]{1,0:T(8,128)}) custom-call(bf16[128,1024]{1,0:T(8,128)(2,1)} %bitcast.17, bf16[128,1024]{1,0:T(8,128)(2,1)} %bitcast.18, bf16[32,2048]{1,0:T(8,128)(2,1)} %refs_2_.1, bf16[32,1024]{1,0:T(8,128)(2,1)} %refs_3_.1, ...), custom_call_target="tpu_custom_call" | custom-call | tf_op jit(solution)/shard_map/layer/pallas_call | solution.py:1021
  216.4 3.0 %emit.1 = (bf16[128,1024]{1,0:T(8,128)(2,1)}, f32[128,1024]{1,0:T(8,128)}, f32[32,2048]{1,0:T(8,128)}, f32[32,1024]{1,0:T(8,128)}, f32[32,1024]{1,0:T(8,128)}, /...) custom-call(bf16[128,1024]{1,0:T(8,128)(2,1)} %get-tuple-element.28.r, ...), custom_call_target="tpu_custom_call" | custom-call | tf_op jit(solution)/shard_map/emit/pallas_call | solution.py:1035
  219.4 0.0 copy-start
  219.4 0.7 copy-done
  220.1 0.5 slice_bitcast_fusion.1
  220.6 0.5 slice_bitcast_fusion
Async XLA Ops:
  0.6 0.7 copy-start.4
  0.7 0.7 copy-start.1
  0.7 0.7 copy-start.2
  0.7 0.7 copy-start.3
  219.4 0.7 copy-start

commit v4 on v3

--- a/solution.py
+++ b/solution.py
@@ -414,16 +414,19 @@
         send_if(up, piece, here, sem.at[0, 0, k], sem.at[2, c, k], right)
         send_if(down, piece, here, sem.at[1, 0, k], sem.at[2, c, k], left)
 
-    def gather_relay(buf, sem, by, k):
+    def gather_relay(buf, sem, by, k, source=None):
         low, high = jnp.maximum(c - by, 0), jnp.minimum(c + by, n.ctx - 1)
+        from_low, from_high = c - by >= 0, c + by < n.ctx
+        if source == "end":
+            from_low, from_high = c == by, c + by == n.ctx - 1
+        elif source == "between":
+            from_low, from_high = c > by, c + by < n.ctx - 1
         piece, here = part_of(buf, low, k), sem.at[2, low, k]
-        pl.when(c - by >= 0)(functools.partial(arrived, piece, here))
-        cond = (c - by >= 0) & (c + 1 < n.ctx)
-        send_if(cond, piece, piece, sem.at[0, by, k], here, right)
+        pl.when(from_low)(functools.partial(arrived, piece, here))
+        send_if(from_low & (c + 1 < n.ctx), piece, piece, sem.at[0, by, k], here, right)
         piece, here = part_of(buf, high, k), sem.at[2, high, k]
-        pl.when(c + by < n.ctx)(functools.partial(arrived, piece, here))
-        cond = (c + by < n.ctx) & (c > 0)
-        send_if(cond, piece, piece, sem.at[1, by, k], here, left)
+        pl.when(from_high)(functools.partial(arrived, piece, here))
+        send_if(from_high & (c > 0), piece, piece, sem.at[1, by, k], here, left)
 
     def rows_of(k):
         return slice(k * part_rows, (k + 1) * part_rows)
@@ -451,14 +454,18 @@
             scatter_send(c == 0, g.part, g.low, g.sem, n.ctx - 1 - step, k, 0, right)
 
     def scatter_relay(g, step, k):
-        target = step
-        down = (c > target) & (c + 1 < n.ctx)
-        pl.when(down)(functools.partial(scatter_add, g.part, g.high, g.sem, target, k, 1))
-        scatter_send(down, g.part, g.high, g.sem, target, k, 1, left)
-        target = n.ctx - 1 - step
-        up = (c < target) & (c > 0)
-        pl.when(up)(functools.partial(scatter_add, g.part, g.low, g.sem, target, k, 0))
-        scatter_send(up, g.part, g.low, g.sem, target, k, 0, right)
+        near = c < n.ctx // 2
+        low, high = n.ctx - 1 - step, step
+        up, down = (c < low) & (c > 0), (c > high) & (c + 1 < n.ctx)
+
+        def go_up(cond):
+            pl.when(cond)(functools.partial(scatter_add, g.part, g.low, g.sem, low, k, 0))
+            scatter_send(cond, g.part, g.low, g.sem, low, k, 0, right)
+
+        go_up(up & near)
+        pl.when(down)(functools.partial(scatter_add, g.part, g.high, g.sem, high, k, 1))
+        scatter_send(down, g.part, g.high, g.sem, high, k, 1, left)
+        go_up(up & ~near)
 
     def scatter_total(g, out, k):
         span = rows_of(k)
@@ -744,6 +751,7 @@
                 )
             else:
                 r.vv[head - n.heads - n.kv] = u.astype(BF16)
+    weights_forward(plane_o)
     half = n.tokens // 2
 
     def head_forward(h, carry):
@@ -761,7 +769,6 @@
         return carry
 
     lax.fori_loop(0, n.heads, head_forward, 0)
-    weights_forward(plane_o)
     weights_wait(plane_o)
 
     def by_rows(left, right, out):
@@ -784,22 +791,24 @@
         r.mb[c, span, :] = (own * rms(own) * mlp_gain).astype(BF16)
         gather_start(r.mb.at[c], r.mb, r.sem_mb, k)
 
-    for by in range(1, n.ctx - 1):
-        for k in range(PARTS):
-            gather_relay(r.gb, r.sem_gb, by, k)
+    gather_relay(r.gb, r.sem_gb, 1, 0)
     for step in steps:
         scatter_relay(sum_o, step, 0)
+    for by in range(2, n.ctx - 1):
+        gather_relay(r.gb, r.sem_gb, by, 0)
     residual(0)
-    for k in range(1, PARTS):
-        for step in steps:
-            scatter_relay(sum_o, step, k)
-        gather_relay(r.mb, r.sem_mb, 1, k - 1)
-        residual(k)
+    for step in steps:
+        scatter_relay(sum_o, step, 1)
+        if step == 0:
+            gather_relay(r.mb, r.sem_mb, 1, 0, "between")
+    residual(1)
+    gather_relay(r.mb, r.sem_mb, 1, 0, "end")
+    gather_relay(r.mb, r.sem_mb, 1, 1, "between")
+    for by in range(2, n.ctx - 1):
+        gather_relay(r.mb, r.sem_mb, by, 0)
     weights_forward(plane_m)
-    for by in range(2, n.ctx):
-        gather_relay(r.mb, r.sem_mb, by, 0)
-    for k in range(PARTS):
-        gather_relay(r.gb, r.sem_gb, n.ctx - 1, k)
+    gather_relay(r.mb, r.sem_mb, n.ctx - 1, 0)
+    gather_relay(r.gb, r.sem_gb, n.ctx - 1, 0)
     weights_wait(plane_m)
 
     tile = 2 * HEAD_DIM if ff % (2 * HEAD_DIM) == 0 else HEAD_DIM
@@ -843,12 +852,18 @@
         gather_start(r.rb.at[c], r.rb, r.sem_rb, k)
 
     mlp_part(0)
-    for k in range(1, PARTS):
-        for step in steps:
-            gather_relay(r.mb, r.sem_mb, step + 1, k)
-            scatter_relay(sum_x2, step, k - 1)
-        mlp_part(k)
-        residual_back(k - 1)
+    gather_relay(r.mb, r.sem_mb, 1, 1, "end")
+    gather_relay(r.gb, r.sem_gb, 1, 1)
+    for step in steps:
+        scatter_relay(sum_x2, step, 0)
+        if step == 0:
+            for by in range(2, n.ctx - 1):
+                gather_relay(r.mb, r.sem_mb, by, 1)
+                gather_relay(r.gb, r.sem_gb, by, 1)
+    gather_relay(r.mb, r.sem_mb, n.ctx - 1, 1)
+    gather_relay(r.gb, r.sem_gb, n.ctx - 1, 1)
+    mlp_part(1)
+    residual_back(0)
     hidden = r.hid[...].reshape(n.tokens, ff)
     by_rows(hidden, lambda span: r.wm[span, 2 * ff :], r.p_y)
     scatter_start(sum_y, 0)
@@ -862,23 +877,24 @@
         r.gm[:, 2 * ff + at : 2 * ff + at + tile] = mm(upstream, part, FIRST_AXIS).astype(BF16)
     grads_pair(group_m)
     for step in steps:
-        scatter_relay(sum_x2, step, PARTS - 1)
+        scatter_relay(sum_x2, step, 1)
         if step == 0:
+            gather_relay(r.rb, r.sem_rb, 1, 0, "between")
             grads_plane(group_m)
-    for k in range(PARTS - 1):
-        gather_relay(r.rb, r.sem_rb, 1, k)
-    residual_back(PARTS - 1)
-    for k in range(1, PARTS):
-        scatter_start(sum_y, k)
-    for k in range(PARTS - 1):
-        gather_relay(r.rb, r.sem_rb, 2, k)
-    gather_relay(r.rb, r.sem_rb, 1, PARTS - 1)
-    gather_relay(r.rb, r.sem_rb, 2, PARTS - 1)
+        elif step == 1:
+            gather_relay(r.rb, r.sem_rb, 1, 0, "end")
+    for by in range(2, n.ctx - 1):
+        gather_relay(r.rb, r.sem_rb, by, 0)
+    residual_back(1)
+    scatter_start(sum_y, 1)
+    gather_relay(r.rb, r.sem_rb, 1, 1, "between")
+    gather_relay(r.rb, r.sem_rb, 1, 1, "end")
+    for by in range(2, n.ctx - 1):
+        gather_relay(r.rb, r.sem_rb, by, 1)
     for step in steps:
         scatter_relay(sum_y, step, 0)
-    for by in range(3, n.ctx):
-        for k in range(PARTS):
-            gather_relay(r.rb, r.sem_rb, by, k)
+    for k in range(PARTS):
+        gather_relay(r.rb, r.sem_rb, n.ctx - 1, k)
 
     upstream = r.rb[...].reshape(n.tokens, d)
     for at in range(0, o_cols, HEAD_DIM):
@@ -919,9 +935,6 @@
         return term + jnp.sum(gain_term, axis=0, keepdims=True)
 
     q_term = lax.fori_loop(0, n.heads, query_backward, jnp.zeros((1, HEAD_DIM), F32))
-    for k in range(1, PARTS):
-        for step in steps:
-            scatter_relay(sum_y, step, k)
     grads_plane(group_o)
     k_term = jnp.zeros((1, HEAD_DIM), F32)
     for kv in range(n.kv):
@@ -942,6 +955,8 @@
     by_rows(r.dqkv, lambda span: r.wa[span, :o_at], r.p_x1)
     for k in range(PARTS):
         scatter_start(sum_x1, k)
+    for step in steps:
+        scatter_relay(sum_y, step, 1)
     grads_plane(group_q)
     grads_line(group_o)
     for k in range(PARTS):

time: 221 us -> 197 us (0.89)
  Pallas kernels: 217 us -> 193 us
    pallas_call x1, Pallas kernels: 214 us -> 190 us  [fused(): pl.pallas_call(functools.partial(layer_kernel, n, [*inputs, *outputs, *sc...]
where the time goes in v4:
time: 197 us
  Pallas kernels  193 us (98%)
  local copies, waits for them, and re-layouts  2.38 us (1%)
    pallas_call x1, Pallas kernels, fused(): pl.pallas_call(functools.partial(layer_kernel, n, [*inputs, *outputs, *sc...  190 us

profile of v4, /device:TPU:0, one launch (start us, length us, event | category | flops | bytes accessed | tf_op | source)
XLA Modules:
  0.0 197.0 jit_solution(13327028975578180804)
XLA Ops:
  0.6 0.0 copy-start.4
  0.7 0.0 copy-start.1
  0.7 0.0 copy-start.2
  0.7 0.0 copy-start.3
  0.7 0.6 copy-done.4
  1.3 0.0 copy-done.1
  1.3 0.0 copy-done.2
  1.3 0.0 copy-done.3
  1.3 0.6 fusion.1.refs_9_
  1.9 190.3 %layer.1 = (bf16[128,1024]{1,0:T(8,128)(2,1)}, f32[128,1024]{1,0:T(8,128)}, bf16[4,32,1536]{2,1,0:T(8,128)(2,1)}, bf16[4,32,2304]{2,1,0:T(8,128)(2,1)}, f32[24,128]{1,0:T(8,128)}) custom-call(bf16[128,1024]{1,0:T(8,128)(2,1)} %bitcast.17, bf16[128,1024]{1,0:T(8,128)(2,1)} %bitcast.18, bf16[32,2048]{1,0:T(8,128)(2,1)} %refs_2_.1, bf16[32,1024]{1,0:T(8,128)(2,1)} %refs_3_.1, ...), custom_call_target="tpu_custom_call" | custom-call | tf_op jit(solution)/shard_map/layer/pallas_call | solution.py:1036
  192.3 3.0 %emit.1 = (bf16[128,1024]{1,0:T(8,128)(2,1)}, f32[128,1024]{1,0:T(8,128)}, f32[32,2048]{1,0:T(8,128)}, f32[32,1024]{1,0:T(8,128)}, f32[32,1024]{1,0:T(8,128)}, /...) custom-call(bf16[128,1024]{1,0:T(8,128)(2,1)} %get-tuple-element.28.r, ...), custom_call_target="tpu_custom_call" | custom-call | tf_op jit(solution)/shard_map/emit/pallas_call | solution.py:1050
  195.3 0.0 copy-start
  195.3 0.7 copy-done
  195.9 0.5 slice_bitcast_fusion.1
  196.5 0.5 slice_bitcast_fusion
Async XLA Ops:
  0.6 0.7 copy-start.4
  0.7 0.7 copy-start.1
  0.7 0.7 copy-start.2
  0.7 0.7 copy-start.3
  195.3 0.7 copy-start

commit v5 on v4

--- a/solution.py
+++ b/solution.py
@@ -19,6 +19,7 @@
 F32 = jnp.float32
 VMEM_LIMIT = 67043328
 PARTS = 2
+PIECES = 2
 
 
 def mm(left, right, dims=(((1,), (0,)), ((), ()))):
@@ -320,9 +321,9 @@
         out["p_" + name] = bf(c, n.rows, d)
         out["l_" + name] = bf(c, n.rows, d)
         out["r_" + name] = bf(c, n.rows, d)
-        out["sem_" + name] = sem(4, c, PARTS)
+        out["sem_" + name] = sem(4, c, PARTS * PIECES)
     for name in ("xb", "gb", "mb", "rb"):
-        out["sem_" + name] = sem(3, c, PARTS)
+        out["sem_" + name] = sem(3, c, PARTS * PIECES)
     out["sem_wa"] = sem(2, c - 1, 4)
     out["sem_wm"] = sem(2, c - 1, 3)
     for name in ("pq", "po", "pm"):
@@ -331,9 +332,9 @@
         out["sem_" + name] = sem(4, n.chips)
         out["sem_z" + name] = sem(2, c)
     for name in ("g0", "g1"):
-        out[name + "_in"] = f32(n.chips + c, n.gain_rows, HEAD_DIM)
+        out[name + "_in"] = f32(n.fsdp + c, n.gain_rows, HEAD_DIM)
         out[name + "_acc"] = f32(4, n.gain_rows, HEAD_DIM)
-        out["sem_" + name] = sem(2, n.chips + c)
+        out["sem_" + name] = sem(2, n.fsdp + c)
     return out
 
 
@@ -392,27 +393,33 @@
 
     for by in range(1, n.ctx):
         greet(f, ahead(by))
-    for by in range(1, n.chips):
-        greet(chip_ahead(by) * 2 + core, c)
-    greet(sibling, c)
-    pl.semaphore_wait(barrier, n.ctx - 1 + n.chips)
+    for by in range(1, n.fsdp):
+        greet(lax.rem(f + by, n.fsdp), c)
+    pl.semaphore_wait(barrier, n.ctx - 1 + n.fsdp - 1)
 
     right, left = jnp.minimum(c + 1, n.ctx - 1), jnp.maximum(c - 1, 0)
-    part_rows = rows // PARTS
-
-    def part_of(buf, j, k):
-        return buf.at[j, pl.ds(k * part_rows, part_rows), :]
+    part_rows, piece_rows = rows // PARTS, rows // (PARTS * PIECES)
+
+    def pieces_of(k):
+        return range(k * PIECES, (k + 1) * PIECES)
+
+    def part_of(buf, j, i):
+        return buf.at[j, pl.ds(i * piece_rows, piece_rows), :]
 
     def gather_start(src, buf, sem, k, to=None):
-        piece = src.at[pl.ds(k * part_rows, part_rows), :]
-        here = part_of(buf, c, k)
+        for i in pieces_of(k):
+            gather_piece(src, buf, sem, i, to)
+
+    def gather_piece(src, buf, sem, i, to=None):
+        piece = src.at[pl.ds(i * piece_rows, piece_rows), :]
+        here = part_of(buf, c, i)
         up, down = c + 1 < n.ctx, c > 0
         if to == "between":
             up, down = c + 1 < n.ctx - 1, c > 1
         elif to == "ends":
             up, down = c + 1 == n.ctx - 1, c == 1
-        send_if(up, piece, here, sem.at[0, 0, k], sem.at[2, c, k], right)
-        send_if(down, piece, here, sem.at[1, 0, k], sem.at[2, c, k], left)
+        send_if(up, piece, here, sem.at[0, 0, i], sem.at[2, c, i], right)
+        send_if(down, piece, here, sem.at[1, 0, i], sem.at[2, c, i], left)
 
     def gather_relay(buf, sem, by, k, source=None):
         low, high = jnp.maximum(c - by, 0), jnp.minimum(c + by, n.ctx - 1)
@@ -421,51 +428,62 @@
             from_low, from_high = c == by, c + by == n.ctx - 1
         elif source == "between":
             from_low, from_high = c > by, c + by < n.ctx - 1
-        piece, here = part_of(buf, low, k), sem.at[2, low, k]
-        pl.when(from_low)(functools.partial(arrived, piece, here))
-        send_if(from_low & (c + 1 < n.ctx), piece, piece, sem.at[0, by, k], here, right)
-        piece, here = part_of(buf, high, k), sem.at[2, high, k]
-        pl.when(from_high)(functools.partial(arrived, piece, here))
-        send_if(from_high & (c > 0), piece, piece, sem.at[1, by, k], here, left)
+        for i in pieces_of(k):
+            piece, here = part_of(buf, low, i), sem.at[2, low, i]
+            pl.when(from_low)(functools.partial(arrived, piece, here))
+            send_if(from_low & (c + 1 < n.ctx), piece, piece, sem.at[0, by, i], here, right)
+            piece, here = part_of(buf, high, i), sem.at[2, high, i]
+            pl.when(from_high)(functools.partial(arrived, piece, here))
+            send_if(from_high & (c > 0), piece, piece, sem.at[1, by, i], here, left)
 
     def rows_of(k):
         return slice(k * part_rows, (k + 1) * part_rows)
 
-    def scatter_send(cond, part, there, sem, target, k, way, to_c):
+    def scatter_send(cond, part, there, sem, target, i, way, to_c):
         send_if(
             cond,
-            part_of(part, target, k),
-            part_of(there, target, k),
-            sem.at[way, target, k],
-            sem.at[2 + way, target, k],
+            part_of(part, target, i),
+            part_of(there, target, i),
+            sem.at[way, target, i],
+            sem.at[2 + way, target, i],
             to_c,
         )
 
-    def scatter_add(part, there, sem, target, k, way):
-        arrived(part_of(there, target, k), sem.at[2 + way, target, k])
-        span = rows_of(k)
+    def scatter_add(part, there, sem, target, i, way):
+        arrived(part_of(there, target, i), sem.at[2 + way, target, i])
+        span = slice(i * piece_rows, (i + 1) * piece_rows)
         part[target, span, :] = (
             part[target, span, :].astype(F32) + there[target, span, :].astype(F32)
         ).astype(BF16)
 
     def scatter_start(g, k):
         for step in range(n.ctx - 1):
-            scatter_send(c == n.ctx - 1, g.part, g.high, g.sem, step, k, 1, left)
-            scatter_send(c == 0, g.part, g.low, g.sem, n.ctx - 1 - step, k, 0, right)
-
-    def scatter_relay(g, step, k):
-        near = c < n.ctx // 2
-        low, high = n.ctx - 1 - step, step
-        up, down = (c < low) & (c > 0), (c > high) & (c + 1 < n.ctx)
-
-        def go_up(cond):
-            pl.when(cond)(functools.partial(scatter_add, g.part, g.low, g.sem, low, k, 0))
-            scatter_send(cond, g.part, g.low, g.sem, low, k, 0, right)
-
-        go_up(up & near)
-        pl.when(down)(functools.partial(scatter_add, g.part, g.high, g.sem, high, k, 1))
-        scatter_send(down, g.part, g.high, g.sem, high, k, 1, left)
-        go_up(up & ~near)
+            for i in pieces_of(k):
+                scatter_send(c == n.ctx - 1, g.part, g.high, g.sem, step, i, 1, left)
+                scatter_send(c == 0, g.part, g.low, g.sem, n.ctx - 1 - step, i, 0, right)
+
+    def scatter_up(g, step, k, cond):
+        target = n.ctx - 1 - step
+        cond = cond & (c < target) & (c > 0)
+        for i in pieces_of(k):
+            pl.when(cond)(functools.partial(scatter_add, g.part, g.low, g.sem, target, i, 0))
+            scatter_send(cond, g.part, g.low, g.sem, target, i, 0, right)
+
+    def scatter_down(g, step, k, cond):
+        cond = cond & (c > step) & (c + 1 < n.ctx)
+        for i in pieces_of(k):
+            pl.when(cond)(functools.partial(scatter_add, g.part, g.high, g.sem, step, i, 1))
+            scatter_send(cond, g.part, g.high, g.sem, step, i, 1, left)
+
+    def scatter_near(g, k):
+        for step in range(n.ctx - 1):
+            scatter_up(g, step, k, c < n.ctx // 2)
+            scatter_down(g, step, k, c >= n.ctx // 2)
+
+    def scatter_far(g, k):
+        for step in range(n.ctx - 1):
+            scatter_up(g, step, k, c >= n.ctx // 2)
+            scatter_down(g, step, k, c < n.ctx // 2)
 
     def scatter_total(g, out, k):
         span = rows_of(k)
@@ -473,12 +491,14 @@
 
         @pl.when(c > 0)
         def _():
-            arrived(part_of(g.low, c, k), g.sem.at[2, c, k])
+            for i in pieces_of(k):
+                arrived(part_of(g.low, c, i), g.sem.at[2, c, i])
             out[span, :] = out[span, :] + g.low[c, span, :].astype(F32)
 
         @pl.when(c + 1 < n.ctx)
         def _():
-            arrived(part_of(g.high, c, k), g.sem.at[3, c, k])
+            for i in pieces_of(k):
+                arrived(part_of(g.high, c, i), g.sem.at[3, c, i])
             out[span, :] = out[span, :] + g.high[c, span, :].astype(F32)
 
     def block_of(buf, index, span):
@@ -602,10 +622,8 @@
 
     def small_peers(way):
         if way == "line":
-            return [(n.chips + by, f, ahead(by)) for by in range(1, n.ctx)]
-        if way == "plane":
-            return [(by, chip_ahead(by) * 2 + core, c) for by in range(1, n.chips)]
-        return [(0, sibling, c)]
+            return [(n.fsdp + by, f, ahead(by)) for by in range(1, n.ctx)]
+        return [(by, lax.rem(f + by, n.fsdp), c) for by in range(1, n.fsdp)]
 
     def small_send(src, incoming, sem, way):
         for slot, to_f, to_c in small_peers(way):
@@ -679,7 +697,7 @@
     own_attn = weights_own(attn_shards, attn_cols, r.wa, 0)
     own_mlp = weights_own(mlp_shards, mlp_cols, r.wm, 4)
     r.g0_acc[0] = small_sum(r.gp, r.g0_in, r.sem_g0, "line")
-    small_send(r.g0_acc.at[0], r.g0_in, r.sem_g0, "pair")
+    small_send(r.g0_acc.at[0], r.g0_in, r.sem_g0, "plane")
     slots = r.order.shape[1]
     slot_len = n.tokens // slots
     exponent = (lane % (HEAD_DIM // 2)).astype(F32) * (2.0 / HEAD_DIM)
@@ -698,11 +716,9 @@
     for j in range(slots):
         posk = posk + jnp.where(token // slot_len == j, r.order[0, j] * slot_len, 0)
     r.posk[...] = posk
-    r.g0_acc[1] = small_sum(r.g0_acc.at[0], r.g0_in, r.sem_g0, "pair")
-    small_send(r.g0_acc.at[1], r.g0_in, r.sem_g0, "plane")
     weights_spread(own_attn[:3], attn_cols[:3], r.sem_wa, plane_q)
     weights_spread(own_attn[3:], attn_cols[3:], r.sem_wa, plane_o)
-    r.g0_acc[2] = small_sum(r.g0_acc.at[1], r.g0_in, r.sem_g0, "plane")
+    r.g0_acc[2] = small_sum(r.g0_acc.at[0], r.g0_in, r.sem_g0, "plane")
     for j in range(n.lines):
         r.gv[0, :, j * HEAD_DIM : (j + 1) * HEAD_DIM] = r.g0_acc[2, j : j + 1, :]
         r.gv[1, :, j * HEAD_DIM : (j + 1) * HEAD_DIM] = r.g0_acc[
@@ -778,7 +794,6 @@
             out[:, :, at : at + step] = product.astype(BF16).reshape(n.ctx, rows, step)
 
     by_rows(r.at, lambda span: r.wa[span, o_at:], r.p_o)
-    steps = range(n.ctx - 1)
     for k in range(PARTS):
         scatter_start(sum_o, k)
     weights_spread(own_mlp, mlp_cols, r.sem_wm, plane_m)
@@ -792,15 +807,14 @@
         gather_start(r.mb.at[c], r.mb, r.sem_mb, k)
 
     gather_relay(r.gb, r.sem_gb, 1, 0)
-    for step in steps:
-        scatter_relay(sum_o, step, 0)
+    scatter_near(sum_o, 0)
+    scatter_far(sum_o, 0)
     for by in range(2, n.ctx - 1):
         gather_relay(r.gb, r.sem_gb, by, 0)
     residual(0)
-    for step in steps:
-        scatter_relay(sum_o, step, 1)
-        if step == 0:
-            gather_relay(r.mb, r.sem_mb, 1, 0, "between")
+    scatter_near(sum_o, 1)
+    gather_relay(r.mb, r.sem_mb, 1, 0, "between")
+    scatter_far(sum_o, 1)
     residual(1)
     gather_relay(r.mb, r.sem_mb, 1, 0, "end")
     gather_relay(r.mb, r.sem_mb, 1, 1, "between")
@@ -854,12 +868,11 @@
     mlp_part(0)
     gather_relay(r.mb, r.sem_mb, 1, 1, "end")
     gather_relay(r.gb, r.sem_gb, 1, 1)
-    for step in steps:
-        scatter_relay(sum_x2, step, 0)
-        if step == 0:
-            for by in range(2, n.ctx - 1):
-                gather_relay(r.mb, r.sem_mb, by, 1)
-                gather_relay(r.gb, r.sem_gb, by, 1)
+    for by in range(2, n.ctx - 1):
+        gather_relay(r.gb, r.sem_gb, by, 1)
+        gather_relay(r.mb, r.sem_mb, by, 1)
+    scatter_near(sum_x2, 0)
+    scatter_far(sum_x2, 0)
     gather_relay(r.mb, r.sem_mb, n.ctx - 1, 1)
     gather_relay(r.gb, r.sem_gb, n.ctx - 1, 1)
     mlp_part(1)
@@ -876,32 +889,29 @@
         part = r.hid[:, :, at : at + tile].reshape(n.tokens, tile)
         r.gm[:, 2 * ff + at : 2 * ff + at + tile] = mm(upstream, part, FIRST_AXIS).astype(BF16)
     grads_pair(group_m)
-    for step in steps:
-        scatter_relay(sum_x2, step, 1)
-        if step == 0:
-            gather_relay(r.rb, r.sem_rb, 1, 0, "between")
-            grads_plane(group_m)
-        elif step == 1:
-            gather_relay(r.rb, r.sem_rb, 1, 0, "end")
+    scatter_near(sum_x2, 1)
+    gather_relay(r.rb, r.sem_rb, 1, 0, "between")
+    grads_plane(group_m)
+    scatter_far(sum_x2, 1)
+    gather_relay(r.rb, r.sem_rb, 1, 0, "end")
     for by in range(2, n.ctx - 1):
         gather_relay(r.rb, r.sem_rb, by, 0)
     residual_back(1)
     scatter_start(sum_y, 1)
+    scatter_near(sum_y, 0)
     gather_relay(r.rb, r.sem_rb, 1, 1, "between")
     gather_relay(r.rb, r.sem_rb, 1, 1, "end")
     for by in range(2, n.ctx - 1):
         gather_relay(r.rb, r.sem_rb, by, 1)
-    for step in steps:
-        scatter_relay(sum_y, step, 0)
+    scatter_far(sum_y, 0)
     for k in range(PARTS):
         gather_relay(r.rb, r.sem_rb, n.ctx - 1, k)
 
     upstream = r.rb[...].reshape(n.tokens, d)
     for at in range(0, o_cols, HEAD_DIM):
         r.da[at // HEAD_DIM] = mm(upstream, r.wa[:, o_at + at : o_at + at + HEAD_DIM])
-    r.ga[:, o_at:] = mm(upstream, r.at[...], FIRST_AXIS).astype(BF16)
-    grads_pair(group_o)
     grads_line(group_m)
+    scatter_near(sum_y, 1)
     r.dk[...] = jnp.zeros_like(r.dk)
     r.dv[...] = jnp.zeros_like(r.dv)
 
@@ -935,7 +945,6 @@
         return term + jnp.sum(gain_term, axis=0, keepdims=True)
 
     q_term = lax.fori_loop(0, n.heads, query_backward, jnp.zeros((1, HEAD_DIM), F32))
-    grads_plane(group_o)
     k_term = jnp.zeros((1, HEAD_DIM), F32)
     for kv in range(n.kv):
         u = r.kp[kv]
@@ -947,23 +956,25 @@
         at += k_cols
         r.dqkv[:, at : at + HEAD_DIM] = r.dv[kv].astype(BF16)
         k_term = k_term + jnp.sum(gain_term, axis=0, keepdims=True)
+    by_rows(r.dqkv, lambda span: r.wa[span, :o_at], r.p_x1)
+    for k in range(PARTS):
+        scatter_start(sum_x1, k)
     for at in range(0, o_at, 2 * HEAD_DIM):
         r.ga[:, at : at + 2 * HEAD_DIM] = mm(
             r.xn[...], r.dqkv[:, at : at + 2 * HEAD_DIM], FIRST_AXIS
         ).astype(BF16)
     grads_pair(group_q)
-    by_rows(r.dqkv, lambda span: r.wa[span, :o_at], r.p_x1)
-    for k in range(PARTS):
-        scatter_start(sum_x1, k)
-    for step in steps:
-        scatter_relay(sum_y, step, 1)
+    r.ga[:, o_at:] = mm(upstream, r.at[...], FIRST_AXIS).astype(BF16)
+    grads_pair(group_o)
     grads_plane(group_q)
+    grads_plane(group_o)
+    scatter_near(sum_x1, 0)
+    scatter_far(sum_y, 1)
+    scatter_far(sum_x1, 0)
+    scatter_near(sum_x1, 1)
+    scatter_far(sum_x1, 1)
+    grads_line(group_q)
     grads_line(group_o)
-    for k in range(PARTS):
-        for step in steps:
-            scatter_relay(sum_x1, step, k)
-        if k == 0:
-            grads_line(group_q)
     for k in range(PARTS):
         scatter_total(sum_y, r.ho, k)
     r.out_hidden[...] = r.ho[...].astype(BF16)
@@ -976,10 +987,8 @@
     r.out_input[...] = r.dh[...] + from_norm
     r.g1_acc[3, 2 * n.lines : 2 * n.lines + 1, :] = q_term
     r.g1_acc[3, 2 * n.lines + 1 : 2 * n.lines + 2, :] = k_term
-    small_send(r.g1_acc.at[3], r.g1_in, r.sem_g1, "pair")
-    r.g1_acc[0] = small_sum(r.g1_acc.at[3], r.g1_in, r.sem_g1, "pair")
-    small_send(r.g1_acc.at[0], r.g1_in, r.sem_g1, "plane")
-    r.g1_acc[1] = small_sum(r.g1_acc.at[0], r.g1_in, r.sem_g1, "plane")
+    small_send(r.g1_acc.at[3], r.g1_in, r.sem_g1, "plane")
+    r.g1_acc[1] = small_sum(r.g1_acc.at[3], r.g1_in, r.sem_g1, "plane")
     small_send(r.g1_acc.at[1], r.g1_in, r.sem_g1, "line")
     grads_wait(group_m)
     grads_wait(group_o)

time: 197 us -> 184 us (0.934)
  Pallas kernels: 193 us -> 180 us
    pallas_call x1, Pallas kernels: 190 us -> 177 us  [fused(): pl.pallas_call(functools.partial(layer_kernel, n, [*inputs, *outputs, *sc...]
where the time goes in v5:
time: 184 us
  Pallas kernels  180 us (98%)
  local copies, waits for them, and re-layouts  2.38 us (1%)
    pallas_call x1, Pallas kernels, fused(): pl.pallas_call(functools.partial(layer_kernel, n, [*inputs, *outputs, *sc...  177 us

profile of v5, /device:TPU:0, one launch (start us, length us, event | category | flops | bytes accessed | tf_op | source)
XLA Modules:
  0.0 183.5 jit_solution(179075295285192240)
XLA Ops:
  0.6 0.0 copy-start.4
  0.7 0.0 copy-start.1
  0.7 0.0 copy-start.2
  0.7 0.0 copy-start.3
  0.7 0.6 copy-done.4
  1.3 0.0 copy-done.1
  1.3 0.0 copy-done.2
  1.3 0.0 copy-done.3
  1.3 0.6 fusion.1.refs_9_
  1.9 176.9 %layer.1 = (bf16[128,1024]{1,0:T(8,128)(2,1)}, f32[128,1024]{1,0:T(8,128)}, bf16[4,32,1536]{2,1,0:T(8,128)(2,1)}, bf16[4,32,2304]{2,1,0:T(8,128)(2,1)}, f32[24,128]{1,0:T(8,128)}) custom-call(bf16[128,1024]{1,0:T(8,128)(2,1)} %bitcast.17, bf16[128,1024]{1,0:T(8,128)(2,1)} %bitcast.18, bf16[32,2048]{1,0:T(8,128)(2,1)} %refs_2_.1, bf16[32,1024]{1,0:T(8,128)(2,1)} %refs_3_.1, ...), custom_call_target="tpu_custom_call" | custom-call | tf_op jit(solution)/shard_map/layer/pallas_call | solution.py:1045
  178.8 3.0 %emit.1 = (bf16[128,1024]{1,0:T(8,128)(2,1)}, f32[128,1024]{1,0:T(8,128)}, f32[32,2048]{1,0:T(8,128)}, f32[32,1024]{1,0:T(8,128)}, f32[32,1024]{1,0:T(8,128)}, /...) custom-call(bf16[128,1024]{1,0:T(8,128)(2,1)} %get-tuple-element.28.r, ...), custom_call_target="tpu_custom_call" | custom-call | tf_op jit(solution)/shard_map/emit/pallas_call | solution.py:1059
  181.8 0.0 copy-start
  181.8 0.7 copy-done
  182.5 0.5 slice_bitcast_fusion.1
  183.0 0.5 slice_bitcast_fusion
Async XLA Ops:
  0.6 0.7 copy-start.4
  0.7 0.7 copy-start.1
  0.7 0.7 copy-start.2
  0.7 0.7 copy-start.3
  181.8 0.7 copy-start

commit v6 on v5

--- a/solution.py
+++ b/solution.py
@@ -321,25 +321,28 @@
         out["p_" + name] = bf(c, n.rows, d)
         out["l_" + name] = bf(c, n.rows, d)
         out["r_" + name] = bf(c, n.rows, d)
-        out["sem_" + name] = sem(4, c, PARTS * PIECES)
+        out["snd_" + name] = sem(2, c - 1)
+        out["rcv_" + name] = sem(2, c - 1, PARTS * PIECES)
     for name in ("xb", "gb", "mb", "rb"):
-        out["sem_" + name] = sem(3, c, PARTS * PIECES)
-    out["sem_wa"] = sem(2, c - 1, 4)
-    out["sem_wm"] = sem(2, c - 1, 3)
+        out["snd_" + name] = sem(2, c - 1)
+        out["rcv_" + name] = sem(c, PARTS * PIECES)
+    out["snd_w"] = sem(2, c - 1)
+    out["rcv_w"] = sem(3, c - 1)
     for name in ("pq", "po", "pm"):
-        out["sem_" + name] = sem(4, n.chips)
+        out["sem_" + name] = sem(3 + n.chips)
     for name in ("gm", "go", "gq"):
-        out["sem_" + name] = sem(4, n.chips)
-        out["sem_z" + name] = sem(2, c)
+        out["sem_" + name] = sem(5 + n.chips)
     for name in ("g0", "g1"):
         out[name + "_in"] = f32(n.fsdp + c, n.gain_rows, HEAD_DIM)
         out[name + "_acc"] = f32(4, n.gain_rows, HEAD_DIM)
-        out["sem_" + name] = sem(2, n.fsdp + c)
+        out["sem_" + name] = sem(4)
     return out
 
 
 def layer_kernel(n, names, *refs):
     r = types.SimpleNamespace(**dict(zip(names, refs)))
+    for name in ("o", "y", "x2", "x1", "xb", "gb", "mb", "rb"):
+        setattr(r, "sem_" + name, (getattr(r, "snd_" + name), getattr(r, "rcv_" + name)))
     c, f = lax.axis_index("ctx"), lax.axis_index("fsdp")
     chip, core = f // 2, f % 2
     sibling = chip * 2 + 1 - core
@@ -369,17 +372,17 @@
         )
 
     def send(src, dst, send_sem, recv_sem, to_f=None, to_c=None):
-        copy = remote(src, dst, send_sem, recv_sem, to_f, to_c)
-        copy.start()
-        sends.append(copy.wait_send)
+        remote(src, dst, send_sem, recv_sem, to_f, to_c).start()
+
+    def sent(like, send_sem, cond=None):
+        wait = remote(like, like, send_sem, send_sem).wait_send
+        sends.append(wait if cond is None else (lambda: pl.when(cond)(wait)))
 
     def arrived(dst, recv_sem):
         remote(dst, dst, recv_sem, recv_sem).wait_recv()
 
     def send_if(cond, src, dst, send_sem, recv_sem, to_c):
-        copy = remote(src, dst, send_sem, recv_sem, None, to_c)
-        pl.when(cond)(copy.start)
-        sends.append(lambda: pl.when(cond)(copy.wait_send))
+        pl.when(cond)(remote(src, dst, send_sem, recv_sem, None, to_c).start)
 
     barrier = pltpu.get_barrier_semaphore()
 
@@ -418,8 +421,8 @@
             up, down = c + 1 < n.ctx - 1, c > 1
         elif to == "ends":
             up, down = c + 1 == n.ctx - 1, c == 1
-        send_if(up, piece, here, sem.at[0, 0, i], sem.at[2, c, i], right)
-        send_if(down, piece, here, sem.at[1, 0, i], sem.at[2, c, i], left)
+        send_if(up, piece, here, sem[0].at[0, 0], sem[1].at[c, i], right)
+        send_if(down, piece, here, sem[0].at[1, 0], sem[1].at[c, i], left)
 
     def gather_relay(buf, sem, by, k, source=None):
         low, high = jnp.maximum(c - by, 0), jnp.minimum(c + by, n.ctx - 1)
@@ -429,12 +432,17 @@
         elif source == "between":
             from_low, from_high = c > by, c + by < n.ctx - 1
         for i in pieces_of(k):
-            piece, here = part_of(buf, low, i), sem.at[2, low, i]
+            piece, here = part_of(buf, low, i), sem[1].at[low, i]
             pl.when(from_low)(functools.partial(arrived, piece, here))
-            send_if(from_low & (c + 1 < n.ctx), piece, piece, sem.at[0, by, i], here, right)
-            piece, here = part_of(buf, high, i), sem.at[2, high, i]
+            send_if(from_low & (c + 1 < n.ctx), piece, piece, sem[0].at[0, by], here, right)
+            piece, here = part_of(buf, high, i), sem[1].at[high, i]
             pl.when(from_high)(functools.partial(arrived, piece, here))
-            send_if(from_high & (c > 0), piece, piece, sem.at[1, by, i], here, left)
+            send_if(from_high & (c > 0), piece, piece, sem[0].at[1, by], here, left)
+
+    def gather_sent(buf, sem):
+        for by in range(n.ctx - 1):
+            sent(buf.at[0], sem[0].at[0, by], (c - by >= 0) & (c + 1 < n.ctx))
+            sent(buf.at[0], sem[0].at[1, by], (c + by < n.ctx) & (c > 0))
 
     def rows_of(k):
         return slice(k * part_rows, (k + 1) * part_rows)
@@ -444,13 +452,13 @@
             cond,
             part_of(part, target, i),
             part_of(there, target, i),
-            sem.at[way, target, i],
-            sem.at[2 + way, target, i],
+            sem[0].at[way, target - 1 + way],
+            sem[1].at[way, target - 1 + way, i],
             to_c,
         )
 
     def scatter_add(part, there, sem, target, i, way):
-        arrived(part_of(there, target, i), sem.at[2 + way, target, i])
+        arrived(part_of(there, target, i), sem[1].at[way, target - 1 + way, i])
         span = slice(i * piece_rows, (i + 1) * piece_rows)
         part[target, span, :] = (
             part[target, span, :].astype(F32) + there[target, span, :].astype(F32)
@@ -485,6 +493,12 @@
             scatter_up(g, step, k, c >= n.ctx // 2)
             scatter_down(g, step, k, c < n.ctx // 2)
 
+    def scatter_sent(g):
+        for target in range(1, n.ctx):
+            sent(g.part.at[0], g.sem[0].at[0, target - 1], c < target)
+        for target in range(n.ctx - 1):
+            sent(g.part.at[0], g.sem[0].at[1, target], c > target)
+
     def scatter_total(g, out, k):
         span = rows_of(k)
         out[span, :] = out[span, :] + g.part[c, span, :].astype(F32)
@@ -492,43 +506,48 @@
         @pl.when(c > 0)
         def _():
             for i in pieces_of(k):
-                arrived(part_of(g.low, c, i), g.sem.at[2, c, i])
+                arrived(part_of(g.low, c, i), g.sem[1].at[0, jnp.maximum(c - 1, 0), i])
             out[span, :] = out[span, :] + g.low[c, span, :].astype(F32)
 
         @pl.when(c + 1 < n.ctx)
         def _():
             for i in pieces_of(k):
-                arrived(part_of(g.high, c, i), g.sem.at[3, c, i])
+                arrived(part_of(g.high, c, i), g.sem[1].at[1, jnp.minimum(c, n.ctx - 2), i])
             out[span, :] = out[span, :] + g.high[c, span, :].astype(F32)
 
     def block_of(buf, index, span):
         return buf.at[pl.ds(pl.multiple_of(index * block, block), block), pl.ds(*span)]
+
+    def blocks_of(buf, count, span):
+        return buf.at[pl.ds(0, count * block), pl.ds(*span)]
 
     def piece_of(buf, line, at, width):
         start = pl.multiple_of(f * block + line * shard, shard)
         return buf.at[pl.ds(start, shard), pl.ds(at, width)]
 
-    def weights_send(shards, cols, buf, sem, now=None):
+    def weights_send(shards, cols, buf, send_sem, recv_sems, now=None):
         for by in range(1, n.ctx):
+            at_end = (ahead(by) == 0) | (ahead(by) == n.ctx - 1)
             at = 0
-            for i, (src, width) in enumerate(zip(shards, cols)):
+            for src, width, recv_sem in zip(shards, cols, recv_sems):
                 column = pl.multiple_of(ahead(by) * width, HEAD_DIM)
                 copy = remote(
                     src.at[:, pl.ds(column, width)],
                     piece_of(buf, c, at, width),
-                    sem.at[0, by - 1, i],
-                    sem.at[1, by - 1, i],
+                    send_sem.at[by - 1],
+                    recv_sem.at[by - 1],
                     None,
                     ahead(by),
                 )
-                at_end = (ahead(by) == 0) | (ahead(by) == n.ctx - 1)
                 if now is None:
                     copy.start()
                 else:
                     pl.when(at_end if now == "ends" else ~at_end)(copy.start)
-                if now != "ends":
-                    sends.append(copy.wait_send)
                 at += width
+
+    def weights_sent(cols, buf, send_sem):
+        for by in range(1, n.ctx):
+            sent(piece_of(buf, c, 0, sum(cols)), send_sem.at[by - 1])
 
     def weights_own(shards, cols, buf, first):
         at, out = 0, []
@@ -544,28 +563,26 @@
             at += width
         return out
 
-    def weights_spread(own, cols, sem, g):
+    def weights_spread(own, g):
         for copy in own:
             copy.wait()
         for by in range(1, n.ctx):
-            at = g.span[0]
-            for i, width in enumerate(cols):
-                arrived(piece_of(g.buf, behind(by), at, width), sem.at[1, by - 1, g.first + i])
-                at += width
+            arrived(piece_of(g.buf, behind(by), *g.span), g.line.at[by - 1])
         mine = block_of(g.buf, f, g.span)
         for by in range(1, n.chips):
-            send(mine, mine, g.sem.at[0, by], g.sem.at[1, by], chip_ahead(by) * 2 + core)
-        send(mine, mine, g.sem.at[2, 0], g.sem.at[3, 0], sibling)
+            send(mine, mine, g.sem.at[0], g.sem.at[2 + by], chip_ahead(by) * 2 + core)
+        send(mine, mine, g.sem.at[1], g.sem.at[2], sibling)
 
     def weights_forward(g):
         for by in range(1, n.chips):
             piece = block_of(g.buf, chip_behind(by) * 2 + core, g.span)
-            arrived(piece, g.sem.at[1, by])
-            send(piece, piece, g.sem.at[2, by], g.sem.at[3, by], sibling)
+            arrived(piece, g.sem.at[2 + by])
+            send(piece, piece, g.sem.at[1], g.sem.at[2], sibling)
+        sent(blocks_of(g.buf, n.chips - 1, g.span), g.sem.at[0])
+        sent(blocks_of(g.buf, n.chips, g.span), g.sem.at[1])
 
     def weights_wait(g):
-        for by in range(n.chips):
-            arrived(block_of(g.buf, chip_behind(by) * 2 + 1 - core, g.span), g.sem.at[3, by])
+        arrived(blocks_of(g.buf, n.chips, g.span), g.sem.at[2])
 
     def share_of(buf, index, span):
         return buf.at[pl.ds(pl.multiple_of(index * block, block), block), pl.ds(*span)]
@@ -575,64 +592,71 @@
             send(
                 share_of(g.whole, chip_ahead(by) * 2 + 1 - core, g.span),
                 g.pair.at[by, :, pl.ds(*g.span)],
-                g.sem.at[0, by],
-                g.sem.at[1, by],
+                g.sem.at[0],
+                g.sem.at[5 + by],
                 sibling,
             )
+        sent(g.pair.at[:, :, pl.ds(*g.span)], g.sem.at[0])
 
     def grads_plane(g):
         for by in range(1, n.chips):
             theirs = g.pair.at[by, :, pl.ds(*g.span)]
-            arrived(theirs, g.sem.at[1, by])
+            arrived(theirs, g.sem.at[5 + by])
             piece = share_of(g.whole, chip_ahead(by) * 2 + core, g.span)
             piece[...] = (piece[...].astype(F32) + theirs[...].astype(F32)).astype(BF16)
             send(
                 piece,
                 g.plane.at[by - 1, :, pl.ds(*g.span)],
-                g.sem.at[2, by],
-                g.sem.at[3, by],
+                g.sem.at[1],
+                g.sem.at[2],
                 chip_ahead(by) * 2 + core,
             )
+        sent(g.plane.at[:, :, pl.ds(*g.span)], g.sem.at[1])
 
     def grads_line(g):
         theirs = g.pair.at[0, :, pl.ds(*g.span)]
-        arrived(theirs, g.sem.at[1, 0])
+        arrived(theirs, g.sem.at[5])
         acc = share_of(g.whole, f, g.span)[...].astype(F32) + theirs[...].astype(F32)
+        arrived(g.plane.at[:, :, pl.ds(*g.span)], g.sem.at[2])
         for by in range(1, n.chips):
-            theirs = g.plane.at[by - 1, :, pl.ds(*g.span)]
-            arrived(theirs, g.sem.at[3, by])
-            acc = acc + theirs[...].astype(F32)
+            acc = acc + g.plane[by - 1, :, pl.ds(*g.span)].astype(F32)
         g.total[:, pl.ds(*g.span)] = acc.astype(BF16)
         for by in range(1, n.ctx):
             start = pl.multiple_of(ahead(by) * shard, shard)
             send(
                 g.total.at[pl.ds(start, shard), pl.ds(*g.span)],
                 g.land.at[c, :, pl.ds(*g.span)],
-                g.line_sem.at[0, by],
-                g.line_sem.at[1, by],
+                g.sem.at[3],
+                g.sem.at[4],
                 None,
                 ahead(by),
             )
+        sent(g.land.at[pl.ds(0, n.ctx - 1), :, pl.ds(*g.span)], g.sem.at[3])
         start = pl.multiple_of(c * shard, shard)
         g.land[c, :, pl.ds(*g.span)] = g.total[pl.ds(start, shard), pl.ds(*g.span)]
 
     def grads_wait(g):
-        for by in range(1, n.ctx):
-            arrived(g.land.at[behind(by), :, pl.ds(*g.span)], g.line_sem.at[1, by])
+        arrived(g.land.at[pl.ds(0, n.ctx - 1), :, pl.ds(*g.span)], g.sem.at[4])
 
     def small_peers(way):
         if way == "line":
-            return [(n.fsdp + by, f, ahead(by)) for by in range(1, n.ctx)]
-        return [(by, lax.rem(f + by, n.fsdp), c) for by in range(1, n.fsdp)]
+            return [(n.fsdp + by - 1, f, ahead(by)) for by in range(1, n.ctx)]
+        return [(by - 1, lax.rem(f + by, n.fsdp), c) for by in range(1, n.fsdp)]
+
+    def small_span(incoming, way):
+        first, count = (n.fsdp, n.ctx - 1) if way == "line" else (0, n.fsdp - 1)
+        return incoming.at[pl.ds(first, count)]
 
     def small_send(src, incoming, sem, way):
+        at = 2 * (way == "line")
         for slot, to_f, to_c in small_peers(way):
-            send(src, incoming.at[slot], sem.at[0, slot], sem.at[1, slot], to_f, to_c)
+            send(src, incoming.at[slot], sem.at[at], sem.at[at + 1], to_f, to_c)
+        sent(small_span(incoming, way), sem.at[at])
 
     def small_sum(own, incoming, sem, way):
         total = own[...]
+        arrived(small_span(incoming, way), sem.at[2 * (way == "line") + 1])
         for slot, _, _ in small_peers(way):
-            arrived(incoming.at[slot], sem.at[1, slot])
             total = total + incoming[slot]
         return total
 
@@ -651,16 +675,19 @@
     o_at = q_cols + 2 * k_cols
     attn_bufs = dict(whole=r.ga, pair=r.ga_sib, plane=r.ga_in, total=r.ga_z, land=r.ga_land)
     mlp_bufs = dict(whole=r.gm, pair=r.gm_sib, plane=r.gm_in, total=r.gm_z, land=r.gm_land)
-    plane_q = types.SimpleNamespace(buf=r.wa, span=(0, o_at), first=0, sem=r.sem_pq)
-    plane_o = types.SimpleNamespace(buf=r.wa, span=(o_at, o_cols), first=3, sem=r.sem_po)
-    plane_m = types.SimpleNamespace(buf=r.wm, span=(0, n.mlp_cols), first=0, sem=r.sem_pm)
+    line_q, line_o, line_m = (r.rcv_w.at[i] for i in range(3))
+    plane_q = types.SimpleNamespace(buf=r.wa, span=(0, o_at), line=line_q, sem=r.sem_pq)
+    plane_o = types.SimpleNamespace(buf=r.wa, span=(o_at, o_cols), line=line_o, sem=r.sem_po)
+    plane_m = types.SimpleNamespace(buf=r.wm, span=(0, n.mlp_cols), line=line_m, sem=r.sem_pm)
+    to_attn = (r.wa, r.snd_w.at[0], (line_q, line_q, line_q, line_o))
+    to_mlp = (r.wm, r.snd_w.at[1], (line_m, line_m, line_m))
     group_m = types.SimpleNamespace(
-        **mlp_bufs, span=(0, n.mlp_cols), sem=r.sem_gm, line_sem=r.sem_zgm
+        **mlp_bufs, span=(0, n.mlp_cols), sem=r.sem_gm
     )
     group_o = types.SimpleNamespace(
-        **attn_bufs, span=(o_at, o_cols), sem=r.sem_go, line_sem=r.sem_zgo
-    )
-    group_q = types.SimpleNamespace(**attn_bufs, span=(0, o_at), sem=r.sem_gq, line_sem=r.sem_zgq)
+        **attn_bufs, span=(o_at, o_cols), sem=r.sem_go
+    )
+    group_q = types.SimpleNamespace(**attn_bufs, span=(0, o_at), sem=r.sem_gq)
 
     sum_o, sum_y, sum_x2, sum_x1 = (
         types.SimpleNamespace(part=part, low=low, high=high, sem=sem)
@@ -687,7 +714,7 @@
     place(2 * n.lines, me * n.few, n.few, 2 * n.each)
     place(2 * n.lines + 1, me * n.few, n.few, 2 * n.each + n.few)
     small_send(r.gp, r.g0_in, r.sem_g0, "line")
-    weights_send(attn_shards, attn_cols, r.wa, r.sem_wa)
+    weights_send(attn_shards, attn_cols, *to_attn)
     for k in range(PARTS):
         gather_start(r.hidden, r.xb, r.sem_xb, k)
     own_x = pltpu.make_async_copy(r.hidden, r.xb.at[c], r.local_sem.at[7])
@@ -716,8 +743,8 @@
     for j in range(slots):
         posk = posk + jnp.where(token // slot_len == j, r.order[0, j] * slot_len, 0)
     r.posk[...] = posk
-    weights_spread(own_attn[:3], attn_cols[:3], r.sem_wa, plane_q)
-    weights_spread(own_attn[3:], attn_cols[3:], r.sem_wa, plane_o)
+    weights_spread(own_attn[:3], plane_q)
+    weights_spread(own_attn[3:], plane_o)
     r.g0_acc[2] = small_sum(r.g0_acc.at[0], r.g0_in, r.sem_g0, "plane")
     for j in range(n.lines):
         r.gv[0, :, j * HEAD_DIM : (j + 1) * HEAD_DIM] = r.g0_acc[2, j : j + 1, :]
@@ -729,7 +756,7 @@
     attn_gain, mlp_gain = r.gv[0], r.gv[1]
     for by in range(1, n.ctx):
         if by == n.ctx - 1:
-            weights_send(mlp_shards, mlp_cols, r.wm, r.sem_wm, "between")
+            weights_send(mlp_shards, mlp_cols, *to_mlp, "between")
             for k in range(PARTS):
                 gather_start(r.cot, r.gb, r.sem_gb, k, "between")
         for k in range(PARTS):
@@ -746,7 +773,7 @@
     lax.fori_loop(0, n.ctx, norm_rows, 0)
     weights_forward(plane_q)
     weights_wait(plane_q)
-    weights_send(mlp_shards, mlp_cols, r.wm, r.sem_wm, "ends")
+    weights_send(mlp_shards, mlp_cols, *to_mlp, "ends")
     for k in range(PARTS):
         gather_start(r.cot, r.gb, r.sem_gb, k, "ends")
 
@@ -796,7 +823,7 @@
     by_rows(r.at, lambda span: r.wa[span, o_at:], r.p_o)
     for k in range(PARTS):
         scatter_start(sum_o, k)
-    weights_spread(own_mlp, mlp_cols, r.sem_wm, plane_m)
+    weights_spread(own_mlp, plane_m)
 
     def residual(k):
         span = rows_of(k)
@@ -994,6 +1021,12 @@
     grads_wait(group_o)
     grads_wait(group_q)
     r.out_gains[...] = small_sum(r.g1_acc.at[1], r.g1_in, r.sem_g1, "line")
+    for buf, sem in ((r.xb, r.sem_xb), (r.gb, r.sem_gb), (r.mb, r.sem_mb), (r.rb, r.sem_rb)):
+        gather_sent(buf, sem)
+    for g in (sum_o, sum_y, sum_x2, sum_x1):
+        scatter_sent(g)
+    weights_sent(attn_cols, *to_attn[:2])
+    weights_sent(mlp_cols, *to_mlp[:2])
     for wait in sends:
         wait()
 

time: 184 us -> 180 us (0.978)
  Pallas kernels: 180 us -> 176 us
    pallas_call x1, Pallas kernels: 177 us -> 173 us  [fused(): pl.pallas_call(functools.partial(layer_kernel, n, [*inputs, *outputs, *sc...]
where the time goes in v6:
time: 180 us; the launch traced here: 179 us
  Pallas kernels  176 us (98%)
  local copies, waits for them, and re-layouts  2.38 us (1%)
    pallas_call x1, Pallas kernels, fused(): pl.pallas_call(functools.partial(layer_kernel, n, [*inputs, *outputs, *sc...  173 us

profile of v6, /device:TPU:0, one launch (start us, length us, event | category | flops | bytes accessed | tf_op | source)
XLA Modules:
  0.0 179.5 jit_solution(17494540380387085108)
XLA Ops:
  0.6 0.0 copy-start.4
  0.7 0.0 copy-start.1
  0.7 0.0 copy-start.2
  0.7 0.0 copy-start.3
  0.7 0.6 copy-done.4
  1.3 0.0 copy-done.1
  1.3 0.0 copy-done.2
  1.3 0.0 copy-done.3
  1.3 0.6 fusion.1.refs_9_
  1.9 172.8 %layer.1 = (bf16[128,1024]{1,0:T(8,128)(2,1)}, f32[128,1024]{1,0:T(8,128)}, bf16[4,32,1536]{2,1,0:T(8,128)(2,1)}, bf16[4,32,2304]{2,1,0:T(8,128)(2,1)}, f32[24,128]{1,0:T(8,128)}) custom-call(bf16[128,1024]{1,0:T(8,128)(2,1)} %bitcast.17, bf16[128,1024]{1,0:T(8,128)(2,1)} %bitcast.18, bf16[32,2048]{1,0:T(8,128)(2,1)} %refs_2_.1, bf16[32,1024]{1,0:T(8,128)(2,1)} %refs_3_.1, ...), custom_call_target="tpu_custom_call" | custom-call | tf_op jit(solution)/shard_map/layer/pallas_call | solution.py:1078
  174.8 3.0 %emit.1 = (bf16[128,1024]{1,0:T(8,128)(2,1)}, f32[128,1024]{1,0:T(8,128)}, f32[32,2048]{1,0:T(8,128)}, f32[32,1024]{1,0:T(8,128)}, f32[32,1024]{1,0:T(8,128)}, /...) custom-call(bf16[128,1024]{1,0:T(8,128)(2,1)} %get-tuple-element.28.r, ...), custom_call_target="tpu_custom_call" | custom-call | tf_op jit(solution)/shard_map/emit/pallas_call | solution.py:1092
  177.8 0.0 copy-start
  177.8 0.7 copy-done
  178.4 0.5 slice_bitcast_fusion.1
  178.9 0.5 slice_bitcast_fusion
Async XLA Ops:
  0.6 0.7 copy-start.4
  0.7 0.7 copy-start.1
  0.7 0.7 copy-start.2
  0.7 0.7 copy-start.3
  177.8 0.7 copy-start

commit v7 on v6

--- a/solution.py
+++ b/solution.py
@@ -938,6 +938,8 @@
     for at in range(0, o_cols, HEAD_DIM):
         r.da[at // HEAD_DIM] = mm(upstream, r.wa[:, o_at + at : o_at + at + HEAD_DIM])
     grads_line(group_m)
+    r.ga[:, o_at:] = mm(upstream, r.at[...], FIRST_AXIS).astype(BF16)
+    grads_pair(group_o)
     scatter_near(sum_y, 1)
     r.dk[...] = jnp.zeros_like(r.dk)
     r.dv[...] = jnp.zeros_like(r.dv)
@@ -972,6 +974,7 @@
         return term + jnp.sum(gain_term, axis=0, keepdims=True)
 
     q_term = lax.fori_loop(0, n.heads, query_backward, jnp.zeros((1, HEAD_DIM), F32))
+    grads_plane(group_o)
     k_term = jnp.zeros((1, HEAD_DIM), F32)
     for kv in range(n.kv):
         u = r.kp[kv]
@@ -991,17 +994,23 @@
             r.xn[...], r.dqkv[:, at : at + 2 * HEAD_DIM], FIRST_AXIS
         ).astype(BF16)
     grads_pair(group_q)
-    r.ga[:, o_at:] = mm(upstream, r.at[...], FIRST_AXIS).astype(BF16)
-    grads_pair(group_o)
+    for j in range(n.ctx):
+        x = r.xb[j].astype(F32)
+        share = r.p_x1[j].astype(F32) * (x * rms(x))
+        save_lines(0, jnp.sum(share, axis=0, keepdims=True))
+    r.g1_acc[3, 2 * n.lines : 2 * n.lines + 1, :] = q_term
+    r.g1_acc[3, 2 * n.lines + 1 : 2 * n.lines + 2, :] = k_term
+    small_send(r.g1_acc.at[3], r.g1_in, r.sem_g1, "plane")
     grads_plane(group_q)
-    grads_plane(group_o)
     scatter_near(sum_x1, 0)
     scatter_far(sum_y, 1)
     scatter_far(sum_x1, 0)
+    grads_line(group_o)
+    r.g1_acc[1] = small_sum(r.g1_acc.at[3], r.g1_in, r.sem_g1, "plane")
+    small_send(r.g1_acc.at[1], r.g1_in, r.sem_g1, "line")
     scatter_near(sum_x1, 1)
+    grads_line(group_q)
     scatter_far(sum_x1, 1)
-    grads_line(group_q)
-    grads_line(group_o)
     for k in range(PARTS):
         scatter_total(sum_y, r.ho, k)
     r.out_hidden[...] = r.ho[...].astype(BF16)
@@ -1009,14 +1018,8 @@
     for k in range(PARTS):
         scatter_total(sum_x1, r.out_input, k)
     x = r.xb[c].astype(F32)
-    from_norm, term = norm_back(x, rms(x), attn_gain, r.out_input[...])
-    save_lines(0, jnp.sum(term, axis=0, keepdims=True))
+    from_norm, _ = norm_back(x, rms(x), attn_gain, r.out_input[...])
     r.out_input[...] = r.dh[...] + from_norm
-    r.g1_acc[3, 2 * n.lines : 2 * n.lines + 1, :] = q_term
-    r.g1_acc[3, 2 * n.lines + 1 : 2 * n.lines + 2, :] = k_term
-    small_send(r.g1_acc.at[3], r.g1_in, r.sem_g1, "plane")
-    r.g1_acc[1] = small_sum(r.g1_acc.at[3], r.g1_in, r.sem_g1, "plane")
-    small_send(r.g1_acc.at[1], r.g1_in, r.sem_g1, "line")
     grads_wait(group_m)
     grads_wait(group_o)
     grads_wait(group_q)
@@ -1088,8 +1091,9 @@
     )(*[value for value, _ in inputs.values()])
 
     finals = [(n.rows, n.width, BF16), (n.rows, n.width, F32)]
-    finals += [(s.shape[0], s.shape[1], F32) for s in shards] + [(8, HEAD_DIM, F32)]
-    result, input_grad, oq, ok, ov, oo, og, ou, od, sums = pl.pallas_call(
+    finals += [(*s.shape, F32) for s in shards]
+    finals += [(1, size, F32) for size in (n.each, n.each, n.few, n.few)]
+    result, input_grad, oq, ok, ov, oo, og, ou, od, *gains = pl.pallas_call(
         functools.partial(emit_kernel, n),
         out_shape=tuple(jax.ShapeDtypeStruct(f[:2], f[2]) for f in finals),
         in_specs=[vmem] * len(outputs),
@@ -1103,10 +1107,10 @@
         ok,
         ov,
         oo,
-        sums[0, : n.each],
-        sums[2, : n.few],
-        sums[3, : n.few],
-        sums[1, : n.each],
+        gains[0].reshape(n.each),
+        gains[2].reshape(n.few),
+        gains[3].reshape(n.few),
+        gains[1].reshape(n.each),
         og,
         ou,
         od,
@@ -1128,18 +1132,17 @@
             which += 1
     me = lax.axis_index("fsdp") * n.ctx + lax.axis_index("ctx")
     row, at = me * n.each // HEAD_DIM, lax.rem(me * n.each, HEAD_DIM)
-    sums_out = outs[which]
-    sums_out[...] = jnp.zeros_like(sums_out)
-    for i, (line, lane) in enumerate(
+    for out, (line, lane) in zip(
+        outs[which:],
         (
             (row, at),
             (n.lines + row, at),
             (2 * n.lines, me * n.few),
             (2 * n.lines + 1, me * n.few),
-        )
+        ),
     ):
         back = lax.rem(HEAD_DIM - lane, HEAD_DIM)
-        sums_out[i : i + 1, :] = pltpu.roll(sums[pl.ds(line, 1), :], back, 1)
+        out[...] = pltpu.roll(sums[pl.ds(line, 1), :], back, 1)[:, : out.shape[1]]
 
 
 def fits(ctx, fsdp, shard_rows):

time: 180 us -> 176 us (0.978)
  Pallas kernels: 176 us -> 174 us
    pallas_call x1, Pallas kernels: 173 us -> 171 us  [fused(): pl.pallas_call(functools.partial(layer_kernel, n, [*inputs, *outputs, *sc...]
where the time goes in v7:
time: 176 us
  Pallas kernels  174 us (99%)
    pallas_call x1, Pallas kernels, fused(): pl.pallas_call(functools.partial(layer_kernel, n, [*inputs, *outputs, *sc...  171 us

profile of v7, /device:TPU:0, one launch (start us, length us, event | category | flops | bytes accessed | tf_op | source)
XLA Modules:
  0.0 175.8 jit_solution(6985678259932550427)
XLA Ops:
  0.6 0.0 copy-start.3
  0.7 0.0 copy-start
  0.7 0.0 copy-start.1
  0.7 0.0 copy-start.2
  0.7 0.6 copy-done.3
  1.3 0.0 copy-done
  1.3 0.0 copy-done.1
  1.3 0.0 copy-done.2
  1.3 0.6 fusion.1.refs_9_
  1.9 170.8 %layer.1 = (bf16[128,1024]{1,0:T(8,128)(2,1)}, f32[128,1024]{1,0:T(8,128)}, bf16[4,32,1536]{2,1,0:T(8,128)(2,1)}, bf16[4,32,2304]{2,1,0:T(8,128)(2,1)}, f32[24,128]{1,0:T(8,128)}) custom-call(bf16[128,1024]{1,0:T(8,128)(2,1)} %bitcast.13, bf16[128,1024]{1,0:T(8,128)(2,1)} %bitcast.14, bf16[32,2048]{1,0:T(8,128)(2,1)} %refs_2_.1, bf16[32,1024]{1,0:T(8,128)(2,1)} %refs_3_.1, ...), custom_call_target="tpu_custom_call" | custom-call | tf_op jit(solution)/shard_map/layer/pallas_call | solution.py:1081
  172.7 3.0 %emit.1 = (bf16[128,1024]{1,0:T(8,128)(2,1)}, f32[128,1024]{1,0:T(8,128)}, f32[32,2048]{1,0:T(8,128)}, f32[32,1024]{1,0:T(8,128)}, f32[32,1024]{1,0:T(8,128)}, /...) custom-call(bf16[128,1024]{1,0:T(8,128)(2,1)} %get-tuple-element.31., ...), custom_call_target="tpu_custom_call" | custom-call | tf_op jit(solution)/shard_map/emit/pallas_call | solution.py:1096
Async XLA Ops:
  0.6 0.7 copy-start.3
  0.7 0.7 copy-start
  0.7 0.7 copy-start.1
  0.7 0.7 copy-start.2

commit v8 on v7

--- a/solution.py
+++ b/solution.py
@@ -892,12 +892,12 @@
         r.rb[c, span, :] = r.dh[span, :].astype(BF16)
         gather_start(r.rb.at[c], r.rb, r.sem_rb, k)
 
-    mlp_part(0)
     gather_relay(r.mb, r.sem_mb, 1, 1, "end")
     gather_relay(r.gb, r.sem_gb, 1, 1)
     for by in range(2, n.ctx - 1):
         gather_relay(r.gb, r.sem_gb, by, 1)
         gather_relay(r.mb, r.sem_mb, by, 1)
+    mlp_part(0)
     scatter_near(sum_x2, 0)
     scatter_far(sum_x2, 0)
     gather_relay(r.mb, r.sem_mb, n.ctx - 1, 1)
@@ -937,7 +937,6 @@
     upstream = r.rb[...].reshape(n.tokens, d)
     for at in range(0, o_cols, HEAD_DIM):
         r.da[at // HEAD_DIM] = mm(upstream, r.wa[:, o_at + at : o_at + at + HEAD_DIM])
-    grads_line(group_m)
     r.ga[:, o_at:] = mm(upstream, r.at[...], FIRST_AXIS).astype(BF16)
     grads_pair(group_o)
     scatter_near(sum_y, 1)
@@ -962,7 +961,9 @@
         r.dv[kv] = r.dv[kv] + mm(r.eb[...], r.wb[...], FIRST_AXIS)
         return carry
 
-    lax.fori_loop(0, n.heads, head_backward, 0)
+    lax.fori_loop(0, n.heads // 2, head_backward, 0)
+    grads_line(group_m)
+    lax.fori_loop(n.heads // 2, n.heads, head_backward, 0)
 
     def query_backward(h, term):
         u = r.qp[h]

time: 176 us -> 171 us (0.972)
  Pallas kernels: 174 us -> 169 us
    pallas_call x1, Pallas kernels: 171 us -> 166 us  [fused(): pl.pallas_call(functools.partial(layer_kernel, n, [*inputs, *outputs, *sc...]
where the time goes in v8:
time: 171 us
  Pallas kernels  169 us (99%)
    pallas_call x1, Pallas kernels, fused(): pl.pallas_call(functools.partial(layer_kernel, n, [*inputs, *outputs, *sc...  166 us

profile of v8, /device:TPU:0, one launch (start us, length us, event | category | flops | bytes accessed | tf_op | source)
XLA Modules:
  0.0 171.0 jit_solution(2909412619031742776)
XLA Ops:
  0.6 0.0 copy-start.3
  0.7 0.0 copy-start
  0.7 0.0 copy-start.1
  0.7 0.0 copy-start.2
  0.7 0.6 copy-done.3
  1.3 0.0 copy-done
  1.3 0.0 copy-done.1
  1.3 0.0 copy-done.2
  1.3 0.6 fusion.1.refs_9_
  1.9 166.0 %layer.1 = (bf16[128,1024]{1,0:T(8,128)(2,1)}, f32[128,1024]{1,0:T(8,128)}, bf16[4,32,1536]{2,1,0:T(8,128)(2,1)}, bf16[4,32,2304]{2,1,0:T(8,128)(2,1)}, f32[24,128]{1,0:T(8,128)}) custom-call(bf16[128,1024]{1,0:T(8,128)(2,1)} %bitcast.13, bf16[128,1024]{1,0:T(8,128)(2,1)} %bitcast.14, bf16[32,2048]{1,0:T(8,128)(2,1)} %refs_2_.1, bf16[32,1024]{1,0:T(8,128)(2,1)} %refs_3_.1, ...), custom_call_target="tpu_custom_call" | custom-call | tf_op jit(solution)/shard_map/layer/pallas_call | solution.py:1082
  168.0 3.0 %emit.1 = (bf16[128,1024]{1,0:T(8,128)(2,1)}, f32[128,1024]{1,0:T(8,128)}, f32[32,2048]{1,0:T(8,128)}, f32[32,1024]{1,0:T(8,128)}, f32[32,1024]{1,0:T(8,128)}, /...) custom-call(bf16[128,1024]{1,0:T(8,128)(2,1)} %get-tuple-element.31., ...), custom_call_target="tpu_custom_call" | custom-call | tf_op jit(solution)/shard_map/emit/pallas_call | solution.py:1097
Async XLA Ops:
  0.6 0.7 copy-start.3
  0.7 0.7 copy-start
  0.7 0.7 copy-start.1
  0.7 0.7 copy-start.2

commit v9 on v8

--- a/solution.py
+++ b/solution.py
@@ -1097,8 +1097,14 @@
     result, input_grad, oq, ok, ov, oo, og, ou, od, *gains = pl.pallas_call(
         functools.partial(emit_kernel, n),
         out_shape=tuple(jax.ShapeDtypeStruct(f[:2], f[2]) for f in finals),
-        in_specs=[vmem] * len(outputs),
-        out_specs=tuple(vmem for _ in finals),
+        in_specs=[hbm] * (len(outputs) - 1) + [vmem],
+        out_specs=tuple(hbm if i < 2 + len(shards) else vmem for i in range(len(finals))),
+        scratch_shapes=[
+            *(pltpu.VMEM(a.shape, a.dtype) for a in landed[:-1]),
+            *(pltpu.VMEM(a.shape, F32) for a in shards),
+            pltpu.SemaphoreType.DMA((len(outputs) - 1,)),
+            pltpu.SemaphoreType.DMA((2 + len(shards),)),
+        ],
         name="emit",
     )(*landed)
     return (
@@ -1118,19 +1124,34 @@
     )
 
 
-def emit_kernel(n, result, input_grad, attn_land, mlp_land, sums, *outs):
-    outs[0][...] = result[...]
-    outs[1][...] = input_grad[...]
+def emit_kernel(n, *refs):
+    sources, sums, outs = refs[:4], refs[4], refs[5:18]
+    held, wide, in_sem, out_sem = refs[18:22], refs[22:29], refs[29], refs[30]
+    loads = [pltpu.make_async_copy(sources[i], held[i], in_sem.at[i]) for i in range(4)]
+    stores = []
+
+    def store(src, i):
+        copy = pltpu.make_async_copy(src, outs[i], out_sem.at[i])
+        copy.start()
+        stores.append(copy)
+
+    for i in (3, 2, 1, 0):
+        loads[i].start()
     which = 2
-    for land, widths in ((attn_land, n.cols[:4]), (mlp_land, n.cols[4:])):
-        at = 0
+    for i, widths, first in ((3, n.cols[4:], 6), (2, n.cols[:4], 2)):
+        loads[i].wait()
+        land, at, which = held[i], 0, first
         for width in widths:
+            out = wide[which - 2]
             for j in range(n.ctx):
-                outs[which][:, j * width : (j + 1) * width] = land[j, :, at : at + width].astype(
-                    F32
-                )
+                out[:, j * width : (j + 1) * width] = land[j, :, at : at + width].astype(F32)
+            store(out, which)
             at += width
             which += 1
+    for i in (1, 0):
+        loads[i].wait()
+        store(held[i], i)
+    which = 9
     me = lax.axis_index("fsdp") * n.ctx + lax.axis_index("ctx")
     row, at = me * n.each // HEAD_DIM, lax.rem(me * n.each, HEAD_DIM)
     for out, (line, lane) in zip(
@@ -1144,6 +1165,8 @@
     ):
         back = lax.rem(HEAD_DIM - lane, HEAD_DIM)
         out[...] = pltpu.roll(sums[pl.ds(line, 1), :], back, 1)[:, : out.shape[1]]
+    for copy in stores:
+        copy.wait()
 
 
 def fits(ctx, fsdp, shard_rows):

time: 171 us -> 172 us (level)
  no operation moved by 1% of the time
where the time goes in v9:
time: 172 us
  Pallas kernels  170 us (99%)
    pallas_call x1, Pallas kernels, fused(): pl.pallas_call(functools.partial(layer_kernel, n, [*inputs, *outputs, *sc...  166 us
    pallas_call x1, Pallas kernels, fused(): pl.pallas_call(functools.partial(emit_kernel, n), out_shape=tuple((jax.Sh...  3.96 us

profile of v9, /device:TPU:0, one launch (start us, length us, event | category | flops | bytes accessed | tf_op | source)
XLA Modules:
  0.0 172.1 jit_solution(16372733506467743910)
XLA Ops:
  0.6 0.0 copy-start.3
  0.7 0.0 copy-start
  0.7 0.0 copy-start.1
  0.7 0.0 copy-start.2
  0.7 0.6 copy-done.3
  1.3 0.0 copy-done
  1.3 0.0 copy-done.1
  1.3 0.0 copy-done.2
  1.3 0.6 fusion.1.refs_9_
  1.9 166.0 %layer.1 = (bf16[128,1024]{1,0:T(8,128)(2,1)}, f32[128,1024]{1,0:T(8,128)}, bf16[4,32,1536]{2,1,0:T(8,128)(2,1)}, bf16[4,32,2304]{2,1,0:T(8,128)(2,1)}, f32[24,128]{1,0:T(8,128)}) custom-call(bf16[128,1024]{1,0:T(8,128)(2,1)} %bitcast.13, bf16[128,1024]{1,0:T(8,128)(2,1)} %bitcast.14, bf16[32,2048]{1,0:T(8,128)(2,1)} %refs_2_.1, bf16[32,1024]{1,0:T(8,128)(2,1)} %refs_3_.1, ...), custom_call_target="tpu_custom_call" | custom-call | tf_op jit(solution)/shard_map/layer/pallas_call | solution.py:1082
  168.0 4.0 %emit.1 = (bf16[128,1024]{1,0:T(8,128)(2,1)}, f32[128,1024]{1,0:T(8,128)}, f32[32,2048]{1,0:T(8,128)}, f32[32,1024]{1,0:T(8,128)}, f32[32,1024]{1,0:T(8,128)}, /...) custom-call(bf16[128,1024]{1,0:T(8,128)(2,1)} %get-tuple-element.31., ...), custom_call_target="tpu_custom_call" | custom-call | tf_op jit(solution)/shard_map/emit/pallas_call | solution.py:1097
Async XLA Ops:
  0.6 0.7 copy-start.3
  0.7 0.7 copy-start
  0.7 0.7 copy-start.1
  0.7 0.7 copy-start.2
